TPU v7x, 8 devices: a whole 2x2x1 slice. The times are simulated.
8 devices in a mesh: dp: 2 (over z, y), sp: 4 (over x, core).
Axes of the slice: x: 2, y: 2, z: 1, core: 2. Of those that a mesh axis runs over, the one named last changes fastest.
Arguments:
- tok_in: bfloat16 [4096, 2560], P(('dp', 'sp')), parts along dimension 0
- tok_pos: int32 [4096], P(('dp', 'sp')), parts along dimension 0
- w_dq: bfloat16 [2560, 768], replicated
- g_q: float32 [768], replicated
- w_uq: bfloat16 [768, 40, 96], replicated
- w_dkv: bfloat16 [2560, 288], replicated
- g_kv: float32 [256], replicated
- w_uk: bfloat16 [256, 40, 64], replicated
- w_uv: bfloat16 [256, 40, 64], replicated
- w_o: bfloat16 [40, 64, 2560], replicated
Outputs:
- output 1: bfloat16 [4096, 2560], P(('dp', 'sp')), parts along dimension 0
- output 2: bfloat16 [4096, 256], P(('dp', 'sp')), parts along dimension 0
- output 3: bfloat16 [4096, 32], P(('dp', 'sp')), parts along dimension 0
There are 2 independent parts. A program takes and returns all parts, laid end to end along the dimension named above; an argument that names none is the same for every part.
All inputs are finite; a program needn't handle non-finite values.
Results may differ from a plain program's by a relative error of at most 0.00435966.
Values are sent between devices in bfloat16 or wider.
A program may use at most 1 GiB of HBM per device.

v0:
```python
import math
import jax
import jax.numpy as jnp
from jax import lax
from jax.sharding import PartitionSpec as P

ROPE_THETA = 10000.0
YARN_FACTOR = 40.0
ORIG_CTX = 4096.0
BETA_FAST = 32.0
BETA_SLOW = 1.0
NORM_EPS = 1e-6


def rope_freqs(rot_dim):
    half_dim = rot_dim // 2
    log_base = 2.0 * math.log(ROPE_THETA)
    low_idx = max(math.floor(rot_dim * math.log(ORIG_CTX / (BETA_FAST * 2.0 * math.pi)) / log_base), 0)
    high_idx = min(math.ceil(rot_dim * math.log(ORIG_CTX / (BETA_SLOW * 2.0 * math.pi)) / log_base), half_dim - 1)
    spread = max(high_idx - low_idx, 0.001)
    freq_list = []
    for freq_idx in range(half_dim):
        base_freq = ROPE_THETA ** (-2.0 * freq_idx / rot_dim)
        ramp_val = min(max((freq_idx - low_idx) / spread, 0.0), 1.0)
        freq_list.append(base_freq / YARN_FACTOR * ramp_val + base_freq * (1.0 - ramp_val))
    return jnp.asarray(freq_list, dtype=jnp.float32)


def rotate_half(act_in, cos_t, sin_t):
    half_dim = act_in.shape[-1] // 2
    first = act_in[..., :half_dim]
    second = act_in[..., half_dim:]
    return jnp.concatenate([first * cos_t - second * sin_t, second * cos_t + first * sin_t], axis=-1)


def rms_norm(act_in, gain):
    mean_sq = jnp.mean(act_in * act_in, axis=-1, keepdims=True)
    return act_in * lax.rsqrt(mean_sq + NORM_EPS) * gain


def solution(mesh):
    groups = mesh.shape['sp']
    tok_spec = P(('dp', 'sp'))
    rows_spec = P(('dp', 'sp'), None)
    replicated = P()

    def local_step(tok_in, tok_pos, w_dq, g_q, w_uq, w_dkv, g_kv, w_uk, w_uv, w_o):
        rows = tok_in.shape[0]
        num_heads = w_uq.shape[1]
        qk_dim = w_uq.shape[2]
        kv_rank = g_kv.shape[0]
        rot_dim = w_dkv.shape[1] - kv_rank
        nope_dim = qk_dim - rot_dim
        v_dim = w_uv.shape[2]
        seq_len = rows * groups
        attn_scale = (0.1 * math.log(YARN_FACTOR) + 1.0) ** 2 / math.sqrt(qk_dim)
        angles = tok_pos.astype(jnp.float32)[:, None] * rope_freqs(rot_dim)[None, :]
        cos_t = jnp.cos(angles)
        sin_t = jnp.sin(angles)
        q_lat = rms_norm(jnp.dot(tok_in, w_dq, preferred_element_type=jnp.float32), g_q).astype(jnp.bfloat16)
        q_full = jnp.einsum('tc,che->the', q_lat, w_uq, preferred_element_type=jnp.float32)
        q_all = jnp.concatenate([q_full[:, :, :nope_dim], rotate_half(q_full[:, :, nope_dim:], cos_t[:, None, :], sin_t[:, None, :])], axis=-1).astype(jnp.bfloat16)
        kv_lat = jnp.dot(tok_in, w_dkv, preferred_element_type=jnp.float32)
        cache_kv = rms_norm(kv_lat[:, :kv_rank], g_kv).astype(jnp.bfloat16)
        cache_pe = rotate_half(kv_lat[:, kv_rank:], cos_t, sin_t).astype(jnp.bfloat16)
        k_nope = jnp.einsum('tc,chn->thn', cache_kv, w_uk, preferred_element_type=jnp.float32).astype(jnp.bfloat16)
        values = jnp.einsum('tc,chv->thv', cache_kv, w_uv, preferred_element_type=jnp.float32).astype(jnp.bfloat16)
        k_all = jnp.concatenate([k_nope, jnp.broadcast_to(cache_pe[:, None, :], (rows, num_heads, rot_dim))], axis=-1)
        q_heads = lax.all_to_all(q_all, 'sp', 1, 0, tiled=True)
        k_heads = lax.all_to_all(k_all, 'sp', 1, 0, tiled=True)
        v_heads = lax.all_to_all(values, 'sp', 1, 0, tiled=True)
        key_idx = jnp.arange(seq_len)

        def block_attention(blk_idx):
            start = blk_idx * rows
            q_blk = lax.dynamic_slice_in_dim(q_heads, start, rows, axis=0)
            logits = jnp.einsum('qhe,khe->hqk', q_blk, k_heads, preferred_element_type=jnp.float32) * attn_scale
            row_idx = start + jnp.arange(rows)
            logits = jnp.where(key_idx[None, None, :] <= row_idx[None, :, None], logits, -jnp.inf)
            attn_prob = jax.nn.softmax(logits, axis=-1).astype(jnp.bfloat16)
            return jnp.einsum('hqk,khv->qhv', attn_prob, v_heads, preferred_element_type=jnp.float32).astype(jnp.bfloat16)

        o_heads = lax.map(block_attention, jnp.arange(groups)).reshape(seq_len, num_heads // groups, v_dim)
        o_local = lax.all_to_all(o_heads, 'sp', 0, 1, tiled=True)
        attn_out = jnp.einsum('thv,hvd->td', o_local, w_o, preferred_element_type=jnp.float32).astype(jnp.bfloat16)
        return attn_out, cache_kv, cache_pe

    return jax.shard_map(local_step, mesh=mesh, in_specs=(rows_spec, tok_spec, replicated, replicated, replicated, replicated, replicated, replicated, replicated, replicated), out_specs=(rows_spec, rows_spec, rows_spec), check_vma=False)
```

profile of v0, /device:TPU:3, one launch (start us, length us, event | category | flops | bytes accessed | tf_op | source)
XLA Modules:
  0.0 382.0 jit_solution(9862432558145264942)
XLA Ops:
  0.7 1.7 copy-done
  2.4 2.3 fusion.34
  4.9 0.8 fusion.36
  5.8 1.9 convert_element_type.37
  7.7 4.5 %all-to-all-start.2 = ((bf16[512,40,64]{0,2,1:T(8,128)(2,1)}), bf16[512,40,64]{0,2,1:T(8,128)(2,1)}, u32[]{:S(2)}, u32[]{:S(2)}) async-start(bf16[512,40,64]{0,2,1:T(8,128)(2,1)} %convert_element_type.37), calls=%async_computation.2 | async-start | bytes 5242880 | tf_op jit(solution)/shard_map/all_to_all | solution.py:71
  12.2 4.4 %multiply_reduce_fusion = (f32[512]{0:T(512)S(1)}, f32[512,768]{1,0:T(8,128)S(1)}) fusion(bf16[512,2560]{1,0:T(8,128)(2,1)S(1)} %copy-done, bf16[2560,768]{1,0:T(8,128)(2,1)} %param.15), kind=kOutput, calls=%fused_computation.28 | convolution fusion | flops 2014051840 | bytes 8128512 | tf_op jit(solution)/shard_map/dot_general | solution.py:60
  16.7 5.5 %fusion.26 = f32[512,3840]{0,1:S(1)} fusion(bf16[768,3840]{0,1:T(8,128)(2,1)} %bitcast.69, f32[512,768]{1,0:T(8,128)S(1)} %get-tuple-element.85, f32[768]{0:T(1024)S(1)} %copy-done.10, f32[512]{0:T(512)S(1)} %add_rsqrt_fusion.1), kind=kOutput, calls=%fused_computation.31 | convolution fusion | flops 3021078528 | bytes 15340544
  22.2 0.4 slice.48
  23.1 0.5 subtract_convert_fusion
  23.5 2.1 pad_maximum_fusion
  25.6 15.2 %all-to-all-done.2 = bf16[512,40,64]{0,2,1:T(8,128)(2,1)} async-done(((bf16[512,40,64]{0,2,1:T(8,128)(2,1)}), bf16[512,40,64]{0,2,1:T(8,128)(2,1)}, u32[]{:S(2)}, u32[]{:S(2)}) %all-to-all-start.2) | async-done | bytes 2621472 | tf_op jit(solution)/shard_map/all_to_all | solution.py:71
  40.9 7.1 %all-to-all-start = ((bf16[512,40,96]{0,2,1:T(8,128)(2,1)}), bf16[512,40,96]{0,2,1:T(8,128)(2,1)}, u32[]{:S(2)}, u32[]{:S(2)}) async-start(bf16[512,40,96]{0,2,1:T(8,128)(2,1)} %pad_maximum_fusion), calls=%async_computation | async-start | bytes 7864320 | tf_op jit(solution)/shard_map/all_to_all | solution.py:69
  48.0 0.8 fusion.35
  48.9 0.4 convert_element_type.36
  49.3 0.6 copy-done.6
  50.0 2.4 pad_maximum_fusion.1
  52.5 38.9 %all-to-all-done = bf16[512,40,96]{0,2,1:T(8,128)(2,1)} async-done(((bf16[512,40,96]{0,2,1:T(8,128)(2,1)}), bf16[512,40,96]{0,2,1:T(8,128)(2,1)}, u32[]{:S(2)}, u32[]{:S(2)}) %all-to-all-start) | async-done | bytes 3932192 | tf_op jit(solution)/shard_map/all_to_all | solution.py:69
  91.4 6.5 %all-to-all-start.1 = ((bf16[512,40,96]{0,2,1:T(8,128)(2,1)}), bf16[512,40,96]{0,2,1:T(8,128)(2,1)}, u32[]{:S(2)}, u32[]{:S(2)}) async-start(bf16[512,40,96]{0,2,1:T(8,128)(2,1)} %pad_maximum_fusion.1), calls=%async_computation.1 | async-start | bytes 7864320 | tf_op jit(solution)/shard_map/all_to_all | solution.py:70
  97.9 3.6 copy.45
  101.5 4.6 %copy.43 = bf16[4,10,12,8,512]{4,3,0,2,1:T(8,128)(2,1)} copy(bf16[4,10,12,8,512]{4,3,2,1,0:T(8,128)(2,1)} %bitcast.24) | data formatting | bytes 7864320 | tf_op jit(solution)/shard_map/all_to_all | solution.py:69
  106.1 35.0 %all-to-all-done.1 = bf16[512,40,96]{0,2,1:T(8,128)(2,1)} async-done(((bf16[512,40,96]{0,2,1:T(8,128)(2,1)}), bf16[512,40,96]{0,2,1:T(8,128)(2,1)}, u32[]{:S(2)}, u32[]{:S(2)}) %all-to-all-start.1) | async-done | bytes 3932192 | tf_op jit(solution)/shard_map/all_to_all | solution.py:70
  141.1 4.6 %copy.44 = bf16[4,10,12,8,512]{4,3,0,2,1:T(8,128)(2,1)} copy(bf16[4,10,12,8,512]{4,3,2,1,0:T(8,128)(2,1)} %bitcast.26) | data formatting | bytes 7864320 | tf_op jit(solution)/shard_map/all_to_all | solution.py:70
  145.7 156.4 %while.11 = (s32[]{:T(128)}, bf16[4,512,10,64]{1,3,2,0:T(8,128)(2,1)}, s32[4]{0:T(128)S(1)}, bf16[2048,10,96]{0,2,1:T(8,128)(2,1)}, bf16[2048,10,96]{0,2,1:T(8,1...) while((s32[]{:T(128)}, ...), condition=%wide.region_5.6_spmd.clone, body=%wide.region_2.5_spmd.clone.sunk | while | flops 3419736576 | bytes 94220968 | solution.py:83
  145.7 0.6 dynamic_slice.24
  146.9 0.7 iota_compare_fusion.2
  147.6 20.4 %fusion.59 = (f32[10,512]{1,0:T(8,128)S(1)}, f32[10,512,2048]{2,1,0:T(8,128)}) fusion(pred[512,2048]{1,0:T(8,128)(4,1)S(1)} %iota_compare_fusion.2, bf16[2048,10,96]{0,2,1:T(8,128)(2,1)} %get-tuple-element.151, bf16[2048,10,96]{0,2,1:T(8,128)(2,1)} %get-tuple-element.150, s32[]{:T(128)S(6)} %select_n.22), kind=kOutput, calls=%fused_computation.43.clone.1 | convolution fusion | flops 2055211008 | bytes 47927300 | tf_op jit(solution)/shard_map/while/body/eval_jaxpr/sub | solution.py:80
  168.0 16.8 %fusion.60 = bf16[4,512,10,64]{1,3,2,0:T(8,128)(2,1)} fusion(bf16[4,512,10,64]{1,3,2,0:T(8,128)(2,1)} %get-tuple-element.138, s32[]{:T(128)} %get-tuple-element.137, bf16[2048,10,64]{0,2,1:T(8,128)(2,1)} %get-tuple-element.152, f32[10,512,2048]{2,1,0:T(8,128)} %get-tuple-element.125, f32[10,512]{1,0:T(8,128)S(1)} %get-tuple-element.126), kind=kOutput, calls=%fused_computation.14.clone.1 | convolution fusion | flops 1363476480 | bytes 45240832 | tf_op jit(solution)/shard_map/while/body/eval_jaxpr/hqk,khv->qhv/dot_general | solution.py:81
  184.8 0.6 dynamic_slice.24
  186.0 0.7 iota_compare_fusion.2
  186.7 20.4 %fusion.59 = (f32[10,512]{1,0:T(8,128)S(1)}, f32[10,512,2048]{2,1,0:T(8,128)}) fusion(pred[512,2048]{1,0:T(8,128)(4,1)S(1)} %iota_compare_fusion.2, bf16[2048,10,96]{0,2,1:T(8,128)(2,1)} %get-tuple-element.151, bf16[2048,10,96]{0,2,1:T(8,128)(2,1)} %get-tuple-element.150, s32[]{:T(128)S(6)} %select_n.22), kind=kOutput, calls=%fused_computation.43.clone.1 | convolution fusion | flops 2055211008 | bytes 47927300 | tf_op jit(solution)/shard_map/while/body/eval_jaxpr/sub | solution.py:80
  207.1 16.8 %fusion.60 = bf16[4,512,10,64]{1,3,2,0:T(8,128)(2,1)} fusion(bf16[4,512,10,64]{1,3,2,0:T(8,128)(2,1)} %get-tuple-element.138, s32[]{:T(128)} %get-tuple-element.137, bf16[2048,10,64]{0,2,1:T(8,128)(2,1)} %get-tuple-element.152, f32[10,512,2048]{2,1,0:T(8,128)} %get-tuple-element.125, f32[10,512]{1,0:T(8,128)S(1)} %get-tuple-element.126), kind=kOutput, calls=%fused_computation.14.clone.1 | convolution fusion | flops 1363476480 | bytes 45240832 | tf_op jit(solution)/shard_map/while/body/eval_jaxpr/hqk,khv->qhv/dot_general | solution.py:81
  223.9 0.6 dynamic_slice.24
  225.1 0.7 iota_compare_fusion.2
  225.8 20.4 %fusion.59 = (f32[10,512]{1,0:T(8,128)S(1)}, f32[10,512,2048]{2,1,0:T(8,128)}) fusion(pred[512,2048]{1,0:T(8,128)(4,1)S(1)} %iota_compare_fusion.2, bf16[2048,10,96]{0,2,1:T(8,128)(2,1)} %get-tuple-element.151, bf16[2048,10,96]{0,2,1:T(8,128)(2,1)} %get-tuple-element.150, s32[]{:T(128)S(6)} %select_n.22), kind=kOutput, calls=%fused_computation.43.clone.1 | convolution fusion | flops 2055211008 | bytes 47927300 | tf_op jit(solution)/shard_map/while/body/eval_jaxpr/sub | solution.py:80
  246.2 16.8 %fusion.60 = bf16[4,512,10,64]{1,3,2,0:T(8,128)(2,1)} fusion(bf16[4,512,10,64]{1,3,2,0:T(8,128)(2,1)} %get-tuple-element.138, s32[]{:T(128)} %get-tuple-element.137, bf16[2048,10,64]{0,2,1:T(8,128)(2,1)} %get-tuple-element.152, f32[10,512,2048]{2,1,0:T(8,128)} %get-tuple-element.125, f32[10,512]{1,0:T(8,128)S(1)} %get-tuple-element.126), kind=kOutput, calls=%fused_computation.14.clone.1 | convolution fusion | flops 1363476480 | bytes 45240832 | tf_op jit(solution)/shard_map/while/body/eval_jaxpr/hqk,khv->qhv/dot_general | solution.py:81
  263.0 0.6 dynamic_slice.24
  264.3 0.7 iota_compare_fusion.2
  264.9 20.4 %fusion.59 = (f32[10,512]{1,0:T(8,128)S(1)}, f32[10,512,2048]{2,1,0:T(8,128)}) fusion(pred[512,2048]{1,0:T(8,128)(4,1)S(1)} %iota_compare_fusion.2, bf16[2048,10,96]{0,2,1:T(8,128)(2,1)} %get-tuple-element.151, bf16[2048,10,96]{0,2,1:T(8,128)(2,1)} %get-tuple-element.150, s32[]{:T(128)S(6)} %select_n.22), kind=kOutput, calls=%fused_computation.43.clone.1 | convolution fusion | flops 2055211008 | bytes 47927300 | tf_op jit(solution)/shard_map/while/body/eval_jaxpr/sub | solution.py:80
  285.3 16.8 %fusion.60 = bf16[4,512,10,64]{1,3,2,0:T(8,128)(2,1)} fusion(bf16[4,512,10,64]{1,3,2,0:T(8,128)(2,1)} %get-tuple-element.138, s32[]{:T(128)} %get-tuple-element.137, bf16[2048,10,64]{0,2,1:T(8,128)(2,1)} %get-tuple-element.152, f32[10,512,2048]{2,1,0:T(8,128)} %get-tuple-element.125, f32[10,512]{1,0:T(8,128)S(1)} %get-tuple-element.126), kind=kOutput, calls=%fused_computation.14.clone.1 | convolution fusion | flops 1363476480 | bytes 45240832 | tf_op jit(solution)/shard_map/while/body/eval_jaxpr/hqk,khv->qhv/dot_general | solution.py:81
  302.1 10.2 %copy.40 = bf16[4,512,10,64]{3,2,1,0:T(8,128)(2,1)} copy(bf16[4,512,10,64]{1,3,2,0:T(8,128)(2,1)} %get-tuple-element.40) | data formatting | bytes 5242880 | tf_op jit(solution)/shard_map/reshape | solution.py:83
  312.3 7.5 %reshape.134 = bf16[4,2,163840]{2,1,0:T(2,128)(2,1)} reshape(bf16[2048,10,64]{2,1,0:T(8,128)(2,1)} %bitcast.58) | data formatting | bytes 5242880
  319.8 5.7 %all-to-all-start.3 = ((bf16[4,2,163840]{2,1,0:T(2,128)(2,1)}), bf16[4,2,163840]{2,1,0:T(2,128)(2,1)S(1)}, u32[]{:S(2)}, u32[]{:S(2)}) async-start(bf16[4,2,163840]{2,1,0:T(2,128)(2,1)} %reshape.134), calls=%async_computation.3 | async-start | bytes 5242880 | tf_op jit(solution)/shard_map/all_to_all | solution.py:84
  325.5 0.8 copy.37
  326.3 28.2 %all-to-all-done.3 = bf16[4,2,163840]{2,1,0:T(2,128)(2,1)S(1)} async-done(((bf16[4,2,163840]{2,1,0:T(2,128)(2,1)}), bf16[4,2,163840]{2,1,0:T(2,128)(2,1)S(1)}, u32[]{:S(2)}, u32[]{:S(2)}) %all-to-all-start.3) | async-done | bytes 2621472 | tf_op jit(solution)/shard_map/all_to_all | solution.py:84
  354.5 5.8 %reshape.135 = bf16[2048,10,64]{2,1,0:T(8,128)(2,1)} reshape(bf16[4,2,163840]{2,1,0:T(2,128)(2,1)S(1)} %all-to-all-done.3) | data formatting | bytes 5242880
  360.3 9.7 %copy.41 = bf16[4,512,10,64]{1,0,3,2:T(4,128)(2,1)S(1)} copy(bf16[4,512,10,64]{3,2,1,0:T(8,128)(2,1)} %bitcast.59) | data formatting | bytes 5242880 | tf_op jit(solution)/shard_map/all_to_all | solution.py:84
  370.0 0.6 copy.36
  370.6 11.3 %bitcast_convert_fusion = bf16[512,2560]{1,0:T(8,128)(2,1)} fusion(bf16[512,40,64]{0,2,1:T(8,128)(2,1)S(1)} %bitcast.68, bf16[40,64,2560]{2,1,0:T(8,128)(2,1)} %param.22), kind=kOutput, calls=%fused_computation.24 | convolution fusion | flops 6712197120 | bytes 18350080 | tf_op jit(solution)/shard_map/thv,hvd->td/dot_general | solution.py:85
  (34 shorter events, 0.9 us)
Async XLA Ops:
  0.6 1.7 copy-start
  0.6 4.1 %copy-start.8 = (f32[256]{0:T(256)S(1)}, f32[256]{0:T(256)}, u32[]{:S(2)}) copy-start(f32[256]{0:T(256)} %param.19) | copy-start | bytes 3076
  0.7 4.3 %copy-start.4 = (bf16[256,40,64]{0,2,1:T(8,128)(2,1)S(1)}, bf16[256,40,64]{0,2,1:T(8,128)(2,1)}, u32[]{:S(2)}) copy-start(bf16[256,40,64]{0,2,1:T(8,128)(2,1)} %param.21) | copy-start | bytes 3932164
  4.9 43.1 %copy-start.2 = (bf16[512,256]{0,1:T(8,128)(2,1)}, bf16[512,256]{0,1:T(8,128)(2,1)S(1)}, u32[]{:S(2)}) copy-start(bf16[512,256]{0,1:T(8,128)(2,1)S(1)} %multiply_convert_fusion.2) | copy-start | bytes 786436
  7.7 33.2 %all-to-all-start.2 = ((bf16[512,40,64]{0,2,1:T(8,128)(2,1)}), bf16[512,40,64]{0,2,1:T(8,128)(2,1)}, u32[]{:S(2)}, u32[]{:S(2)}) async-start(bf16[512,40,64]{0,2,1:T(8,128)(2,1)} %convert_element_type.37), calls=%async_computation.2 | async-start | bytes 5242880 | tf_op jit(solution)/shard_map/all_to_all | solution.py:71
  12.2 4.4 %copy-start.7 = (s32[512]{0:T(512)S(1)}, s32[512]{0:T(512)}, u32[]{:S(2)}) copy-start(s32[512]{0:T(512)} %param.14) | copy-start | bytes 6148
  12.2 4.4 %copy-start.10 = (f32[768]{0:T(1024)S(1)}, f32[768]{0:T(1024)}, u32[]{:S(2)}) copy-start(f32[768]{0:T(1024)} %param.16) | copy-start | bytes 9220
  22.2 0.7 copy-start.9
  25.6 22.4 %copy-start.5 = (bf16[256,40,64]{0,2,1:T(8,128)(2,1)S(1)}, bf16[256,40,64]{0,2,1:T(8,128)(2,1)}, u32[]{:S(2)}) copy-start(bf16[256,40,64]{0,2,1:T(8,128)(2,1)} %param.20) | copy-start | bytes 3932164
  40.9 50.5 %all-to-all-start = ((bf16[512,40,96]{0,2,1:T(8,128)(2,1)}), bf16[512,40,96]{0,2,1:T(8,128)(2,1)}, u32[]{:S(2)}, u32[]{:S(2)}) async-start(bf16[512,40,96]{0,2,1:T(8,128)(2,1)} %pad_maximum_fusion), calls=%async_computation | async-start | bytes 7864320 | tf_op jit(solution)/shard_map/all_to_all | solution.py:69
  49.3 0.6 copy-start.6
  91.4 49.7 %all-to-all-start.1 = ((bf16[512,40,96]{0,2,1:T(8,128)(2,1)}), bf16[512,40,96]{0,2,1:T(8,128)(2,1)}, u32[]{:S(2)}, u32[]{:S(2)}) async-start(bf16[512,40,96]{0,2,1:T(8,128)(2,1)} %pad_maximum_fusion.1), calls=%async_computation.1 | async-start | bytes 7864320 | tf_op jit(solution)/shard_map/all_to_all | solution.py:70
  319.8 5.7 %copy-start.3 = (bf16[512,256]{0,1:T(8,128)(2,1)S(1)}, bf16[512,256]{0,1:T(8,128)(2,1)}, u32[]{:S(2)}) copy-start(bf16[512,256]{0,1:T(8,128)(2,1)} %copy-done.2) | copy-start | bytes 786436
  319.8 34.7 %all-to-all-start.3 = ((bf16[4,2,163840]{2,1,0:T(2,128)(2,1)}), bf16[4,2,163840]{2,1,0:T(2,128)(2,1)S(1)}, u32[]{:S(2)}, u32[]{:S(2)}) async-start(bf16[4,2,163840]{2,1,0:T(2,128)(2,1)} %reshape.134), calls=%async_computation.3 | async-start | bytes 5242880 | tf_op jit(solution)/shard_map/all_to_all | solution.py:84
  370.6 11.4 %copy-start.1 = (bf16[512,2560]{1,0:T(8,128)(2,1)S(1)}, bf16[512,2560]{1,0:T(8,128)(2,1)}, u32[]{:S(2)}) copy-start(bf16[512,2560]{1,0:T(8,128)(2,1)} %param.13) | copy-start | bytes 7864324
where the time goes:
time: 386 us; the launch traced here: 382 us
  matrix products  174 us (45%)
  waiting for transfers between devices  117 us (30%)
  local copies, waits for them, and re-layouts  53 us (14%)
  starting transfers between devices  23.9 us (6%)
  other arithmetic  10.3 us (3%)
    sub x4, matrix products, block_attention(): attn_prob = jax.nn.softmax(logits, axis=-1).astype(jnp.bfloat16)  81.7 us
    dot_general x4, matrix products, block_attention(): jnp.einsum('hqk,khv->qhv', attn_prob, v_heads, preferred_element_type=jnp...  67 us
    all_to_all x1, waiting for transfers between devices, local_step(): q_heads = lax.all_to_all(q_all, 'sp', 1, 0, tiled=True)  38.9 us
    all_to_all x1, waiting for transfers between devices, local_step(): k_heads = lax.all_to_all(k_all, 'sp', 1, 0, tiled=True)  35 us
    all_to_all x1, waiting for transfers between devices, local_step(): o_local = lax.all_to_all(o_heads, 'sp', 0, 1, tiled=True)  28.2 us
    unnamed x25, local copies, waits for them, and re-layouts  16.7 us
    all_to_all x1, waiting for transfers between devices, local_step(): v_heads = lax.all_to_all(values, 'sp', 1, 0, tiled=True)  15.2 us
    dot_general x1, matrix products, local_step(): jnp.einsum('thv,hvd->td', o_local, w_o, preferred_element_type=jnp.float32)  11.3 us
  transfers between devices with their start and end apart: 4, of which 4 were waited for; matrix products, arithmetic and copies ran while one was open for 7% of the time, Pallas kernels for 0%

commit v1 on v0

v1 whole, which is shorter than its diff:
```python
import functools
import math
import jax
import jax.numpy as jnp
from jax import lax
from jax.experimental import pallas as pl
from jax.experimental.pallas import tpu as pltpu
from jax.sharding import PartitionSpec as P

ROPE_THETA = 10000.0
YARN_FACTOR = 40.0
ORIG_CTX = 4096.0
BETA_FAST = 32.0
BETA_SLOW = 1.0
NORM_EPS = 1e-6


def rope_freqs(rot_dim):
    half_dim = rot_dim // 2
    log_base = 2.0 * math.log(ROPE_THETA)
    low_idx = max(math.floor(rot_dim * math.log(ORIG_CTX / (BETA_FAST * 2.0 * math.pi)) / log_base), 0)
    high_idx = min(math.ceil(rot_dim * math.log(ORIG_CTX / (BETA_SLOW * 2.0 * math.pi)) / log_base), half_dim - 1)
    spread = max(high_idx - low_idx, 0.001)
    freq_list = []
    for freq_idx in range(half_dim):
        base_freq = ROPE_THETA ** (-2.0 * freq_idx / rot_dim)
        ramp_val = min(max((freq_idx - low_idx) / spread, 0.0), 1.0)
        freq_list.append(base_freq / YARN_FACTOR * ramp_val + base_freq * (1.0 - ramp_val))
    return jnp.asarray(freq_list, dtype=jnp.float32)


def rotate_half(act_in, cos_t, sin_t):
    half_dim = act_in.shape[-1] // 2
    first = act_in[..., :half_dim]
    second = act_in[..., half_dim:]
    return jnp.concatenate([first * cos_t - second * sin_t, second * cos_t + first * sin_t], axis=-1)


def rms_norm(act_in, gain):
    mean_sq = jnp.mean(act_in * act_in, axis=-1, keepdims=True)
    return act_in * lax.rsqrt(mean_sq + NORM_EPS) * gain


ATTN_GROUP = 8


def attention_kernel(nprev_ref, qt_ref, ck_ref, wuk_ref, wuv_ref, wo_hbm, out_ref,
                     qaug, kn, vt, s_a, s_b, c_a, c_b, m_s, l_s, acc, o_nat, wo, wo_sem,
                     *, scale2, rows, nope, rot, vdim):
    nprev = nprev_ref[0]
    heads = qt_ref.shape[0]
    G = ATTN_GROUP
    wo_copy = pltpu.make_async_copy(wo_hbm, wo, wo_sem)
    wo_copy.start()
    qaug[...] = jnp.zeros_like(qaug)
    NT = (((1,), (1,)), ((), ()))
    NN = (((1,), (0,)), ((), ()))
    f32 = jnp.float32
    bf16 = jnp.bfloat16
    half = rows // 2

    def keys(h, start, size):
        return jnp.concatenate([kn[h // 2, pl.ds(start, size), :], ck_ref[pl.ds(start, size), 256:384]], axis=1)

    def scores(h, blk, s_ref, c_ref):
        start = pl.multiple_of(blk * rows, rows)
        s = lax.dot_general(keys(h, start, rows), qaug[h], NN, preferred_element_type=f32)
        s_ref[...] = s
        c_ref[...] = jnp.max(s, axis=0, keepdims=True)

    def absorb(h, blk, s_ref, c_ref):
        start = pl.multiple_of(blk * rows, rows)
        m_old = m_s[h]
        m_new = jnp.maximum(m_old, c_ref[...])
        m_s[h] = m_new
        alpha = jnp.exp2((m_old - m_new) * scale2)
        p = jnp.exp2((s_ref[...] - m_new) * scale2)
        l_s[h] = l_s[h] * alpha + jnp.sum(p, axis=0, keepdims=True)
        pv = lax.dot_general(vt[h, :, pl.ds(start, rows)], p.astype(bf16), NN, preferred_element_type=f32)
        acc[h] = acc[h] * alpha + pv

    row_i = lax.broadcasted_iota(jnp.int32, (half, half), 0)
    col_i = lax.broadcasted_iota(jnp.int32, (half, half), 1)
    visible = row_i <= col_i
    own = pl.multiple_of(nprev * rows, rows)

    def diagonal(h):
        for a in range(2):
            qh = qaug[h, :, a * half:(a + 1) * half]
            nk = (a + 1) * half
            s = lax.dot_general(keys(h, own, nk), qh, NN, preferred_element_type=f32)
            tail = jnp.where(visible, s[a * half:, :], -jnp.inf)
            s = tail if a == 0 else jnp.concatenate([s[:half, :], tail], axis=0)
            m = jnp.max(s, axis=0, keepdims=True)
            p = jnp.exp2((s - m) * scale2)
            cols = slice(a * half, (a + 1) * half)
            m_s[h, :, cols] = m
            l_s[h, :, cols] = jnp.sum(p, axis=0, keepdims=True)
            acc[h, :, cols] = lax.dot_general(vt[h, :, pl.ds(own, nk)], p.astype(bf16), NN, preferred_element_type=f32)

    def group(g, carry):
        for h in range(G):
            lo = (h % 2) * nope
            qaug[h, lo:lo + nope, :] = qt_ref[g * G + h, :nope, :]
            qaug[h, 2 * nope:2 * nope + rot, :] = qt_ref[g * G + h, nope:, :]

        def up(b, c2):
            start = pl.multiple_of(b * rows, rows)
            ckb = ck_ref[pl.ds(start, rows), :256]
            for j in range(G // 4):
                wk = wuk_ref[pl.ds(pl.multiple_of((g * G + 4 * j) * nope, 4 * nope), 4 * nope), :]
                kk = lax.dot_general(ckb, wk, NT, preferred_element_type=f32).astype(bf16)
                kn[2 * j, pl.ds(start, rows), :] = kk[:, :128]
                kn[2 * j + 1, pl.ds(start, rows), :] = kk[:, 128:]
                wv = wuv_ref[pl.ds(pl.multiple_of((g * G + 4 * j) * vdim, 4 * vdim), 4 * vdim), :]
                vv = lax.dot_general(wv, ckb, NT, preferred_element_type=f32).astype(bf16)
                for i in range(4):
                    vt[4 * j + i, :, pl.ds(start, rows)] = vv[i * vdim:(i + 1) * vdim, :]
            return c2

        lax.fori_loop(0, nprev + 1, up, 0)
        for h in range(G):
            diagonal(h)

        @pl.when(nprev > 0)
        def _():
            scores(0, 0, s_a, c_a)

            def pair(t, c2):
                i0 = 2 * t
                h0, b0 = i0 // nprev, i0 % nprev
                i1 = i0 + 1
                h1, b1 = i1 // nprev, i1 % nprev
                i2 = jnp.minimum(i0 + 2, G * nprev - 1)
                h2, b2 = i2 // nprev, i2 % nprev
                scores(h1, b1, s_b, c_b)
                absorb(h0, b0, s_a, c_a)
                scores(h2, b2, s_a, c_a)
                absorb(h1, b1, s_b, c_b)
                return c2

            lax.fori_loop(0, G * nprev // 2, pair, 0)

        for j in range(G // 2):
            o2 = jnp.concatenate([acc[2 * j] / l_s[2 * j], acc[2 * j + 1] / l_s[2 * j + 1]], axis=0)
            o_nat[g * (G // 2) + j] = o2.T.astype(bf16)
        return carry

    lax.fori_loop(0, heads // G, group, 0)
    wo_copy.wait()
    npair = heads // 2
    o_all = jnp.concatenate([o_nat[j] for j in range(npair)], axis=1)
    d = wo.shape[1]
    for n in range(0, d, 512):
        out_ref[:, n:n + 512] = lax.dot_general(o_all, wo[:, n:n + 512], NN, preferred_element_type=f32).astype(bf16)


def attention(nprev, qt, ck, wukt, wuvt, wo, scale2):
    heads, qk, rows = qt.shape
    seq = ck.shape[0]
    vdim = wuvt.shape[0] // heads
    nope = wukt.shape[0] // heads
    rot = qk - nope
    G = ATTN_GROUP
    vm = pl.BlockSpec(memory_space=pltpu.VMEM)
    f32 = jnp.float32
    bf16 = jnp.bfloat16
    return pl.pallas_call(
        functools.partial(attention_kernel, scale2=scale2, rows=rows, nope=nope, rot=rot, vdim=vdim),
        out_shape=jax.ShapeDtypeStruct((rows, wo.shape[1]), bf16),
        in_specs=[pl.BlockSpec(memory_space=pltpu.SMEM), vm, vm, vm, vm, pl.BlockSpec(memory_space=pl.ANY)],
        out_specs=vm,
        scratch_shapes=[
            pltpu.VMEM((G, 256, rows), bf16),
            pltpu.VMEM((G // 2, seq, 128), bf16),
            pltpu.VMEM((G, vdim, seq), bf16),
            pltpu.VMEM((rows, rows), f32),
            pltpu.VMEM((rows, rows), f32),
            pltpu.VMEM((1, rows), f32),
            pltpu.VMEM((1, rows), f32),
            pltpu.VMEM((G, 1, rows), f32),
            pltpu.VMEM((G, 1, rows), f32),
            pltpu.VMEM((G, vdim, rows), f32),
            pltpu.VMEM((heads // 2, rows, 2 * vdim), bf16),
            pltpu.VMEM(wo.shape, bf16),
            pltpu.SemaphoreType.DMA,
        ],
        compiler_params=pltpu.CompilerParams(vmem_limit_bytes=60 * 1024 * 1024),
        cost_estimate=pl.CostEstimate(flops=40_000_000_000, bytes_accessed=40_000_000, transcendentals=30_000_000),
    )(nprev, qt, ck, wukt, wuvt, wo)


def solution(mesh):
    tok_spec = P(('dp', 'sp'))
    rows_spec = P(('dp', 'sp'), None)
    replicated = P()

    def local_step(tok_in, tok_pos, w_dq, g_q, w_uq, w_dkv, g_kv, w_uk, w_uv, w_o):
        rows = tok_in.shape[0]
        q_rank, num_heads, qk_dim = w_uq.shape
        kv_rank = g_kv.shape[0]
        rot_dim = w_dkv.shape[1] - kv_rank
        nope_dim = qk_dim - rot_dim
        v_dim = w_uv.shape[2]
        attn_scale = (0.1 * math.log(YARN_FACTOR) + 1.0) ** 2 / math.sqrt(qk_dim)
        f32 = jnp.float32
        angles = tok_pos.astype(f32)[:, None] * rope_freqs(rot_dim)[None, :]
        cos_t = jnp.cos(angles)
        sin_t = jnp.sin(angles)
        kv_lat = jnp.dot(tok_in, w_dkv, preferred_element_type=f32)
        cache_kv = rms_norm(kv_lat[:, :kv_rank], g_kv).astype(jnp.bfloat16)
        cache_pe = rotate_half(kv_lat[:, kv_rank:], cos_t, sin_t).astype(jnp.bfloat16)
        ck = jnp.concatenate([cache_kv, jnp.pad(cache_pe, ((0, 0), (0, 128 - rot_dim)))], axis=1)
        ck_all = lax.all_gather(ck, 'sp', axis=0, tiled=True)
        q_lat = rms_norm(jnp.dot(tok_in, w_dq, preferred_element_type=f32), g_q).astype(jnp.bfloat16)
        q_full = jnp.einsum('tc,che->het', q_lat, w_uq, preferred_element_type=f32)
        z1 = q_full[:, nope_dim:nope_dim + rot_dim // 2]
        z2 = q_full[:, nope_dim + rot_dim // 2:]
        ct, st = cos_t.T[None], sin_t.T[None]
        qt = jnp.concatenate([q_full[:, :nope_dim], z1 * ct - z2 * st, z2 * ct + z1 * st], axis=1).astype(jnp.bfloat16)
        wukt = jnp.transpose(w_uk, (1, 2, 0)).reshape(num_heads * nope_dim, kv_rank)
        wuvt = jnp.transpose(w_uv, (1, 2, 0)).reshape(num_heads * v_dim, kv_rank)
        nprev = lax.axis_index('sp').astype(jnp.int32)[None]
        attn_out = attention(nprev, qt, ck_all, wukt, wuvt, w_o.reshape(num_heads * v_dim, -1), attn_scale * math.log2(math.e))
        return attn_out, cache_kv, cache_pe

    return jax.shard_map(local_step, mesh=mesh, in_specs=(rows_spec, tok_spec, replicated, replicated, replicated, replicated, replicated, replicated, replicated, replicated), out_specs=(rows_spec, rows_spec, rows_spec), check_vma=False)
```

time: 386 us -> 135 us (0.35)
  matrix products: 174 us -> 12.5 us
  waiting for transfers between devices: 117 us -> 0.02 us
  Pallas kernels: 0 us -> 92.6 us
  local copies, waits for them, and re-layouts: 53 us -> 8.67 us
  starting transfers between devices: 23.9 us -> 0.04 us
  between operations: 0.85 us -> 14.2 us
    all_to_all x4 -> x0, waiting for transfers between devices: 117 us -> none  [the longest x1 38.9 us: local_step(): q_heads = lax.all_to_all(q_all, 'sp', 1, 0, tiled=True)]
    pallas_call x0 -> x1, Pallas kernels: none -> 92.6 us  [attention(): pl.pallas_call(functools.partial(attention_kernel, scale2=scale2, rows=ro...]
    sub x4 -> x0, matrix products: 81.7 us -> none  [block_attention(): attn_prob = jax.nn.softmax(logits, axis=-1).astype(jnp.bfloat16)]
    dot_general x7 -> x2, matrix products: 85.1 us -> 6.72 us  [the longest x1 4.39 us: local_step(): jnp.dot(tok_in, w_dq, preferred_element_type=f32)]
    all_to_all x4 -> x0, starting transfers between devices: 23.9 us -> none  [the longest x1 7.15 us: local_step(): q_heads = lax.all_to_all(q_all, 'sp', 1, 0, tiled=True)]
    all_to_all x5 -> x0, local copies, waits for them, and re-layouts: 23.1 us -> none  [the longest x2 10.3 us: local_step(): o_local = lax.all_to_all(o_heads, 'sp', 0, 1, tiled=True)]
    unnamed x25 -> x17, local copies, waits for them, and re-layouts: 16.7 us -> 5.84 us
    reshape x1 -> x0, local copies, waits for them, and re-layouts: 10.2 us -> none  [local_step(): lax.map(block_attention, jnp.arange(groups))]
  transfers between devices with their start and end apart: 4 -> 1, of which waited for: 4 -> 0; matrix products, arithmetic and copies ran while one was open for 7% -> 12% of each run, Pallas kernels for 0% -> 0%
where the time goes in v1:
time: 135 us
  Pallas kernels  92.6 us (69%)
  between operations  14.2 us (11%)
  matrix products  12.5 us (9%)
  local copies, waits for them, and re-layouts  8.67 us (6%)
  other arithmetic  6.67 us (5%)
    pallas_call x1, Pallas kernels, attention(): pl.pallas_call(functools.partial(attention_kernel, scale2=scale2, rows=ro...  92.6 us
    unnamed x17, local copies, waits for them, and re-layouts  5.84 us
    unnamed x1, matrix products  5.75 us
    dot_general x1, matrix products, local_step(): jnp.dot(tok_in, w_dq, preferred_element_type=f32)  4.39 us
  transfers between devices with their start and end apart: 1, of which 0 were waited for; matrix products, arithmetic and copies ran while one was open for 12% of the time, Pallas kernels for 0%

profile of v1, /device:TPU:3, one launch (start us, length us, event | category | flops | bytes accessed | tf_op | source)
XLA Modules:
  0.0 134.7 jit_solution(6857255790287453555)
XLA Ops:
  7.2 0.0 copy-start
  7.2 0.0 all-gather.2.cloned.1.call-start
  7.2 0.8 convert_element_type.14
  8.1 0.9 copy-done
  8.9 0.0 copy-start.5
  8.9 2.3 %fusion.13 = f32[512,288]{0,1:T(8,128)S(1)} fusion(bf16[512,2560]{1,0:T(8,128)(2,1)S(1)} %copy-done, bf16[2560,288]{0,1:T(8,128)(2,1)} %param.16), kind=kOutput, calls=%fused_computation.29 | convolution fusion | flops 754974720 | bytes 4685824 | tf_op jit(solution)/shard_map/dot_general | solution.py:210
  11.3 0.0 copy-start.6
  11.3 0.8 slice.31
  12.1 0.0 copy-done.5
  12.1 0.2 fusion.10
  12.3 0.0 copy-start.4
  12.3 0.6 copy-done.4
  12.9 0.1 copy.19
  13.1 1.2 copy.20
  14.3 0.1 multiply_reduce_fusion.1
  14.5 0.0 copy-done.6
  14.5 0.1 multiply_convert_fusion.2
  14.6 0.0 copy-start.3
  14.7 0.8 fusion.4
  15.5 0.0 all-gather.2.cloned.1.call-update
  15.5 0.0 copy-start.7
  15.5 4.4 %multiply_reduce_fusion = (f32[512]{0:T(512)S(1)}, f32[512,768]{1,0:T(8,128)S(1)}) fusion(bf16[512,2560]{1,0:T(8,128)(2,1)S(1)} %copy-done, bf16[2560,768]{1,0:T(8,128)(2,1)} %param.13), kind=kOutput, calls=%fused_computation.3 | convolution fusion | flops 2014051840 | bytes 8128512 | tf_op jit(solution)/shard_map/dot_general | solution.py:215
  19.9 0.0 copy-done.3
  19.9 0.0 copy-done.7
  19.9 5.7 %fusion = f32[512,3840]{0,1:S(1)} fusion(bf16[768,3840]{0,1:T(8,128)(2,1)} %bitcast.20, f32[512,768]{1,0:T(8,128)S(1)} %get-tuple-element.13, f32[768]{0:T(1024)S(1)} %copy-done.7, f32[512]{0:T(512)S(1)} %add_rsqrt_fusion.1), kind=kOutput, calls=%fused_computation.6 | convolution fusion | flops 3021078528 | bytes 15340544
  25.7 0.0 copy-start.2
  25.7 3.0 %copy-done.2 = f32[512,3840]{0,1} copy-done((f32[512,3840]{0,1}, f32[512,3840]{0,1:S(1)}, u32[]{:S(2)}) %copy-start.2) | copy-done | bytes 7864344
  28.7 1.9 %slice.43 = bf16[40,64,512]{2,1,0:T(8,128)(2,1)} slice(f32[40,96,512]{2,1,0:T(8,128)S(1)} %bitcast.17), slice={[0:40], [0:64], [0:512]} | slice | bytes 5242880 | tf_op jit(solution)/shard_map/slice | solution.py:220
  30.6 0.0 copy-start.1
  30.6 0.2 multiply_cosine_fusion.1
  30.8 2.3 %subtract_convert_fusion = (bf16[40,16,512]{2,1,0:T(8,128)(2,1)S(1)}, bf16[40,16,512]{2,1,0:T(8,128)(2,1)S(1)}) fusion(f32[40,96,512]{2,1,0:T(8,128)} %bitcast.18, f32[16,512]{1,0:T(8,128)S(1)} %get-tuple-element.11, f32[16,512]{1,0:T(8,128)S(1)} %get-tuple-element.10), kind=kLoop, calls=%fused_computation.5 | loop fusion | flops 2621440 | bytes 3997696 | tf_op jit(solution)/shard_map/convert.3
  33.1 0.0 copy-done.1
  33.2 2.0 %pad_maximum_fusion.qt_ref = bf16[40,96,512]{2,1,0:T(8,128)(2,1)} fusion(bf16[40,16,512]{2,1,0:T(8,128)(2,1)S(1)} %get-tuple-element.7, bf16[40,16,512]{2,1,0:T(8,128)(2,1)S(1)} %get-tuple-element.6, bf16[40,64,512]{2,1,0:T(8,128)(2,1)S(1)} %copy-done.1), kind=kLoop, calls=%fused_computation.1 | loop fusion | flops 11796480 | bytes 7864320 | tf_op jit(solution)/shard_map/concatenate | solution.py:220
  35.2 0.0 all-gather.2.cloned.1.call-done.ck_ref
  35.2 92.6 %shard_map.130 = bf16[512,2560]{1,0:T(8,128)(2,1)} custom-call(s32[1]{0:T(128)} %bitcast.nprev_ref, bf16[40,96,512]{2,1,0:T(8,128)(2,1)} %pad_maximum_fusion.qt_ref, bf16[2048,384]{1,0:T(8,128)(2,1)} %all-gather.2.cloned.1.call-done.ck_ref, bf16[2560,256]{1,0:T(8,128)(2,1)} %bitcast.21, bf16[2560,256]{1,0:T(8,128)(2,1)} %bitcast.22, bf16[2560,2560]{1,0:T(8,128)(2,1)} %bitcast.19), custom_call_target="tpu_custom_call" | custom-call | flops 40000000000 | bytes 40000000 | tf_op jit(solution)/shard_map/pallas_call | solution.py:168
  (3 shorter events, 0.0 us)
Async XLA Ops:
  7.2 1.8 %copy-start = (bf16[512,2560]{1,0:T(8,128)(2,1)S(1)}, bf16[512,2560]{1,0:T(8,128)(2,1)}, u32[]{:S(2)}) copy-start(bf16[512,2560]{1,0:T(8,128)(2,1)} %param.11) | copy-start | bytes 7864324
  7.2 28.0 %all-gather.2.cloned.1.call-start = ((), (), s32[]{:S(2)}) async-start(), calls=%async_computation | async-start | bytes 1966080 | tf_op jit(solution)/shard_map/all_gather | solution.py:214
  8.9 3.2 %copy-start.5 = (f32[16]{0:T(128)S(1)}, f32[16]{0:T(128)}, u32[]{:S(2)}) copy-start(f32[16]{0:T(128)} %constant.19.clone) | copy-start | bytes 196
  11.3 3.2 %copy-start.6 = (f32[256]{0:T(256)S(1)}, f32[256]{0:T(256)}, u32[]{:S(2)}) copy-start(f32[256]{0:T(256)} %param.17) | copy-start | bytes 3076
  12.3 0.6 copy-start.4
  14.6 5.3 %copy-start.3 = (bf16[512,256]{1,0:T(8,128)(2,1)}, bf16[512,256]{1,0:T(8,128)(2,1)S(1)}, u32[]{:S(2)}) copy-start(bf16[512,256]{1,0:T(8,128)(2,1)S(1)} %multiply_convert_fusion.2) | copy-start | bytes 786436
  15.5 4.4 %copy-start.7 = (f32[768]{0:T(1024)S(1)}, f32[768]{0:T(1024)}, u32[]{:S(2)}) copy-start(f32[768]{0:T(1024)} %param.14) | copy-start | bytes 9220
  25.7 3.1 %copy-start.2 = (f32[512,3840]{0,1}, f32[512,3840]{0,1:S(1)}, u32[]{:S(2)}) copy-start(f32[512,3840]{0,1:S(1)} %fusion) | copy-start | bytes 23592964
  30.6 2.5 %copy-start.1 = (bf16[40,64,512]{2,1,0:T(8,128)(2,1)S(1)}, bf16[40,64,512]{2,1,0:T(8,128)(2,1)}, u32[]{:S(2)}) copy-start(bf16[40,64,512]{2,1,0:T(8,128)(2,1)} %slice.43) | copy-start | bytes 7864324
Sparse Core Ops, SparseCore 0:
  15.6 16.8 all-gather.1

commit v2 on v1

--- a/solution.py
+++ b/solution.py
@@ -41,62 +41,90 @@
     return act_in * lax.rsqrt(mean_sq + NORM_EPS) * gain
 
 
-ATTN_GROUP = 8
+HEAD_GROUP = 20
+QUAD = 4
 
 
 def attention_kernel(nprev_ref, qt_ref, ck_ref, wuk_ref, wuv_ref, wo_hbm, out_ref,
-                     qaug, kn, vt, s_a, s_b, c_a, c_b, m_s, l_s, acc, o_nat, wo, wo_sem,
+                     qaug, kn, vt, s_buf, c_buf, p_buf, al_buf, m_s, acc, o_nat, wo, wo_sem,
                      *, scale2, rows, nope, rot, vdim):
     nprev = nprev_ref[0]
     heads = qt_ref.shape[0]
-    G = ATTN_GROUP
+    G = HEAD_GROUP
+    nq = G // QUAD
     wo_copy = pltpu.make_async_copy(wo_hbm, wo, wo_sem)
     wo_copy.start()
     qaug[...] = jnp.zeros_like(qaug)
+    vt[:, vdim:, :] = jnp.ones((vt.shape[0], vt.shape[1] - vdim, vt.shape[2]), vt.dtype)
     NT = (((1,), (1,)), ((), ()))
     NN = (((1,), (0,)), ((), ()))
     f32 = jnp.float32
     bf16 = jnp.bfloat16
     half = rows // 2
-
-    def keys(h, start, size):
-        return jnp.concatenate([kn[h // 2, pl.ds(start, size), :], ck_ref[pl.ds(start, size), 256:384]], axis=1)
-
-    def scores(h, blk, s_ref, c_ref):
-        start = pl.multiple_of(blk * rows, rows)
-        s = lax.dot_general(keys(h, start, rows), qaug[h], NN, preferred_element_type=f32)
-        s_ref[...] = s
-        c_ref[...] = jnp.max(s, axis=0, keepdims=True)
-
-    def absorb(h, blk, s_ref, c_ref):
-        start = pl.multiple_of(blk * rows, rows)
-        m_old = m_s[h]
-        m_new = jnp.maximum(m_old, c_ref[...])
-        m_s[h] = m_new
-        alpha = jnp.exp2((m_old - m_new) * scale2)
-        p = jnp.exp2((s_ref[...] - m_new) * scale2)
-        l_s[h] = l_s[h] * alpha + jnp.sum(p, axis=0, keepdims=True)
-        pv = lax.dot_general(vt[h, :, pl.ds(start, rows)], p.astype(bf16), NN, preferred_element_type=f32)
-        acc[h] = acc[h] * alpha + pv
-
+    FULL = ((0, 0), (1, 0), (0, 1), (1, 1))
+    OWN = ((0, 0), (0, 1), (1, 1))
     row_i = lax.broadcasted_iota(jnp.int32, (half, half), 0)
     col_i = lax.broadcasted_iota(jnp.int32, (half, half), 1)
-    visible = row_i <= col_i
-    own = pl.multiple_of(nprev * rows, rows)
-
-    def diagonal(h):
+
+    def cols(a):
+        return slice(a * half, (a + 1) * half)
+
+    def score_stage(u, quad, blk, pieces):
+        start = pl.multiple_of(blk * rows, rows)
+        tops = [None, None]
+        for k, a in pieces:
+            lhs = jnp.concatenate([kn[quad * (QUAD // 2) + u // 2, pl.ds(start + k * half, half), :],
+                                   ck_ref[pl.ds(start + k * half, half), 256:384]], axis=1)
+            s = lax.dot_general(lhs, qaug[quad * QUAD + u, :, cols(a)], NN, preferred_element_type=f32)
+            if pieces is OWN and k == a:
+                s = jnp.where(row_i <= col_i, s, -jnp.inf)
+            s_buf[u, cols(k), cols(a)] = s
+            top = jnp.max(s, axis=0, keepdims=True)
+            tops[a] = top if tops[a] is None else jnp.maximum(tops[a], top)
         for a in range(2):
-            qh = qaug[h, :, a * half:(a + 1) * half]
-            nk = (a + 1) * half
-            s = lax.dot_general(keys(h, own, nk), qh, NN, preferred_element_type=f32)
-            tail = jnp.where(visible, s[a * half:, :], -jnp.inf)
-            s = tail if a == 0 else jnp.concatenate([s[:half, :], tail], axis=0)
-            m = jnp.max(s, axis=0, keepdims=True)
-            p = jnp.exp2((s - m) * scale2)
-            cols = slice(a * half, (a + 1) * half)
-            m_s[h, :, cols] = m
-            l_s[h, :, cols] = jnp.sum(p, axis=0, keepdims=True)
-            acc[h, :, cols] = lax.dot_general(vt[h, :, pl.ds(own, nk)], p.astype(bf16), NN, preferred_element_type=f32)
+            c_buf[u, :, cols(a)] = tops[a]
+
+    def exp_stage(u, quad, pieces):
+        h = quad * QUAD + u
+        m_new = c_buf[u]
+        if pieces is FULL:
+            m_old = m_s[h]
+            m_new = jnp.maximum(m_old, m_new)
+            al_buf[u] = jnp.exp2((m_old - m_new) * scale2)
+        m_s[h] = m_new
+        for k, a in pieces:
+            p_buf[u, cols(k), cols(a)] = jnp.exp2((s_buf[u, cols(k), cols(a)] - m_new[:, cols(a)]) * scale2).astype(bf16)
+
+    def value_stage(u, quad, blk, pieces):
+        h = quad * QUAD + u
+        start = pl.multiple_of(blk * rows, rows)
+        for a in range(2):
+            nk = rows if pieces is FULL else (a + 1) * half
+            t = lax.dot_general(vt[h, :, pl.ds(start, nk)], p_buf[u, :nk, cols(a)], NN, preferred_element_type=f32)
+            if pieces is FULL:
+                t = t + acc[h, :, cols(a)] * al_buf[u, :, cols(a)]
+            acc[h, :, cols(a)] = t
+
+    def pipeline(count, place, pieces):
+        def step(i, first, last):
+            for u in range(QUAD):
+                if first < 1:
+                    value_stage(u, *place(i - 2), pieces)
+                if first < 2 and last < 2:
+                    exp_stage(u, place(i - 1)[0], pieces)
+                if last < 1:
+                    score_stage(u, *place(i), pieces)
+
+        step(0, 2, 0)
+        step(1, 1, 0)
+
+        def body(i, c):
+            step(i, 0, 0)
+            return c
+
+        lax.fori_loop(2, count, body, 0)
+        step(count, 0, 1)
+        step(count + 1, 0, 2)
 
     def group(g, carry):
         for h in range(G):
@@ -107,7 +135,7 @@
         def up(b, c2):
             start = pl.multiple_of(b * rows, rows)
             ckb = ck_ref[pl.ds(start, rows), :256]
-            for j in range(G // 4):
+            for j in range(nq):
                 wk = wuk_ref[pl.ds(pl.multiple_of((g * G + 4 * j) * nope, 4 * nope), 4 * nope), :]
                 kk = lax.dot_general(ckb, wk, NT, preferred_element_type=f32).astype(bf16)
                 kn[2 * j, pl.ds(start, rows), :] = kk[:, :128]
@@ -115,34 +143,18 @@
                 wv = wuv_ref[pl.ds(pl.multiple_of((g * G + 4 * j) * vdim, 4 * vdim), 4 * vdim), :]
                 vv = lax.dot_general(wv, ckb, NT, preferred_element_type=f32).astype(bf16)
                 for i in range(4):
-                    vt[4 * j + i, :, pl.ds(start, rows)] = vv[i * vdim:(i + 1) * vdim, :]
+                    vt[4 * j + i, :vdim, pl.ds(start, rows)] = vv[i * vdim:(i + 1) * vdim, :]
             return c2
 
         lax.fori_loop(0, nprev + 1, up, 0)
-        for h in range(G):
-            diagonal(h)
+        pipeline(nq, lambda i: (i, nprev), OWN)
 
         @pl.when(nprev > 0)
         def _():
-            scores(0, 0, s_a, c_a)
-
-            def pair(t, c2):
-                i0 = 2 * t
-                h0, b0 = i0 // nprev, i0 % nprev
-                i1 = i0 + 1
-                h1, b1 = i1 // nprev, i1 % nprev
-                i2 = jnp.minimum(i0 + 2, G * nprev - 1)
-                h2, b2 = i2 // nprev, i2 % nprev
-                scores(h1, b1, s_b, c_b)
-                absorb(h0, b0, s_a, c_a)
-                scores(h2, b2, s_a, c_a)
-                absorb(h1, b1, s_b, c_b)
-                return c2
-
-            lax.fori_loop(0, G * nprev // 2, pair, 0)
+            pipeline(nq * nprev, lambda i: (lax.rem(i, nq), lax.div(i, nq)), FULL)
 
         for j in range(G // 2):
-            o2 = jnp.concatenate([acc[2 * j] / l_s[2 * j], acc[2 * j + 1] / l_s[2 * j + 1]], axis=0)
+            o2 = jnp.concatenate([acc[h, :vdim, :] / acc[h, vdim:vdim + 1, :] for h in (2 * j, 2 * j + 1)], axis=0)
             o_nat[g * (G // 2) + j] = o2.T.astype(bf16)
         return carry
 
@@ -161,7 +173,7 @@
     vdim = wuvt.shape[0] // heads
     nope = wukt.shape[0] // heads
     rot = qk - nope
-    G = ATTN_GROUP
+    G = HEAD_GROUP
     vm = pl.BlockSpec(memory_space=pltpu.VMEM)
     f32 = jnp.float32
     bf16 = jnp.bfloat16
@@ -173,19 +185,18 @@
         scratch_shapes=[
             pltpu.VMEM((G, 256, rows), bf16),
             pltpu.VMEM((G // 2, seq, 128), bf16),
-            pltpu.VMEM((G, vdim, seq), bf16),
-            pltpu.VMEM((rows, rows), f32),
-            pltpu.VMEM((rows, rows), f32),
-            pltpu.VMEM((1, rows), f32),
-            pltpu.VMEM((1, rows), f32),
+            pltpu.VMEM((G, vdim + 16, seq), bf16),
+            pltpu.VMEM((QUAD, rows, rows), f32),
+            pltpu.VMEM((QUAD, 1, rows), f32),
+            pltpu.VMEM((QUAD, rows, rows), bf16),
+            pltpu.VMEM((QUAD, 1, rows), f32),
             pltpu.VMEM((G, 1, rows), f32),
-            pltpu.VMEM((G, 1, rows), f32),
-            pltpu.VMEM((G, vdim, rows), f32),
+            pltpu.VMEM((G, vdim + 16, rows), f32),
             pltpu.VMEM((heads // 2, rows, 2 * vdim), bf16),
             pltpu.VMEM(wo.shape, bf16),
             pltpu.SemaphoreType.DMA,
         ],
-        compiler_params=pltpu.CompilerParams(vmem_limit_bytes=60 * 1024 * 1024),
+        compiler_params=pltpu.CompilerParams(vmem_limit_bytes=62 * 1024 * 1024),
         cost_estimate=pl.CostEstimate(flops=40_000_000_000, bytes_accessed=40_000_000, transcendentals=30_000_000),
     )(nprev, qt, ck, wukt, wuvt, wo)
 

time: 135 us -> 106 us (0.79)
  Pallas kernels: 92.6 us -> 65.1 us
  local copies, waits for them, and re-layouts: 8.67 us -> 5.92 us
    pallas_call x1, Pallas kernels: 92.6 us -> 65.1 us  [attention(): pl.pallas_call(functools.partial(attention_kernel, scale2=scale2, rows=ro...]
    unnamed x17, local copies, waits for them, and re-layouts: 5.84 us -> 3.87 us
  transfers between devices with their start and end apart: 1 -> 1, of which waited for: 0 -> 0; matrix products, arithmetic and copies ran while one was open for 12% -> 16% of each run, Pallas kernels for 0% -> 0%
where the time goes in v2:
time: 106 us
  Pallas kernels  65.1 us (61%)
  between operations  14.2 us (13%)
  matrix products  13.6 us (13%)
  other arithmetic  6.63 us (6%)
  local copies, waits for them, and re-layouts  5.92 us (6%)
    pallas_call x1, Pallas kernels, attention(): pl.pallas_call(functools.partial(attention_kernel, scale2=scale2, rows=ro...  65.1 us
    unnamed x1, matrix products  5.75 us
    dot_general x1, matrix products, local_step(): jnp.dot(tok_in, w_dq, preferred_element_type=f32)  5.19 us
    unnamed x17, local copies, waits for them, and re-layouts  3.87 us
    dot_general x1, matrix products, local_step(): kv_lat = jnp.dot(tok_in, w_dkv, preferred_element_type=f32)  2.7 us
    another operation x2, other arithmetic  2.48 us
  transfers between devices with their start and end apart: 1, of which 0 were waited for; matrix products, arithmetic and copies ran while one was open for 16% of the time, Pallas kernels for 0%

profile of v2, /device:TPU:3, one launch (start us, length us, event | category | flops | bytes accessed | tf_op | source)
XLA Modules:
  0.0 105.6 jit_solution(4369826434827164532)
XLA Ops:
  7.2 0.0 copy-start
  7.2 0.0 all-gather.2.cloned.1.call-start
  7.2 0.8 convert_element_type.14
  8.0 0.5 copy-done
  8.6 0.0 copy-start.5
  8.6 2.7 %fusion.13 = f32[512,288]{0,1:T(8,128)S(1)} fusion(bf16[512,2560]{1,0:T(8,128)(2,1)} %param.11, bf16[2560,288]{0,1:T(8,128)(2,1)S(1)} %copy-done), kind=kOutput, calls=%fused_computation.29 | convolution fusion | flops 754974720 | bytes 4685824 | tf_op jit(solution)/shard_map/dot_general | solution.py:221
  11.3 0.0 copy-start.6
  11.3 0.0 copy-done.5
  11.3 0.2 fusion.10
  11.6 0.0 copy-start.4
  11.6 0.1 copy.19
  11.7 0.2 copy.20
  11.9 0.1 multiply_reduce_fusion.1
  12.1 0.0 copy-done.6
  12.1 0.1 multiply_convert_fusion.2
  12.2 0.0 copy-start.3
  12.2 0.8 fusion.4
  13.1 0.0 all-gather.2.cloned.1.call-update
  13.1 0.0 copy-start.7
  13.1 5.2 %multiply_reduce_fusion = (f32[512]{0:T(512)S(1)}, f32[512,768]{1,0:T(8,128)S(1)}) fusion(bf16[512,2560]{1,0:T(8,128)(2,1)} %param.11, bf16[2560,768]{1,0:T(8,128)(2,1)} %param.13), kind=kOutput, calls=%fused_computation.3 | convolution fusion | flops 2014051840 | bytes 8128512 | tf_op jit(solution)/shard_map/dot_general | solution.py:226
  18.3 0.0 copy-done.4
  18.3 0.0 copy-done.3
  18.3 0.0 copy-done.7
  18.3 5.7 %fusion = f32[512,3840]{0,1:S(1)} fusion(bf16[768,3840]{0,1:T(8,128)(2,1)} %bitcast.20, f32[512,768]{1,0:T(8,128)S(1)} %get-tuple-element.13, f32[768]{0:T(1024)S(1)} %copy-done.7, f32[512]{0:T(512)S(1)} %add_rsqrt_fusion.1), kind=kOutput, calls=%fused_computation.6 | convolution fusion | flops 3021078528 | bytes 15340544
  24.1 0.0 copy-start.2
  24.1 3.0 %copy-done.2 = f32[512,3840]{0,1} copy-done((f32[512,3840]{0,1}, f32[512,3840]{0,1:S(1)}, u32[]{:S(2)}) %copy-start.2) | copy-done | bytes 7864344
  27.1 1.9 %slice.43 = bf16[40,64,512]{2,1,0:T(8,128)(2,1)} slice(f32[40,96,512]{2,1,0:T(8,128)S(1)} %bitcast.17), slice={[0:40], [0:64], [0:512]} | slice | bytes 5242880 | tf_op jit(solution)/shard_map/slice | solution.py:231
  29.0 0.0 copy-start.1
  29.0 0.2 multiply_cosine_fusion.1
  29.2 2.3 %subtract_convert_fusion = (bf16[40,16,512]{2,1,0:T(8,128)(2,1)S(1)}, bf16[40,16,512]{2,1,0:T(8,128)(2,1)S(1)}) fusion(f32[40,96,512]{2,1,0:T(8,128)} %bitcast.18, f32[16,512]{1,0:T(8,128)S(1)} %get-tuple-element.11, f32[16,512]{1,0:T(8,128)S(1)} %get-tuple-element.10), kind=kLoop, calls=%fused_computation.5 | loop fusion | flops 2621440 | bytes 3997696 | tf_op jit(solution)/shard_map/convert.3
  31.5 0.0 copy-done.1
  31.6 2.0 %pad_maximum_fusion.qt_ref = bf16[40,96,512]{2,1,0:T(8,128)(2,1)} fusion(bf16[40,16,512]{2,1,0:T(8,128)(2,1)S(1)} %get-tuple-element.7, bf16[40,16,512]{2,1,0:T(8,128)(2,1)S(1)} %get-tuple-element.6, bf16[40,64,512]{2,1,0:T(8,128)(2,1)S(1)} %copy-done.1), kind=kLoop, calls=%fused_computation.1 | loop fusion | flops 11796480 | bytes 7864320 | tf_op jit(solution)/shard_map/concatenate | solution.py:231
  33.6 0.0 all-gather.2.cloned.1.call-done.ck_ref
  33.6 65.1 %shard_map.130 = bf16[512,2560]{1,0:T(8,128)(2,1)} custom-call(s32[1]{0:T(128)} %bitcast.nprev_ref, bf16[40,96,512]{2,1,0:T(8,128)(2,1)} %pad_maximum_fusion.qt_ref, bf16[2048,384]{1,0:T(8,128)(2,1)} %all-gather.2.cloned.1.call-done.ck_ref, bf16[2560,256]{1,0:T(8,128)(2,1)} %bitcast.21, bf16[2560,256]{1,0:T(8,128)(2,1)} %bitcast.22, bf16[2560,2560]{1,0:T(8,128)(2,1)} %bitcast.19), custom_call_target="tpu_custom_call" | custom-call | flops 40000000000 | bytes 40000000 | tf_op jit(solution)/shard_map/pallas_call | solution.py:180
  (4 shorter events, 0.1 us)
Async XLA Ops:
  7.2 1.4 %copy-start = (bf16[2560,288]{0,1:T(8,128)(2,1)S(1)}, bf16[2560,288]{0,1:T(8,128)(2,1)}, u32[]{:S(2)}) copy-start(bf16[2560,288]{0,1:T(8,128)(2,1)} %param.16) | copy-start | bytes 4423684
  7.2 26.4 %all-gather.2.cloned.1.call-start = ((), (), s32[]{:S(2)}) async-start(), calls=%async_computation | async-start | bytes 1966080 | tf_op jit(solution)/shard_map/all_gather | solution.py:225
  8.6 2.8 %copy-start.5 = (f32[16]{0:T(128)S(1)}, f32[16]{0:T(128)}, u32[]{:S(2)}) copy-start(f32[16]{0:T(128)} %constant.19.clone) | copy-start | bytes 196
  11.3 0.8 copy-start.6
  11.6 6.7 %copy-start.4 = (bf16[512,32]{0,1:T(8,128)(2,1)}, bf16[512,32]{0,1:T(8,128)(2,1)S(1)}, u32[]{:S(2)}) copy-start(bf16[512,32]{0,1:T(8,128)(2,1)S(1)} %pad_maximum_fusion.1) | copy-start | bytes 98308
  12.2 6.1 %copy-start.3 = (bf16[512,256]{1,0:T(8,128)(2,1)}, bf16[512,256]{1,0:T(8,128)(2,1)S(1)}, u32[]{:S(2)}) copy-start(bf16[512,256]{1,0:T(8,128)(2,1)S(1)} %multiply_convert_fusion.2) | copy-start | bytes 786436
  13.1 5.2 %copy-start.7 = (f32[768]{0:T(1024)S(1)}, f32[768]{0:T(1024)}, u32[]{:S(2)}) copy-start(f32[768]{0:T(1024)} %param.14) | copy-start | bytes 9220
  24.1 3.1 %copy-start.2 = (f32[512,3840]{0,1}, f32[512,3840]{0,1:S(1)}, u32[]{:S(2)}) copy-start(f32[512,3840]{0,1:S(1)} %fusion) | copy-start | bytes 23592964
  29.0 2.5 %copy-start.1 = (bf16[40,64,512]{2,1,0:T(8,128)(2,1)S(1)}, bf16[40,64,512]{2,1,0:T(8,128)(2,1)}, u32[]{:S(2)}) copy-start(bf16[40,64,512]{2,1,0:T(8,128)(2,1)} %slice.43) | copy-start | bytes 7864324
Sparse Core Ops, SparseCore 0:
  13.2 16.8 all-gather.1

commit v3 on v0

v3 whole, which is shorter than its diff:
```python
import functools
import math
import jax
import jax.numpy as jnp
from jax import lax
from jax.experimental import pallas as pl
from jax.experimental.pallas import tpu as pltpu
from jax.sharding import PartitionSpec as P

ROPE_THETA = 10000.0
YARN_FACTOR = 40.0
ORIG_CTX = 4096.0
BETA_FAST = 32.0
BETA_SLOW = 1.0
NORM_EPS = 1e-6


def rope_freqs(rot_dim):
    half_dim = rot_dim // 2
    log_base = 2.0 * math.log(ROPE_THETA)
    low_idx = max(math.floor(rot_dim * math.log(ORIG_CTX / (BETA_FAST * 2.0 * math.pi)) / log_base), 0)
    high_idx = min(math.ceil(rot_dim * math.log(ORIG_CTX / (BETA_SLOW * 2.0 * math.pi)) / log_base), half_dim - 1)
    spread = max(high_idx - low_idx, 0.001)
    freq_list = []
    for freq_idx in range(half_dim):
        base_freq = ROPE_THETA ** (-2.0 * freq_idx / rot_dim)
        ramp_val = min(max((freq_idx - low_idx) / spread, 0.0), 1.0)
        freq_list.append(base_freq / YARN_FACTOR * ramp_val + base_freq * (1.0 - ramp_val))
    return jnp.asarray(freq_list, dtype=jnp.float32)


GROUP = 8
SLOTS = 3
HELPED = (2, 1)


def layer_kernel(trig_in, gq_ref, gkv_ref, x_hbm, wdkv_hbm, wdq_hbm, wuq_hbm, wuk_hbm, wuv_hbm,
                 o_hbm, ckv_out, cpe_out,
                 x, wdkv, wdq, wuq, wuk, wuv, qlat, trig, ckv, pet, pen, qaug, kn, vt,
                 s_buf, c_buf, p_buf, al_buf, m_s, acc, o_nat, o_help,
                 load_sem, c_send, c_recv, pe_send, pe_recv, q_send, q_recv, t_send, t_recv, o_send, o_recv, out_sem,
                 *, scale2, rows, nope, rot, vdim, heads, groups):
    f32 = jnp.float32
    bf16 = jnp.bfloat16
    NT = (((1,), (1,)), ((), ()))
    NN = (((1,), (0,)), ((), ()))
    half = rows // 2
    qk = nope + rot
    pairs = GROUP // 2
    ngroup = heads // GROUP
    me = lax.axis_index('sp')
    partner = groups - 1 - me
    given = jnp.where(me == groups - 1, HELPED[0], jnp.where(me == groups - 2, HELPED[1], 0))
    helped = jnp.where(me == 0, HELPED[0], jnp.where(me == 1, HELPED[1], 0))
    n_own = ngroup - given
    n_all = n_own + helped

    loads = [pltpu.make_async_copy(s, d, load_sem.at[i]) for i, (s, d) in enumerate(
        ((x_hbm, x), (wdkv_hbm, wdkv), (wdq_hbm, wdq), (wuq_hbm, wuq), (wuk_hbm, wuk), (wuv_hbm, wuv)))]
    for c in loads:
        c.start()
    barrier = pltpu.get_barrier_semaphore()
    for d in range(1, groups):
        pl.semaphore_signal(barrier, inc=1, device_id={'sp': lax.rem(me + d, groups)}, device_id_type=pl.DeviceIdType.MESH)

    def remote(s, d, ssem, rsem, to):
        return pltpu.make_async_remote_copy(src_ref=s, dst_ref=d, send_sem=ssem, recv_sem=rsem,
                                            device_id={'sp': to}, device_id_type=pl.DeviceIdType.MESH)

    def latent_copies(origin, to):
        return (remote(ckv.at[origin], ckv.at[origin], c_send.at[to], c_recv.at[origin], to),
                remote(pet.at[origin], pet.at[origin], pe_send.at[to], pe_recv.at[origin], to))

    def query_copies(to):
        return (remote(qlat.at[0], qlat.at[1], q_send, q_recv, to),
                remote(trig.at[0], trig.at[1], t_send, t_recv, to))

    def start(copies):
        for c in copies:
            c.start()

    def received(origin):
        for c in latent_copies(origin, me):
            c.wait_recv()
        unpack_rope(origin)

    def unpack_rope(origin):
        wide = jnp.concatenate([pet[origin].astype(f32), jnp.zeros((128 - rot, rows), f32)], axis=0)
        pen[origin] = wide.T.astype(bf16)

    trig[0] = trig_in[...]
    hr = rot // 2
    loads[0].wait()
    loads[1].wait()
    kvt = lax.dot_general(wdkv[...], x[...], NT, preferred_element_type=f32)
    rank = ckv.shape[2]
    a = kvt[:rank]
    norm = a * lax.rsqrt(jnp.sum(a * a, axis=0, keepdims=True) / rank + NORM_EPS) * gkv_ref[...]
    c_own = norm.T.astype(bf16)
    ckv[me] = c_own
    ckv_out[...] = c_own
    z1, z2 = kvt[rank:rank + hr], kvt[rank + hr:]
    cos_t, sin_t = trig_in[:hr], trig_in[hr:]
    pe_own = jnp.concatenate([z1 * cos_t - z2 * sin_t, z2 * cos_t + z1 * sin_t], axis=0).astype(bf16)
    pet[me] = pe_own
    cpe_out[...] = pe_own
    loads[2].wait()
    ql = lax.dot_general(x[...], wdq[...], NN, preferred_element_type=f32)
    qrank = ql.shape[1]
    ql = ql * lax.rsqrt(jnp.sum(ql * ql, axis=1, keepdims=True) / qrank + NORM_EPS) * gq_ref[...]
    qlat[0] = ql.astype(bf16)
    pl.semaphore_wait(barrier, groups - 1)

    @pl.when(me == 0)
    def _():
        for t in (1, 3, 2):
            start(latent_copies(me, t))

    @pl.when(me == 1)
    def _():
        for t in (0, 2, 3):
            start(latent_copies(me, t))

    @pl.when(me == 2)
    def _():
        for t in (3, 0):
            start(latent_copies(me, t))

    unpack_rope(me)
    qaug[...] = jnp.zeros_like(qaug)
    vt[:, vdim:, :] = jnp.ones((vt.shape[0], vt.shape[1] - vdim, vt.shape[2]), vt.dtype)
    for c in loads[3:]:
        c.wait()

    @pl.when(me == 3)
    def _():
        start(query_copies(0))
        start(latent_copies(me, 0))

    FULL = ((0, 0), (1, 0), (0, 1), (1, 1))
    OWN = ((0, 0), (0, 1), (1, 1))
    row_i = lax.broadcasted_iota(jnp.int32, (half, half), 0)
    col_i = lax.broadcasted_iota(jnp.int32, (half, half), 1)

    def cols(i):
        return slice(i * half, (i + 1) * half)

    def score_stage(u, blk, own):
        tops = [None, None]
        for k, i in (OWN if own else FULL):
            lhs = jnp.concatenate([kn[u // 2, pl.ds(pl.multiple_of(blk * rows + k * half, half), half), :], pen[blk, cols(k), :]], axis=1)
            s = lax.dot_general(lhs, qaug[u, :, cols(i)], NN, preferred_element_type=f32)
            if own and k == i:
                s = jnp.where(row_i <= col_i, s, -jnp.inf)
            s_buf[u, cols(k), cols(i)] = s
            top = jnp.max(s, axis=0, keepdims=True)
            tops[i] = top if tops[i] is None else jnp.maximum(tops[i], top)
        if own:
            s_buf[u, cols(1), cols(0)] = jnp.full((half, half), -jnp.inf, f32)
        for i in range(2):
            c_buf[u, :, cols(i)] = tops[i]

    def exp_stage(u, slot):
        h = slot * GROUP + u
        m_old = m_s[h]
        m_new = jnp.maximum(m_old, c_buf[u])
        al_buf[u] = jnp.exp2((m_old - m_new) * scale2)
        m_s[h] = m_new
        for k, i in FULL:
            p_buf[u, cols(k), cols(i)] = jnp.exp2((s_buf[u, cols(k), cols(i)] - m_new[:, cols(i)]) * scale2).astype(bf16)

    def value_stage(u, slot, blk):
        h = slot * GROUP + u
        v = vt[h, :, pl.ds(pl.multiple_of(blk * rows, rows), rows)]
        for i in range(2):
            t = lax.dot_general(v, p_buf[u, :, cols(i)], NN, preferred_element_type=f32)
            acc[h, :, cols(i)] = t + acc[h, :, cols(i)] * al_buf[u, :, cols(i)]

    def output_copy(grp):
        return pltpu.make_async_copy(o_nat.at[pl.ds(grp * pairs, pairs)], o_hbm.at[pl.ds(grp * pairs, pairs)], out_sem.at[grp])

    def help_copy(k):
        grp = ngroup - helped + k
        return remote(o_help.at[k], o_nat.at[pl.ds(grp * pairs, pairs)], o_send.at[k], o_recv.at[k], partner)

    def finish(slot, gi):
        outs = []
        for j in range(pairs):
            t = jnp.concatenate([acc[slot * GROUP + h, :vdim, :] / acc[slot * GROUP + h, vdim:vdim + 1, :] for h in (2 * j, 2 * j + 1)], axis=0)
            outs.append(t.T.astype(bf16))

        @pl.when(gi < n_own)
        def _():
            for j in range(pairs):
                o_nat[gi * pairs + j] = outs[j]
            output_copy(gi).start()

        @pl.when(gi >= n_own)
        def _():
            for j in range(pairs):
                o_help[gi - n_own, j] = outs[j]
            help_copy(gi - n_own).start()

    def step(carry, new, own):
        (slot1, blk1, last1, gi1), (slot2, blk2, last2, gi2) = carry
        for u in range(GROUP):
            value_stage(u, slot2, blk2)
            exp_stage(u, slot1)
            if new is not None:
                score_stage(u, new[1], own)

        @pl.when(last2 == 1)
        def _():
            finish(slot2, gi2)

        return (new if new is not None else (SLOTS, 0, 0, 0)), (slot1, blk1, last1, gi1)

    def keys_and_values(slot, head0, blk):
        c = ckv[blk]
        at = pl.multiple_of(blk * rows, rows)
        for j in range(GROUP // 4):
            wk = wuk[pl.ds(pl.multiple_of((head0 + 4 * j) * nope, 4 * nope), 4 * nope), :]
            kk = lax.dot_general(c, wk, NT, preferred_element_type=f32).astype(bf16)
            kn[2 * j, pl.ds(at, rows), :] = kk[:, :128]
            kn[2 * j + 1, pl.ds(at, rows), :] = kk[:, 128:]
            wv = wuv[pl.ds(pl.multiple_of((head0 + 4 * j) * vdim, 4 * vdim), 4 * vdim), :]
            vv = lax.dot_general(wv, c, NT, preferred_element_type=f32).astype(bf16)
            for i in range(4):
                vt[slot * GROUP + 4 * j + i, :vdim, pl.ds(at, rows)] = vv[i * vdim:(i + 1) * vdim, :]

    def queries(src, head0):
        ct, st = trig[src, :hr], trig[src, hr:]
        for j in range(GROUP // 4):
            w = wuq[pl.ds(pl.multiple_of((head0 + 4 * j) * qk, 4 * qk), 4 * qk), :]
            q = lax.dot_general(w, qlat[src], NT, preferred_element_type=f32)
            for i in range(4):
                u = 4 * j + i
                qh = q[i * qk:(i + 1) * qk]
                lo = (u % 2) * nope
                qaug[u, lo:lo + nope, :] = qh[:nope].astype(bf16)
                r1, r2 = qh[nope:nope + hr], qh[nope + hr:]
                qaug[u, 2 * nope:2 * nope + rot, :] = jnp.concatenate([r1 * ct - r2 * st, r2 * ct + r1 * st], axis=0).astype(bf16)

    def group(gi, carry):
        helping = (gi >= n_own).astype(jnp.int32)
        target = jnp.where(gi >= n_own, partner, me)
        head0 = jnp.where(gi >= n_own, ngroup - helped + gi - n_own, gi) * GROUP
        slot = lax.rem(gi, SLOTS)

        @pl.when(gi == n_own)
        def _():
            for c in query_copies(me):
                c.wait_recv()
            received(2)

            @pl.when(me == 0)
            def _():
                received(1)
                received(3)

        queries(helping, head0)
        keys_and_values(slot, head0, target)
        for u in range(GROUP):
            m_s[slot * GROUP + u] = jnp.full((1, rows), -jnp.inf, f32)
            acc[slot * GROUP + u] = jnp.zeros(acc.shape[1:], f32)
        carry = step(carry, (slot, target, (target == 0).astype(jnp.int32), gi), True)

        def previous(j, carry):
            blk = lax.rem(j + target - 1, target)

            @pl.when(gi == 0)
            def _():
                received(blk)

            keys_and_values(slot, head0, blk)
            return step(carry, (slot, blk, (j == target - 1).astype(jnp.int32), gi), False)

        carry = lax.fori_loop(0, target, previous, carry)

        @pl.when((gi == 0) & (me == 2))
        def _():
            start(query_copies(1))
            start(latent_copies(me, 1))

        return carry

    idle = (jnp.int32(SLOTS), jnp.int32(0), jnp.int32(0), jnp.int32(0))
    carry = lax.fori_loop(0, n_all, group, (idle, idle))
    carry = step(carry, None, False)
    step(carry, None, False)

    @pl.when(me == 0)
    def _():
        for t in (1, 3, 2):
            for c in latent_copies(me, t):
                c.wait_send()

    @pl.when(me == 1)
    def _():
        for t in (0, 2, 3):
            for c in latent_copies(me, t):
                c.wait_send()

    @pl.when(me == 2)
    def _():
        for t in (3, 0, 1):
            for c in latent_copies(me, t):
                c.wait_send()
        for c in query_copies(1):
            c.wait_send()

    @pl.when(me == 3)
    def _():
        for c in latent_copies(me, 0) + query_copies(0):
            c.wait_send()

    for k in range(max(HELPED)):
        @pl.when(k < helped)
        def _():
            help_copy(k).wait_send()

        @pl.when(k < given)
        def _():
            grp = n_own + k
            remote(o_help.at[k], o_nat.at[pl.ds(grp * pairs, pairs)], o_send.at[k], o_recv.at[k], me).wait_recv()
            output_copy(grp).start()

    for grp in range(ngroup):
        output_copy(grp).wait()


def layer(trig, gq, gkv, x, wdkv, wdq, wuq, wuk, wuv, scale2, heads, groups):
    rows, dim = x.shape
    rank = gkv.shape[0]
    rot = wdkv.shape[0] - rank
    qrank = wdq.shape[1]
    nope = wuk.shape[0] // heads
    vdim = wuv.shape[0] // heads
    seq = rows * groups
    vm = pl.BlockSpec(memory_space=pltpu.VMEM)
    anym = pl.BlockSpec(memory_space=pl.ANY)
    f32 = jnp.float32
    bf16 = jnp.bfloat16
    dma = pltpu.SemaphoreType.DMA
    nhelp = max(HELPED)
    return pl.pallas_call(
        functools.partial(layer_kernel, scale2=scale2, rows=rows, nope=nope, rot=rot, vdim=vdim, heads=heads, groups=groups),
        out_shape=(jax.ShapeDtypeStruct((heads // 2, rows, 2 * vdim), bf16),
                   jax.ShapeDtypeStruct((rows, rank), bf16),
                   jax.ShapeDtypeStruct((rot, rows), bf16)),
        in_specs=[vm, vm, vm] + [anym] * 6,
        out_specs=(anym, vm, vm),
        scratch_shapes=[
            pltpu.VMEM(x.shape, bf16),
            pltpu.VMEM(wdkv.shape, bf16),
            pltpu.VMEM(wdq.shape, bf16),
            pltpu.VMEM(wuq.shape, bf16),
            pltpu.VMEM(wuk.shape, bf16),
            pltpu.VMEM(wuv.shape, bf16),
            pltpu.VMEM((2, rows, qrank), bf16),
            pltpu.VMEM((2, rot, rows), f32),
            pltpu.VMEM((groups, rows, rank), bf16),
            pltpu.VMEM((groups, rot, rows), bf16),
            pltpu.VMEM((groups, rows, 128), bf16),
            pltpu.VMEM((GROUP, 256, rows), bf16),
            pltpu.VMEM((GROUP // 2, seq, 128), bf16),
            pltpu.VMEM(((SLOTS + 1) * GROUP, vdim + 16, seq), bf16),
            pltpu.VMEM((GROUP, rows, rows), f32),
            pltpu.VMEM((GROUP, 1, rows), f32),
            pltpu.VMEM((GROUP, rows, rows), bf16),
            pltpu.VMEM((GROUP, 1, rows), f32),
            pltpu.VMEM(((SLOTS + 1) * GROUP, 1, rows), f32),
            pltpu.VMEM(((SLOTS + 1) * GROUP, vdim + 16, rows), f32),
            pltpu.VMEM((heads // 2, rows, 2 * vdim), bf16),
            pltpu.VMEM((nhelp, GROUP // 2, rows, 2 * vdim), bf16),
            dma((6,)),
            dma((groups,)), dma((groups,)), dma((groups,)), dma((groups,)),
            dma, dma, dma, dma,
            dma((nhelp,)), dma((nhelp,)),
            dma((heads // GROUP,)),
        ],
        compiler_params=pltpu.CompilerParams(vmem_limit_bytes=62 * 1024 * 1024, collective_id=0, has_side_effects=True),
        cost_estimate=pl.CostEstimate(flops=40_000_000_000, bytes_accessed=40_000_000, transcendentals=30_000_000),
    )(trig, gq, gkv, x, wdkv, wdq, wuq, wuk, wuv)


def project_kernel(o_ref, w_ref, out_ref):
    o_all = jnp.concatenate([o_ref[j] for j in range(o_ref.shape[0])], axis=1)
    out_ref[...] = jnp.dot(o_all, w_ref[...], preferred_element_type=jnp.float32).astype(out_ref.dtype)


def project(o, w):
    npair, rows, width = o.shape
    dim = w.shape[1]
    tile = 512
    return pl.pallas_call(
        project_kernel,
        grid=(dim // tile,),
        in_specs=[pl.BlockSpec((npair, rows, width), lambda i: (0, 0, 0)), pl.BlockSpec((w.shape[0], tile), lambda i: (0, i))],
        out_specs=pl.BlockSpec((rows, tile), lambda i: (0, i)),
        out_shape=jax.ShapeDtypeStruct((rows, dim), jnp.bfloat16),
        compiler_params=pltpu.CompilerParams(vmem_limit_bytes=24 * 1024 * 1024),
        cost_estimate=pl.CostEstimate(flops=2 * rows * dim * w.shape[0], bytes_accessed=2 * w.size, transcendentals=0),
    )(o, w)


def solution(mesh):
    groups = mesh.shape['sp']
    tok_spec = P(('dp', 'sp'))
    rows_spec = P(('dp', 'sp'), None)
    replicated = P()

    def local_step(tok_in, tok_pos, w_dq, g_q, w_uq, w_dkv, g_kv, w_uk, w_uv, w_o):
        heads, qk_dim = w_uq.shape[1:]
        kv_rank = g_kv.shape[0]
        rot_dim = w_dkv.shape[1] - kv_rank
        v_dim = w_uv.shape[2]
        attn_scale = (0.1 * math.log(YARN_FACTOR) + 1.0) ** 2 / math.sqrt(qk_dim)
        angles = tok_pos.astype(jnp.float32)[None, :] * rope_freqs(rot_dim)[:, None]
        trig = jnp.concatenate([jnp.cos(angles), jnp.sin(angles)], axis=0)

        def flat(w):
            return jnp.transpose(w, (1, 2, 0)).reshape(-1, w.shape[0])

        o, cache_kv, cache_pe = layer(trig, g_q[None, :], g_kv[:, None], tok_in, w_dkv.T, w_dq, flat(w_uq), flat(w_uk), flat(w_uv),
                                      attn_scale * math.log2(math.e), heads, groups)
        attn_out = project(o, w_o.reshape(heads * v_dim, -1))
        return attn_out, cache_kv, cache_pe.T

    return jax.shard_map(local_step, mesh=mesh, in_specs=(rows_spec, tok_spec, replicated, replicated, replicated, replicated, replicated, replicated, replicated, replicated), out_specs=(rows_spec, rows_spec, rows_spec), check_vma=False)
```

time: 386 us -> 87.7 us (0.23)
  matrix products: 174 us -> 0 us
  waiting for transfers between devices: 117 us -> 0 us
  Pallas kernels: 0 us -> 72.9 us
  local copies, waits for them, and re-layouts: 53 us -> 10.5 us
  starting transfers between devices: 23.9 us -> 0 us
  other arithmetic: 10.3 us -> 2.17 us
    all_to_all x4 -> x0, waiting for transfers between devices: 117 us -> none  [the longest x1 38.9 us: local_step(): q_heads = lax.all_to_all(q_all, 'sp', 1, 0, tiled=True)]
    dot_general x7 -> x0, matrix products: 85.1 us -> none  [the longest x4 67 us: block_attention(): jnp.einsum('hqk,khv->qhv', attn_prob, v_heads, preferred_element_type=jnp...]
    sub x4 -> x0, matrix products: 81.7 us -> none  [block_attention(): attn_prob = jax.nn.softmax(logits, axis=-1).astype(jnp.bfloat16)]
    pallas_call x0 -> x2, Pallas kernels: none -> 72.9 us  [the longest x1 63.6 us: layer(): pl.pallas_call(functools.partial(layer_kernel, scale2=scale2, rows=rows,...]
    all_to_all x4 -> x0, starting transfers between devices: 23.9 us -> none  [the longest x1 7.15 us: local_step(): q_heads = lax.all_to_all(q_all, 'sp', 1, 0, tiled=True)]
    all_to_all x5 -> x0, local copies, waits for them, and re-layouts: 23.1 us -> none  [the longest x2 10.3 us: local_step(): o_local = lax.all_to_all(o_heads, 'sp', 0, 1, tiled=True)]
    reshape x1 -> x0, local copies, waits for them, and re-layouts: 10.2 us -> none  [local_step(): lax.map(block_attention, jnp.arange(groups))]
    unnamed x25 -> x10, local copies, waits for them, and re-layouts: 16.7 us -> 7.78 us
  transfers between devices with their start and end apart: 4 -> 0, of which waited for: 4 -> 0; matrix products, arithmetic and copies ran while one was open for 7% -> 0% of each run, Pallas kernels for 0% -> 0%
where the time goes in v3:
time: 87.7 us; the launch traced here: 86.2 us
  Pallas kernels  72.9 us (83%)
  local copies, waits for them, and re-layouts  10.5 us (12%)
  other arithmetic  2.17 us (2%)
    pallas_call x1, Pallas kernels, layer(): pl.pallas_call(functools.partial(layer_kernel, scale2=scale2, rows=rows,...  63.6 us
    pallas_call x1, Pallas kernels, project(): pl.pallas_call(project_kernel, grid=(dim // tile,), in_specs=[pl.BlockSpe...  9.29 us
    unnamed x10, local copies, waits for them, and re-layouts  7.78 us

profile of v3, /device:TPU:3, one launch (start us, length us, event | category | flops | bytes accessed | tf_op | source)
XLA Modules:
  0.0 86.2 jit_solution(2709387204453292554)
XLA Ops:
  0.6 0.7 convert_element_type.3
  1.3 1.3 %broadcast_in_dim.8.gq_ref = f32[1,768]{1,0:T(1,128)} reshape(f32[768]{0:T(1024)} %param.14) | data formatting | bytes 6144 | tf_op jit(solution)/shard_map/broadcast_in_dim | solution.py:425
  2.6 0.9 multiply_cosine_fusion
  3.4 0.6 pad_maximum_fusion.trig_in
  4.1 1.5 %copy.14.gkv_ref = f32[256,1]{1,0:T(8,128)} copy(f32[256,1]{0,1:T(1,128)} %bitcast.15) | data formatting | bytes 2048 | tf_op jit(solution)/shard_map/broadcast_in_dim | solution.py:425
  5.5 63.6 %shard_map.130 = (bf16[20,512,128]{2,1,0:T(8,128)(2,1)}, bf16[512,256]{1,0:T(8,128)(2,1)}, bf16[32,512]{1,0:T(8,128)(2,1)}) custom-call(f32[32,512]{1,0:T(8,128)} %pad_maximum_fusion.trig_in, f32[1,768]{1,0:T(1,128)} %broadcast_in_dim.8.gq_ref, f32[256,1]{1,0:T(8,128)} %copy.14.gkv_ref, bf16[512,2560]{1,0:T(8,128)(2,1)} %x_hbm.1, ...), custom_call_target="tpu_custom_call" | custom-call | flops 40000000000 | bytes 40000000 | tf_op jit(solution)/shard_map/pallas_call | solution.py:346
  69.1 0.0 copy-start
  69.1 4.7 %copy-done = bf16[40,64,2560]{2,1,0:T(8,128)(2,1)S(1)} copy-done((bf16[40,64,2560]{2,1,0:T(8,128)(2,1)S(1)}, bf16[40,64,2560]{2,1,0:T(8,128)(2,1)}, u32[]{:S(2)}) %copy-start) | copy-done | bytes 13107224
  73.9 0.0 copy-start.1
  73.9 1.7 %copy-done.1 = bf16[20,512,128]{2,1,0:T(8,128)(2,1)S(1)} copy-done((bf16[20,512,128]{2,1,0:T(8,128)(2,1)S(1)}, bf16[20,512,128]{2,1,0:T(8,128)(2,1)}, u32[]{:S(2)}) %copy-start.1) | copy-done | bytes 2621464
  75.6 0.0 copy-start.2
  75.6 0.0 copy-start.3
  75.6 9.3 %shard_map.131 = bf16[512,2560]{1,0:T(8,128)(2,1)} custom-call(bf16[20,512,128]{2,1,0:T(8,128)(2,1)S(1)} %copy-done.1, bf16[2560,2560]{1,0:T(8,128)(2,1)S(1)} %bitcast.13), custom_call_target="tpu_custom_call" | custom-call | flops 6710886400 | bytes 13107200 | tf_op jit(solution)/shard_map/pallas_call | solution.py:396
  84.9 0.0 copy-done.2
  84.9 0.7 copy.17
  85.6 0.0 copy-done.3
  85.6 0.6 copy.18
Async XLA Ops:
  69.1 4.7 %copy-start = (bf16[40,64,2560]{2,1,0:T(8,128)(2,1)S(1)}, bf16[40,64,2560]{2,1,0:T(8,128)(2,1)}, u32[]{:S(2)}) copy-start(bf16[40,64,2560]{2,1,0:T(8,128)(2,1)} %param.20) | copy-start | bytes 39321604
  73.9 1.7 %copy-start.1 = (bf16[20,512,128]{2,1,0:T(8,128)(2,1)S(1)}, bf16[20,512,128]{2,1,0:T(8,128)(2,1)}, u32[]{:S(2)}) copy-start(bf16[20,512,128]{2,1,0:T(8,128)(2,1)} %get-tuple-element.6.o_ref) | copy-start | bytes 7864324
  75.6 9.3 %copy-start.2 = (bf16[512,256]{1,0:T(8,128)(2,1)S(1)}, bf16[512,256]{1,0:T(8,128)(2,1)}, u32[]{:S(2)}) copy-start(bf16[512,256]{1,0:T(8,128)(2,1)} %get-tuple-element.15) | copy-start | bytes 786436
  75.6 10.0 %copy-start.3 = (bf16[32,512]{1,0:T(8,128)(2,1)S(1)}, bf16[32,512]{1,0:T(8,128)(2,1)}, u32[]{:S(2)}) copy-start(bf16[32,512]{1,0:T(8,128)(2,1)} %get-tuple-element.8) | copy-start | bytes 98308

commit v4 on v3

--- a/solution.py
+++ b/solution.py
@@ -26,7 +26,7 @@
         base_freq = ROPE_THETA ** (-2.0 * freq_idx / rot_dim)
         ramp_val = min(max((freq_idx - low_idx) / spread, 0.0), 1.0)
         freq_list.append(base_freq / YARN_FACTOR * ramp_val + base_freq * (1.0 - ramp_val))
-    return jnp.asarray(freq_list, dtype=jnp.float32)
+    return freq_list
 
 
 GROUP = 8
@@ -34,11 +34,11 @@
 HELPED = (2, 1)
 
 
-def layer_kernel(trig_in, gq_ref, gkv_ref, x_hbm, wdkv_hbm, wdq_hbm, wuq_hbm, wuk_hbm, wuv_hbm,
+def layer_kernel(pos_ref, gq_ref, gkv_ref, x_hbm, wdkv_hbm, wdq_hbm, wuq_hbm, wuk_hbm, wuv_hbm,
                  o_hbm, ckv_out, cpe_out,
                  x, wdkv, wdq, wuq, wuk, wuv, qlat, trig, ckv, pet, pen, qaug, kn, vt,
                  s_buf, c_buf, p_buf, al_buf, m_s, acc, o_nat, o_help,
-                 load_sem, c_send, c_recv, pe_send, pe_recv, q_send, q_recv, t_send, t_recv, o_send, o_recv, out_sem,
+                 load_sem, c_send, c_recv, pe_send, pe_recv, f_send, q_send, q_recv, t_send, t_recv, o_send, o_recv, out_sem,
                  *, scale2, rows, nope, rot, vdim, heads, groups):
     f32 = jnp.float32
     bf16 = jnp.bfloat16
@@ -71,6 +71,11 @@
         return (remote(ckv.at[origin], ckv.at[origin], c_send.at[to], c_recv.at[origin], to),
                 remote(pet.at[origin], pet.at[origin], pe_send.at[to], pe_recv.at[origin], to))
 
+    def forward_copies(origin):
+        to = 5 - me
+        return (remote(ckv.at[origin], ckv.at[origin], f_send.at[0], c_recv.at[origin], to),
+                remote(pet.at[origin], pet.at[origin], f_send.at[1], pe_recv.at[origin], to))
+
     def query_copies(to):
         return (remote(qlat.at[0], qlat.at[1], q_send, q_recv, to),
                 remote(trig.at[0], trig.at[1], t_send, t_recv, to))
@@ -88,37 +93,43 @@
         wide = jnp.concatenate([pet[origin].astype(f32), jnp.zeros((128 - rot, rows), f32)], axis=0)
         pen[origin] = wide.T.astype(bf16)
 
-    trig[0] = trig_in[...]
     hr = rot // 2
+    freq_i = lax.broadcasted_iota(jnp.int32, (hr, rows), 0)
+    freq = jnp.zeros((hr, rows), f32)
+    for i, f in enumerate(rope_freqs(rot)):
+        freq = jnp.where(freq_i == i, f, freq)
+    angle = pos_ref[...].astype(f32).reshape(1, rows) * freq
+    cos_t, sin_t = jnp.cos(angle), jnp.sin(angle)
+    trig[0, :hr] = cos_t
+    trig[0, hr:] = sin_t
     loads[0].wait()
     loads[1].wait()
     kvt = lax.dot_general(wdkv[...], x[...], NT, preferred_element_type=f32)
     rank = ckv.shape[2]
     a = kvt[:rank]
-    norm = a * lax.rsqrt(jnp.sum(a * a, axis=0, keepdims=True) / rank + NORM_EPS) * gkv_ref[...]
-    c_own = norm.T.astype(bf16)
+    norm = a * lax.rsqrt(jnp.sum(a * a, axis=0, keepdims=True) / rank + NORM_EPS)
+    c_own = (norm.T * gkv_ref[...].reshape(1, rank)).astype(bf16)
     ckv[me] = c_own
     ckv_out[...] = c_own
     z1, z2 = kvt[rank:rank + hr], kvt[rank + hr:]
-    cos_t, sin_t = trig_in[:hr], trig_in[hr:]
     pe_own = jnp.concatenate([z1 * cos_t - z2 * sin_t, z2 * cos_t + z1 * sin_t], axis=0).astype(bf16)
     pet[me] = pe_own
     cpe_out[...] = pe_own
     loads[2].wait()
-    ql = lax.dot_general(x[...], wdq[...], NN, preferred_element_type=f32)
-    qrank = ql.shape[1]
-    ql = ql * lax.rsqrt(jnp.sum(ql * ql, axis=1, keepdims=True) / qrank + NORM_EPS) * gq_ref[...]
-    qlat[0] = ql.astype(bf16)
+    tile = 256
+    qrank = wdq.shape[1]
+    first = lax.dot_general(x[...], wdq[:, :tile], NN, preferred_element_type=f32)
+    s_buf[0, :, :tile] = first
     pl.semaphore_wait(barrier, groups - 1)
 
     @pl.when(me == 0)
     def _():
-        for t in (1, 3, 2):
+        for t in (1, 3):
             start(latent_copies(me, t))
 
     @pl.when(me == 1)
     def _():
-        for t in (0, 2, 3):
+        for t in (2, 0):
             start(latent_copies(me, t))
 
     @pl.when(me == 2)
@@ -126,6 +137,9 @@
         for t in (3, 0):
             start(latent_copies(me, t))
 
+    rest = lax.dot_general(x[...], wdq[:, tile:], NN, preferred_element_type=f32)
+    ql = jnp.concatenate([s_buf[0, :, :tile], rest], axis=1)
+    qlat[0] = (ql * lax.rsqrt(jnp.sum(ql * ql, axis=1, keepdims=True) / qrank + NORM_EPS) * gq_ref[...].reshape(1, qrank)).astype(bf16)
     unpack_rope(me)
     qaug[...] = jnp.zeros_like(qaug)
     vt[:, vdim:, :] = jnp.ones((vt.shape[0], vt.shape[1] - vdim, vt.shape[2]), vt.dtype)
@@ -145,18 +159,29 @@
     def cols(i):
         return slice(i * half, (i + 1) * half)
 
-    def score_stage(u, blk, own):
+    def score_stage(u, blk, own, gi):
         tops = [None, None]
-        for k, i in (OWN if own else FULL):
-            lhs = jnp.concatenate([kn[u // 2, pl.ds(pl.multiple_of(blk * rows + k * half, half), half), :], pen[blk, cols(k), :]], axis=1)
-            s = lax.dot_general(lhs, qaug[u, :, cols(i)], NN, preferred_element_type=f32)
-            if own and k == i:
-                s = jnp.where(row_i <= col_i, s, -jnp.inf)
+
+        def place(s, k, i):
             s_buf[u, cols(k), cols(i)] = s
             top = jnp.max(s, axis=0, keepdims=True)
             tops[i] = top if tops[i] is None else jnp.maximum(tops[i], top)
+
+        def dot(k0, k1, i0, i1):
+            lhs = jnp.concatenate([kn[u // 2, pl.ds(pl.multiple_of(blk * rows + k0 * half, half), (k1 - k0) * half), :],
+                                   pen[blk, k0 * half:k1 * half, :]], axis=1)
+            return lax.dot_general(lhs, qaug[lax.rem(gi, 2), u, :, i0 * half:i1 * half], NN, preferred_element_type=f32)
+
         if own:
+            s = dot(0, 1, 0, 2)
+            place(jnp.where(row_i <= col_i, s[:, :half], -jnp.inf), 0, 0)
+            place(s[:, half:], 0, 1)
+            place(jnp.where(row_i <= col_i, dot(1, 2, 1, 2), -jnp.inf), 1, 1)
             s_buf[u, cols(1), cols(0)] = jnp.full((half, half), -jnp.inf, f32)
+        else:
+            s = dot(0, 2, 0, 2)
+            for k, i in FULL:
+                place(s[cols(k), cols(i)], k, i)
         for i in range(2):
             c_buf[u, :, cols(i)] = tops[i]
 
@@ -171,7 +196,7 @@
 
     def value_stage(u, slot, blk):
         h = slot * GROUP + u
-        v = vt[h, :, pl.ds(pl.multiple_of(blk * rows, rows), rows)]
+        v = vt[jnp.minimum(slot, SLOTS - 1) * GROUP + u, :, pl.ds(pl.multiple_of(blk * rows, rows), rows)]
         for i in range(2):
             t = lax.dot_general(v, p_buf[u, :, cols(i)], NN, preferred_element_type=f32)
             acc[h, :, cols(i)] = t + acc[h, :, cols(i)] * al_buf[u, :, cols(i)]
@@ -188,6 +213,8 @@
         for j in range(pairs):
             t = jnp.concatenate([acc[slot * GROUP + h, :vdim, :] / acc[slot * GROUP + h, vdim:vdim + 1, :] for h in (2 * j, 2 * j + 1)], axis=0)
             outs.append(t.T.astype(bf16))
+        for h in range(GROUP):
+            acc[slot * GROUP + h] = jnp.zeros(acc.shape[1:], f32)
 
         @pl.when(gi < n_own)
         def _():
@@ -201,13 +228,15 @@
                 o_help[gi - n_own, j] = outs[j]
             help_copy(gi - n_own).start()
 
-    def step(carry, new, own):
+    def step(carry, new, own, after=None):
         (slot1, blk1, last1, gi1), (slot2, blk2, last2, gi2) = carry
         for u in range(GROUP):
             value_stage(u, slot2, blk2)
             exp_stage(u, slot1)
             if new is not None:
-                score_stage(u, new[1], own)
+                score_stage(u, new[1], own, new[3])
+        if after is not None:
+            after()
 
         @pl.when(last2 == 1)
         def _():
@@ -228,7 +257,7 @@
             for i in range(4):
                 vt[slot * GROUP + 4 * j + i, :vdim, pl.ds(at, rows)] = vv[i * vdim:(i + 1) * vdim, :]
 
-    def queries(src, head0):
+    def queries(buf, src, head0):
         ct, st = trig[src, :hr], trig[src, hr:]
         for j in range(GROUP // 4):
             w = wuq[pl.ds(pl.multiple_of((head0 + 4 * j) * qk, 4 * qk), 4 * qk), :]
@@ -237,17 +266,30 @@
                 u = 4 * j + i
                 qh = q[i * qk:(i + 1) * qk]
                 lo = (u % 2) * nope
-                qaug[u, lo:lo + nope, :] = qh[:nope].astype(bf16)
+                qaug[buf, u, lo:lo + nope, :] = qh[:nope].astype(bf16)
                 r1, r2 = qh[nope:nope + hr], qh[nope + hr:]
-                qaug[u, 2 * nope:2 * nope + rot, :] = jnp.concatenate([r1 * ct - r2 * st, r2 * ct + r1 * st], axis=0).astype(bf16)
+                qaug[buf, u, 2 * nope:2 * nope + rot, :] = jnp.concatenate([r1 * ct - r2 * st, r2 * ct + r1 * st], axis=0).astype(bf16)
+
+    def place_of(gi):
+        helping = gi >= n_own
+        target = jnp.where(helping, partner, me)
+        head0 = jnp.where(helping, ngroup - helped + gi - n_own, gi) * GROUP
+        return helping.astype(jnp.int32), target, head0, lax.rem(gi, SLOTS)
+
+    def clear(slot):
+        for u in range(GROUP):
+            m_s[slot * GROUP + u] = jnp.full((1, rows), -jnp.inf, f32)
+
+    def earlier(target, j):
+        return lax.rem(j + target - 1, jnp.maximum(target, 1))
 
     def group(gi, carry):
-        helping = (gi >= n_own).astype(jnp.int32)
-        target = jnp.where(gi >= n_own, partner, me)
-        head0 = jnp.where(gi >= n_own, ngroup - helped + gi - n_own, gi) * GROUP
-        slot = lax.rem(gi, SLOTS)
-
-        @pl.when(gi == n_own)
+        _, target, head0, slot = place_of(gi)
+        gn = jnp.minimum(gi + 1, n_all - 1)
+        helping_n, target_n, head_n, _ = place_of(gn)
+        slot_n = lax.rem(gi + 1, SLOTS)
+
+        @pl.when((gi == n_own - 1) & (helped > 0))
         def _():
             for c in query_copies(me):
                 c.wait_recv()
@@ -258,22 +300,33 @@
                 received(1)
                 received(3)
 
-        queries(helping, head0)
-        keys_and_values(slot, head0, target)
-        for u in range(GROUP):
-            m_s[slot * GROUP + u] = jnp.full((1, rows), -jnp.inf, f32)
-            acc[slot * GROUP + u] = jnp.zeros(acc.shape[1:], f32)
-        carry = step(carry, (slot, target, (target == 0).astype(jnp.int32), gi), True)
+        def arrived(j):
+            @pl.when((gi == 0) & (j < target))
+            def _():
+                blk = earlier(target, j)
+                received(blk)
+
+                @pl.when((me >= 2) & (blk == 3 - me))
+                def _():
+                    start(forward_copies(blk))
+
+        def next_keys(j):
+            more = j < target
+            keys_and_values(jnp.where(more, slot, slot_n), jnp.where(more, head0, head_n),
+                            jnp.where(more, earlier(target, j), target_n))
+
+        def after_own():
+            queries(lax.rem(gi + 1, 2), helping_n, head_n)
+            next_keys(0)
+            clear(slot_n)
+
+        arrived(0)
+        carry = step(carry, (slot, target, (target == 0).astype(jnp.int32), gi), True, after_own)
 
         def previous(j, carry):
-            blk = lax.rem(j + target - 1, target)
-
-            @pl.when(gi == 0)
-            def _():
-                received(blk)
-
-            keys_and_values(slot, head0, blk)
-            return step(carry, (slot, blk, (j == target - 1).astype(jnp.int32), gi), False)
+            arrived(j + 1)
+            return step(carry, (slot, earlier(target, j), (j == target - 1).astype(jnp.int32), gi), False,
+                        lambda: next_keys(j + 1))
 
         carry = lax.fori_loop(0, target, previous, carry)
 
@@ -285,19 +338,23 @@
         return carry
 
     idle = (jnp.int32(SLOTS), jnp.int32(0), jnp.int32(0), jnp.int32(0))
+    acc[...] = jnp.zeros_like(acc)
+    queries(0, 0, 0)
+    keys_and_values(0, 0, me)
+    clear(0)
     carry = lax.fori_loop(0, n_all, group, (idle, idle))
     carry = step(carry, None, False)
     step(carry, None, False)
 
     @pl.when(me == 0)
     def _():
-        for t in (1, 3, 2):
+        for t in (1, 3):
             for c in latent_copies(me, t):
                 c.wait_send()
 
     @pl.when(me == 1)
     def _():
-        for t in (0, 2, 3):
+        for t in (2, 0):
             for c in latent_copies(me, t):
                 c.wait_send()
 
@@ -306,12 +363,12 @@
         for t in (3, 0, 1):
             for c in latent_copies(me, t):
                 c.wait_send()
-        for c in query_copies(1):
+        for c in forward_copies(1) + query_copies(1):
             c.wait_send()
 
     @pl.when(me == 3)
     def _():
-        for c in latent_copies(me, 0) + query_copies(0):
+        for c in latent_copies(me, 0) + forward_copies(0) + query_copies(0):
             c.wait_send()
 
     for k in range(max(HELPED)):
@@ -329,7 +386,7 @@
         output_copy(grp).wait()
 
 
-def layer(trig, gq, gkv, x, wdkv, wdq, wuq, wuk, wuv, scale2, heads, groups):
+def layer(pos, gq, gkv, x, wdkv, wdq, wuq, wuk, wuv, scale2, heads, groups):
     rows, dim = x.shape
     rank = gkv.shape[0]
     rot = wdkv.shape[0] - rank
@@ -362,9 +419,9 @@
             pltpu.VMEM((groups, rows, rank), bf16),
             pltpu.VMEM((groups, rot, rows), bf16),
             pltpu.VMEM((groups, rows, 128), bf16),
-            pltpu.VMEM((GROUP, 256, rows), bf16),
+            pltpu.VMEM((2, GROUP, 256, rows), bf16),
             pltpu.VMEM((GROUP // 2, seq, 128), bf16),
-            pltpu.VMEM(((SLOTS + 1) * GROUP, vdim + 16, seq), bf16),
+            pltpu.VMEM((SLOTS * GROUP, vdim + 16, seq), bf16),
             pltpu.VMEM((GROUP, rows, rows), f32),
             pltpu.VMEM((GROUP, 1, rows), f32),
             pltpu.VMEM((GROUP, rows, rows), bf16),
@@ -374,34 +431,43 @@
             pltpu.VMEM((heads // 2, rows, 2 * vdim), bf16),
             pltpu.VMEM((nhelp, GROUP // 2, rows, 2 * vdim), bf16),
             dma((6,)),
-            dma((groups,)), dma((groups,)), dma((groups,)), dma((groups,)),
+            dma((groups,)), dma((groups,)), dma((groups,)), dma((groups,)), dma((2,)),
             dma, dma, dma, dma,
             dma((nhelp,)), dma((nhelp,)),
             dma((heads // GROUP,)),
         ],
         compiler_params=pltpu.CompilerParams(vmem_limit_bytes=62 * 1024 * 1024, collective_id=0, has_side_effects=True),
         cost_estimate=pl.CostEstimate(flops=40_000_000_000, bytes_accessed=40_000_000, transcendentals=30_000_000),
-    )(trig, gq, gkv, x, wdkv, wdq, wuq, wuk, wuv)
-
-
-def project_kernel(o_ref, w_ref, out_ref):
+    )(pos, gq, gkv, x, wdkv, wdq, wuq, wuk, wuv)
+
+
+def project_kernel(o_ref, ckv_ref, cpe_ref, w_ref, out_ref, ckv_out, cpe_out):
+    @pl.when(pl.program_id(0) == 0)
+    def _():
+        ckv_out[...] = ckv_ref[...]
+        cpe_out[...] = cpe_ref[...]
+
     o_all = jnp.concatenate([o_ref[j] for j in range(o_ref.shape[0])], axis=1)
     out_ref[...] = jnp.dot(o_all, w_ref[...], preferred_element_type=jnp.float32).astype(out_ref.dtype)
 
 
-def project(o, w):
+def project(o, ckv, cpe, w):
     npair, rows, width = o.shape
     dim = w.shape[1]
-    tile = 512
+    tile = 256
+
+    def whole(a):
+        return pl.BlockSpec(a.shape, lambda i: (0,) * a.ndim)
+
     return pl.pallas_call(
         project_kernel,
         grid=(dim // tile,),
-        in_specs=[pl.BlockSpec((npair, rows, width), lambda i: (0, 0, 0)), pl.BlockSpec((w.shape[0], tile), lambda i: (0, i))],
-        out_specs=pl.BlockSpec((rows, tile), lambda i: (0, i)),
-        out_shape=jax.ShapeDtypeStruct((rows, dim), jnp.bfloat16),
-        compiler_params=pltpu.CompilerParams(vmem_limit_bytes=24 * 1024 * 1024),
+        in_specs=[whole(o), whole(ckv), whole(cpe), pl.BlockSpec((w.shape[0], tile), lambda i: (0, i))],
+        out_specs=(pl.BlockSpec((rows, tile), lambda i: (0, i)), whole(ckv), whole(cpe)),
+        out_shape=(jax.ShapeDtypeStruct((rows, dim), jnp.bfloat16), jax.ShapeDtypeStruct(ckv.shape, ckv.dtype), jax.ShapeDtypeStruct(cpe.shape, cpe.dtype)),
+        compiler_params=pltpu.CompilerParams(vmem_limit_bytes=62 * 1024 * 1024),
         cost_estimate=pl.CostEstimate(flops=2 * rows * dim * w.shape[0], bytes_accessed=2 * w.size, transcendentals=0),
-    )(o, w)
+    )(o, ckv, cpe, w)
 
 
 def solution(mesh):
@@ -416,15 +482,12 @@
         rot_dim = w_dkv.shape[1] - kv_rank
         v_dim = w_uv.shape[2]
         attn_scale = (0.1 * math.log(YARN_FACTOR) + 1.0) ** 2 / math.sqrt(qk_dim)
-        angles = tok_pos.astype(jnp.float32)[None, :] * rope_freqs(rot_dim)[:, None]
-        trig = jnp.concatenate([jnp.cos(angles), jnp.sin(angles)], axis=0)
-
         def flat(w):
             return jnp.transpose(w, (1, 2, 0)).reshape(-1, w.shape[0])
 
-        o, cache_kv, cache_pe = layer(trig, g_q[None, :], g_kv[:, None], tok_in, w_dkv.T, w_dq, flat(w_uq), flat(w_uk), flat(w_uv),
+        o, ckv, cpe = layer(tok_pos, g_q, g_kv, tok_in, w_dkv.T, w_dq, flat(w_uq), flat(w_uk), flat(w_uv),
                                       attn_scale * math.log2(math.e), heads, groups)
-        attn_out = project(o, w_o.reshape(heads * v_dim, -1))
+        attn_out, cache_kv, cache_pe = project(o, ckv, cpe, w_o.reshape(heads * v_dim, -1))
         return attn_out, cache_kv, cache_pe.T
 
     return jax.shard_map(local_step, mesh=mesh, in_specs=(rows_spec, tok_spec, replicated, replicated, replicated, replicated, replicated, replicated, replicated, replicated), out_specs=(rows_spec, rows_spec, rows_spec), check_vma=False)

time: 87.7 us -> 82.8 us (0.944); the launches traced: 86.2 us -> 82.4 us
  local copies, waits for them, and re-layouts: 10.5 us -> 0 us
  Pallas kernels: 72.9 us -> 81.8 us
  other arithmetic: 2.17 us -> 0 us
    unnamed x10 -> x0, local copies, waits for them, and re-layouts: 7.78 us -> none
    pallas_call x1, Pallas kernels: 9.29 us -> 14.1 us  [project(): pl.pallas_call(project_kernel, grid=(dim // tile,), in_specs=[whole(o), w...]
    pallas_call x1, Pallas kernels: 63.6 us -> 67.6 us  [layer(): pl.pallas_call(functools.partial(layer_kernel, scale2=scale2, rows=rows,...]
    broadcast_in_dim x2 -> x0, local copies, waits for them, and re-layouts: 2.74 us -> none  [the longest x1 1.47 us: local_step(): g_kv[:, None]]
where the time goes in v4:
time: 82.8 us; the launch traced here: 82.4 us
  Pallas kernels  81.8 us (99%)
    pallas_call x1, Pallas kernels, layer(): pl.pallas_call(functools.partial(layer_kernel, scale2=scale2, rows=rows,...  67.6 us
    pallas_call x1, Pallas kernels, project(): pl.pallas_call(project_kernel, grid=(dim // tile,), in_specs=[whole(o), w...  14.1 us

profile of v4, /device:TPU:3, one launch (start us, length us, event | category | flops | bytes accessed | tf_op | source)
XLA Modules:
  0.0 82.4 jit_solution(12643850143058816382)
XLA Ops:
  0.6 67.6 %shard_map.121 = (bf16[20,512,128]{2,1,0:T(8,128)(2,1)}, bf16[512,256]{1,0:T(8,128)(2,1)}, bf16[32,512]{1,0:T(8,128)(2,1)}) custom-call(s32[512]{0:T(512)} %pos_ref.1, f32[768]{0:T(1024)} %gq_ref.1, f32[256]{0:T(256)} %gkv_ref.1, bf16[512,2560]{1,0:T(8,128)(2,1)} %x_hbm.1, bf16[288,2560]{1,0:T(8,128)(2,1)} %bitcast.14, bf16[2560,768]{1,0:T(8,128)(2,1)} %wdq_hbm.1, ...), custom_call_target="tpu_custom_call" | custom-call | flops 40000000000 | bytes 40000000 | tf_op jit(solution)/shard_map/pallas_call | solution.py:403
  68.3 14.1 %shard_map.122 = (bf16[512,2560]{1,0:T(8,128)(2,1)}, bf16[512,256]{1,0:T(8,128)(2,1)}, bf16[32,512]{1,0:T(8,128)(2,1)}) custom-call(bf16[20,512,128]{2,1,0:T(8,128)(2,1)} %get-tuple-element.9.o_ref, bf16[512,256]{1,0:T(8,128)(2,1)} %get-tuple-element.10.ckv_ref, bf16[32,512]{1,0:T(8,128)(2,1)} %get-tuple-element.11.cpe_ref, bf16[2560,2560]{1,0:T(8,128)(2,1)} %bitcast.12), custom_call_target="tpu_custom_call" | custom-call | flops 6710886400 | bytes 13107200 | tf_op jit(solution)/shard_map/pallas_call | solution.py:462

commit v5 on v4

--- a/solution.py
+++ b/solution.py
@@ -31,7 +31,7 @@
 
 GROUP = 8
 SLOTS = 3
-HELPED = (2, 1)
+MOST_HELPED = 2
 
 
 def layer_kernel(pos_ref, gq_ref, gkv_ref, x_hbm, wdkv_hbm, wdq_hbm, wuq_hbm, wuk_hbm, wuv_hbm,
@@ -49,9 +49,9 @@
     pairs = GROUP // 2
     ngroup = heads // GROUP
     me = lax.axis_index('sp')
-    partner = groups - 1 - me
-    given = jnp.where(me == groups - 1, HELPED[0], jnp.where(me == groups - 2, HELPED[1], 0))
-    helped = jnp.where(me == 0, HELPED[0], jnp.where(me == 1, HELPED[1], 0))
+    given = jnp.where(me == 3, 2, jnp.where(me == 2, 1, 0))
+    helped = jnp.where(me == 0, 2, jnp.where(me == 3, 1, 0))
+    partner = jnp.where(me == 0, 3, 2)
     n_own = ngroup - given
     n_all = n_own + helped
 
@@ -134,8 +134,7 @@
 
     @pl.when(me == 2)
     def _():
-        for t in (3, 0):
-            start(latent_copies(me, t))
+        start(latent_copies(me, 3))
 
     rest = lax.dot_general(x[...], wdq[:, tile:], NN, preferred_element_type=f32)
     ql = jnp.concatenate([s_buf[0, :, :tile], rest], axis=1)
@@ -145,6 +144,10 @@
     vt[:, vdim:, :] = jnp.ones((vt.shape[0], vt.shape[1] - vdim, vt.shape[2]), vt.dtype)
     for c in loads[3:]:
         c.wait()
+
+    @pl.when(me == 2)
+    def _():
+        start(query_copies(3))
 
     @pl.when(me == 3)
     def _():
@@ -201,12 +204,18 @@
             t = lax.dot_general(v, p_buf[u, :, cols(i)], NN, preferred_element_type=f32)
             acc[h, :, cols(i)] = t + acc[h, :, cols(i)] * al_buf[u, :, cols(i)]
 
+    def place_of(gi):
+        helping = (gi >= n_own - 1) & (gi < n_own - 1 + helped)
+        target = jnp.where(helping, partner, me)
+        grp = jnp.where(helping, ngroup - helped + gi - n_own + 1, jnp.minimum(gi, n_own - 1))
+        return helping, target, grp, lax.rem(gi, SLOTS)
+
     def output_copy(grp):
         return pltpu.make_async_copy(o_nat.at[pl.ds(grp * pairs, pairs)], o_hbm.at[pl.ds(grp * pairs, pairs)], out_sem.at[grp])
 
-    def help_copy(k):
+    def help_copy(k, to):
         grp = ngroup - helped + k
-        return remote(o_help.at[k], o_nat.at[pl.ds(grp * pairs, pairs)], o_send.at[k], o_recv.at[k], partner)
+        return remote(o_help.at[k], o_nat.at[pl.ds(grp * pairs, pairs)], o_send.at[k], o_recv.at[grp], to)
 
     def finish(slot, gi):
         outs = []
@@ -216,17 +225,20 @@
         for h in range(GROUP):
             acc[slot * GROUP + h] = jnp.zeros(acc.shape[1:], f32)
 
-        @pl.when(gi < n_own)
+        helping, _, grp, _ = place_of(gi)
+
+        @pl.when(jnp.logical_not(helping))
         def _():
             for j in range(pairs):
-                o_nat[gi * pairs + j] = outs[j]
-            output_copy(gi).start()
-
-        @pl.when(gi >= n_own)
-        def _():
+                o_nat[grp * pairs + j] = outs[j]
+            output_copy(grp).start()
+
+        @pl.when(helping)
+        def _():
+            k = gi - n_own + 1
             for j in range(pairs):
-                o_help[gi - n_own, j] = outs[j]
-            help_copy(gi - n_own).start()
+                o_help[k, j] = outs[j]
+            help_copy(k, partner).start()
 
     def step(carry, new, own, after=None):
         (slot1, blk1, last1, gi1), (slot2, blk2, last2, gi2) = carry
@@ -270,12 +282,6 @@
                 r1, r2 = qh[nope:nope + hr], qh[nope + hr:]
                 qaug[buf, u, 2 * nope:2 * nope + rot, :] = jnp.concatenate([r1 * ct - r2 * st, r2 * ct + r1 * st], axis=0).astype(bf16)
 
-    def place_of(gi):
-        helping = gi >= n_own
-        target = jnp.where(helping, partner, me)
-        head0 = jnp.where(helping, ngroup - helped + gi - n_own, gi) * GROUP
-        return helping.astype(jnp.int32), target, head0, lax.rem(gi, SLOTS)
-
     def clear(slot):
         for u in range(GROUP):
             m_s[slot * GROUP + u] = jnp.full((1, rows), -jnp.inf, f32)
@@ -284,21 +290,25 @@
         return lax.rem(j + target - 1, jnp.maximum(target, 1))
 
     def group(gi, carry):
-        _, target, head0, slot = place_of(gi)
+        _, target, grp, slot = place_of(gi)
         gn = jnp.minimum(gi + 1, n_all - 1)
-        helping_n, target_n, head_n, _ = place_of(gn)
+        helping_n, target_n, grp_n, _ = place_of(gn)
         slot_n = lax.rem(gi + 1, SLOTS)
-
-        @pl.when((gi == n_own - 1) & (helped > 0))
+        head0, head_n = grp * GROUP, grp_n * GROUP
+
+        @pl.when((gi == n_own - 2) & (helped > 0))
         def _():
             for c in query_copies(me):
                 c.wait_recv()
+
+        @pl.when((gi == n_own - 2) & (me == 0))
+        def _():
+            received(3)
+
+        @pl.when((gi == n_own - 1) & (me == 0))
+        def _():
+            received(1)
             received(2)
-
-            @pl.when(me == 0)
-            def _():
-                received(1)
-                received(3)
 
         def arrived(j):
             @pl.when((gi == 0) & (j < target))
@@ -316,7 +326,7 @@
                             jnp.where(more, earlier(target, j), target_n))
 
         def after_own():
-            queries(lax.rem(gi + 1, 2), helping_n, head_n)
+            queries(lax.rem(gi + 1, 2), helping_n.astype(jnp.int32), head_n)
             next_keys(0)
             clear(slot_n)
 
@@ -328,12 +338,11 @@
             return step(carry, (slot, earlier(target, j), (j == target - 1).astype(jnp.int32), gi), False,
                         lambda: next_keys(j + 1))
 
+        @pl.when((gi == 0) & (me == 2))
+        def _():
+            start(latent_copies(me, 0))
+
         carry = lax.fori_loop(0, target, previous, carry)
-
-        @pl.when((gi == 0) & (me == 2))
-        def _():
-            start(query_copies(1))
-            start(latent_copies(me, 1))
 
         return carry
 
@@ -346,40 +355,35 @@
     carry = step(carry, None, False)
     step(carry, None, False)
 
+    def sent(copies):
+        for c in copies:
+            c.wait_send()
+
     @pl.when(me == 0)
     def _():
-        for t in (1, 3):
-            for c in latent_copies(me, t):
-                c.wait_send()
+        sent(latent_copies(me, 1) + latent_copies(me, 3))
 
     @pl.when(me == 1)
     def _():
-        for t in (2, 0):
-            for c in latent_copies(me, t):
-                c.wait_send()
+        sent(latent_copies(me, 2) + latent_copies(me, 0))
 
     @pl.when(me == 2)
     def _():
-        for t in (3, 0, 1):
-            for c in latent_copies(me, t):
-                c.wait_send()
-        for c in forward_copies(1) + query_copies(1):
-            c.wait_send()
+        sent(latent_copies(me, 3) + latent_copies(me, 0) + forward_copies(1) + query_copies(3))
 
     @pl.when(me == 3)
     def _():
-        for c in latent_copies(me, 0) + forward_copies(0) + query_copies(0):
-            c.wait_send()
-
-    for k in range(max(HELPED)):
+        sent(latent_copies(me, 0) + forward_copies(0) + query_copies(0))
+
+    for k in range(MOST_HELPED):
         @pl.when(k < helped)
         def _():
-            help_copy(k).wait_send()
+            help_copy(k, partner).wait_send()
 
         @pl.when(k < given)
         def _():
             grp = n_own + k
-            remote(o_help.at[k], o_nat.at[pl.ds(grp * pairs, pairs)], o_send.at[k], o_recv.at[k], me).wait_recv()
+            remote(o_help.at[k], o_nat.at[pl.ds(grp * pairs, pairs)], o_send.at[k], o_recv.at[grp], me).wait_recv()
             output_copy(grp).start()
 
     for grp in range(ngroup):
@@ -399,7 +403,7 @@
     f32 = jnp.float32
     bf16 = jnp.bfloat16
     dma = pltpu.SemaphoreType.DMA
-    nhelp = max(HELPED)
+    nhelp = MOST_HELPED
     return pl.pallas_call(
         functools.partial(layer_kernel, scale2=scale2, rows=rows, nope=nope, rot=rot, vdim=vdim, heads=heads, groups=groups),
         out_shape=(jax.ShapeDtypeStruct((heads // 2, rows, 2 * vdim), bf16),
@@ -433,7 +437,7 @@
             dma((6,)),
             dma((groups,)), dma((groups,)), dma((groups,)), dma((groups,)), dma((2,)),
             dma, dma, dma, dma,
-            dma((nhelp,)), dma((nhelp,)),
+            dma((nhelp,)), dma((heads // GROUP,)),
             dma((heads // GROUP,)),
         ],
         compiler_params=pltpu.CompilerParams(vmem_limit_bytes=62 * 1024 * 1024, collective_id=0, has_side_effects=True),
@@ -454,7 +458,7 @@
 def project(o, ckv, cpe, w):
     npair, rows, width = o.shape
     dim = w.shape[1]
-    tile = 256
+    tile = 512
 
     def whole(a):
         return pl.BlockSpec(a.shape, lambda i: (0,) * a.ndim)

time: 82.8 us -> 77.4 us (0.935)
  Pallas kernels: 81.8 us -> 76.5 us
    pallas_call x1, Pallas kernels: 67.6 us -> 64.6 us  [layer(): pl.pallas_call(functools.partial(layer_kernel, scale2=scale2, rows=rows,...]
    pallas_call x1, Pallas kernels: 14.1 us -> 11.9 us  [project(): pl.pallas_call(project_kernel, grid=(dim // tile,), in_specs=[whole(o), w...]
where the time goes in v5:
time: 77.4 us; the launch traced here: 77.1 us
  Pallas kernels  76.5 us (99%)
    pallas_call x1, Pallas kernels, layer(): pl.pallas_call(functools.partial(layer_kernel, scale2=scale2, rows=rows,...  64.6 us
    pallas_call x1, Pallas kernels, project(): pl.pallas_call(project_kernel, grid=(dim // tile,), in_specs=[whole(o), w...  11.9 us

profile of v5, /device:TPU:3, one launch (start us, length us, event | category | flops | bytes accessed | tf_op | source)
XLA Modules:
  0.0 77.1 jit_solution(9911864691697512606)
XLA Ops:
  0.6 64.6 %shard_map.121 = (bf16[20,512,128]{2,1,0:T(8,128)(2,1)}, bf16[512,256]{1,0:T(8,128)(2,1)}, bf16[32,512]{1,0:T(8,128)(2,1)}) custom-call(s32[512]{0:T(512)} %pos_ref.1, f32[768]{0:T(1024)} %gq_ref.1, f32[256]{0:T(256)} %gkv_ref.1, bf16[512,2560]{1,0:T(8,128)(2,1)} %x_hbm.1, bf16[288,2560]{1,0:T(8,128)(2,1)} %bitcast.14, bf16[2560,768]{1,0:T(8,128)(2,1)} %wdq_hbm.1, ...), custom_call_target="tpu_custom_call" | custom-call | flops 40000000000 | bytes 40000000 | tf_op jit(solution)/shard_map/pallas_call | solution.py:407
  65.2 11.9 %shard_map.122 = (bf16[512,2560]{1,0:T(8,128)(2,1)}, bf16[512,256]{1,0:T(8,128)(2,1)}, bf16[32,512]{1,0:T(8,128)(2,1)}) custom-call(bf16[20,512,128]{2,1,0:T(8,128)(2,1)} %get-tuple-element.9.o_ref, bf16[512,256]{1,0:T(8,128)(2,1)} %get-tuple-element.10.ckv_ref, bf16[32,512]{1,0:T(8,128)(2,1)} %get-tuple-element.11.cpe_ref, bf16[2560,2560]{1,0:T(8,128)(2,1)} %bitcast.12), custom_call_target="tpu_custom_call" | custom-call | flops 6710886400 | bytes 13107200 | tf_op jit(solution)/shard_map/pallas_call | solution.py:466

commit v6 on v5

--- a/solution.py
+++ b/solution.py
@@ -77,8 +77,18 @@
                 remote(pet.at[origin], pet.at[origin], f_send.at[1], pe_recv.at[origin], to))
 
     def query_copies(to):
-        return (remote(qlat.at[0], qlat.at[1], q_send, q_recv, to),
+        return (remote(qlat.at[0], qlat.at[1], q_send.at[0], q_recv.at[0], to),
                 remote(trig.at[0], trig.at[1], t_send, t_recv, to))
+
+    def query_halves():
+        top, low = pl.ds(0, half), pl.ds(half, half)
+        return (remote(qlat.at[0, low], qlat.at[1, low], q_send.at[1], q_recv.at[1], 2),
+                remote(trig.at[0], trig.at[1], t_send, t_recv, 0),
+                remote(qlat.at[0, top], qlat.at[1, top], q_send.at[0], q_recv.at[0], 0))
+
+    def query_relay():
+        low = pl.ds(half, half)
+        return remote(qlat.at[1, low], qlat.at[1, low], q_send.at[2], q_recv.at[2], 0)
 
     def start(copies):
         for c in copies:
@@ -151,7 +161,7 @@
 
     @pl.when(me == 3)
     def _():
-        start(query_copies(0))
+        start(query_halves())
         start(latent_copies(me, 0))
 
     FULL = ((0, 0), (1, 0), (0, 1), (1, 1))
@@ -213,9 +223,19 @@
     def output_copy(grp):
         return pltpu.make_async_copy(o_nat.at[pl.ds(grp * pairs, pairs)], o_hbm.at[pl.ds(grp * pairs, pairs)], out_sem.at[grp])
 
-    def help_copy(k, to):
+    def half_at(grp, part):
+        return o_nat.at[pl.ds(grp * pairs + part * (pairs // 2), pairs // 2)]
+
+    def help_half(k, part, to):
         grp = ngroup - helped + k
-        return remote(o_help.at[k], o_nat.at[pl.ds(grp * pairs, pairs)], o_send.at[k], o_recv.at[grp], to)
+        return remote(o_help.at[k, pl.ds(part * (pairs // 2), pairs // 2)], half_at(grp, part), o_send.at[k, part], o_recv.at[grp, part], to)
+
+    def help_detour():
+        spot = o_help.at[1, pl.ds(pairs // 2, pairs // 2)]
+        return remote(spot, spot, o_send.at[1, 1], o_recv.at[ngroup - 1, 1], 1)
+
+    def help_relay():
+        return remote(o_help.at[1, pl.ds(pairs // 2, pairs // 2)], half_at(ngroup - 1, 1), o_send.at[1, 1], o_recv.at[ngroup - 1, 1], 3)
 
     def finish(slot, gi):
         outs = []
@@ -238,7 +258,16 @@
             k = gi - n_own + 1
             for j in range(pairs):
                 o_help[k, j] = outs[j]
-            help_copy(k, partner).start()
+            help_half(k, 0, partner).start()
+            detour = (me == 0) & (k == 1)
+
+            @pl.when(detour)
+            def _():
+                help_detour().start()
+
+            @pl.when(jnp.logical_not(detour))
+            def _():
+                help_half(k, 1, partner).start()
 
     def step(carry, new, own, after=None):
         (slot1, blk1, last1, gi1), (slot2, blk2, last2, gi2) = carry
@@ -296,13 +325,15 @@
         slot_n = lax.rem(gi + 1, SLOTS)
         head0, head_n = grp * GROUP, grp_n * GROUP
 
-        @pl.when((gi == n_own - 2) & (helped > 0))
+        @pl.when((gi == n_own - 2) & (me == 3))
         def _():
             for c in query_copies(me):
                 c.wait_recv()
 
         @pl.when((gi == n_own - 2) & (me == 0))
         def _():
+            for c in query_halves()[1:] + (query_relay(),):
+                c.wait_recv()
             received(3)
 
         @pl.when((gi == n_own - 1) & (me == 0))
@@ -331,16 +362,19 @@
             clear(slot_n)
 
         arrived(0)
+
+        @pl.when((gi == 0) & (me == 2))
+        def _():
+            query_halves()[0].wait_recv()
+            query_relay().start()
+            start(latent_copies(me, 0))
+
         carry = step(carry, (slot, target, (target == 0).astype(jnp.int32), gi), True, after_own)
 
         def previous(j, carry):
             arrived(j + 1)
             return step(carry, (slot, earlier(target, j), (j == target - 1).astype(jnp.int32), gi), False,
                         lambda: next_keys(j + 1))
-
-        @pl.when((gi == 0) & (me == 2))
-        def _():
-            start(latent_copies(me, 0))
 
         carry = lax.fori_loop(0, target, previous, carry)
 
@@ -355,6 +389,12 @@
     carry = step(carry, None, False)
     step(carry, None, False)
 
+    @pl.when(me == 1)
+    def _():
+        help_detour().wait_recv()
+        help_relay().start()
+        help_relay().wait_send()
+
     def sent(copies):
         for c in copies:
             c.wait_send()
@@ -369,21 +409,23 @@
 
     @pl.when(me == 2)
     def _():
-        sent(latent_copies(me, 3) + latent_copies(me, 0) + forward_copies(1) + query_copies(3))
+        sent(latent_copies(me, 3) + latent_copies(me, 0) + forward_copies(1) + query_copies(3) + (query_relay(),))
 
     @pl.when(me == 3)
     def _():
-        sent(latent_copies(me, 0) + forward_copies(0) + query_copies(0))
+        sent(latent_copies(me, 0) + forward_copies(0) + query_halves())
 
     for k in range(MOST_HELPED):
         @pl.when(k < helped)
         def _():
-            help_copy(k, partner).wait_send()
+            for part in range(2):
+                help_half(k, part, partner).wait_send()
 
         @pl.when(k < given)
         def _():
             grp = n_own + k
-            remote(o_help.at[k], o_nat.at[pl.ds(grp * pairs, pairs)], o_send.at[k], o_recv.at[grp], me).wait_recv()
+            for part in range(2):
+                remote(half_at(grp, part), half_at(grp, part), o_send.at[k, part], o_recv.at[grp, part], me).wait_recv()
             output_copy(grp).start()
 
     for grp in range(ngroup):
@@ -436,8 +478,8 @@
             pltpu.VMEM((nhelp, GROUP // 2, rows, 2 * vdim), bf16),
             dma((6,)),
             dma((groups,)), dma((groups,)), dma((groups,)), dma((groups,)), dma((2,)),
-            dma, dma, dma, dma,
-            dma((nhelp,)), dma((heads // GROUP,)),
+            dma((3,)), dma((3,)), dma, dma,
+            dma((nhelp, 2)), dma((heads // GROUP, 2)),
             dma((heads // GROUP,)),
         ],
         compiler_params=pltpu.CompilerParams(vmem_limit_bytes=62 * 1024 * 1024, collective_id=0, has_side_effects=True),

time: 77.4 us -> 74.3 us (0.960)
  Pallas kernels: 76.5 us -> 73.4 us
    pallas_call x1, Pallas kernels: 64.6 us -> 61.5 us  [layer(): pl.pallas_call(functools.partial(layer_kernel, scale2=scale2, rows=rows,...]
where the time goes in v6:
time: 74.3 us; the launch traced here: 74 us
  Pallas kernels  73.4 us (99%)
    pallas_call x1, Pallas kernels, layer(): pl.pallas_call(functools.partial(layer_kernel, scale2=scale2, rows=rows,...  61.5 us
    pallas_call x1, Pallas kernels, project(): pl.pallas_call(project_kernel, grid=(dim // tile,), in_specs=[whole(o), w...  11.9 us

profile of v6, /device:TPU:3, one launch (start us, length us, event | category | flops | bytes accessed | tf_op | source)
XLA Modules:
  0.0 74.0 jit_solution(9831325274003508267)
XLA Ops:
  0.6 61.5 %shard_map.121 = (bf16[20,512,128]{2,1,0:T(8,128)(2,1)}, bf16[512,256]{1,0:T(8,128)(2,1)}, bf16[32,512]{1,0:T(8,128)(2,1)}) custom-call(s32[512]{0:T(512)} %pos_ref.1, f32[768]{0:T(1024)} %gq_ref.1, f32[256]{0:T(256)} %gkv_ref.1, bf16[512,2560]{1,0:T(8,128)(2,1)} %x_hbm.1, bf16[288,2560]{1,0:T(8,128)(2,1)} %bitcast.14, bf16[2560,768]{1,0:T(8,128)(2,1)} %wdq_hbm.1, ...), custom_call_target="tpu_custom_call" | custom-call | flops 40000000000 | bytes 40000000 | tf_op jit(solution)/shard_map/pallas_call | solution.py:449
  62.1 11.9 %shard_map.122 = (bf16[512,2560]{1,0:T(8,128)(2,1)}, bf16[512,256]{1,0:T(8,128)(2,1)}, bf16[32,512]{1,0:T(8,128)(2,1)}) custom-call(bf16[20,512,128]{2,1,0:T(8,128)(2,1)} %get-tuple-element.9.o_ref, bf16[512,256]{1,0:T(8,128)(2,1)} %get-tuple-element.10.ckv_ref, bf16[32,512]{1,0:T(8,128)(2,1)} %get-tuple-element.11.cpe_ref, bf16[2560,2560]{1,0:T(8,128)(2,1)} %bitcast.12), custom_call_target="tpu_custom_call" | custom-call | flops 6710886400 | bytes 13107200 | tf_op jit(solution)/shard_map/pallas_call | solution.py:508

commit v7 on v6

--- a/solution.py
+++ b/solution.py
@@ -36,7 +36,7 @@
 
 def layer_kernel(pos_ref, gq_ref, gkv_ref, x_hbm, wdkv_hbm, wdq_hbm, wuq_hbm, wuk_hbm, wuv_hbm,
                  o_hbm, ckv_out, cpe_out,
-                 x, wdkv, wdq, wuq, wuk, wuv, qlat, trig, ckv, pet, pen, qaug, kn, vt,
+                 x, wdkv, wdq, wuq, wuk, wuv, qlat, posf, trig, ckv, pet, pen, qaug, kn, vt,
                  s_buf, c_buf, p_buf, al_buf, m_s, acc, o_nat, o_help,
                  load_sem, c_send, c_recv, pe_send, pe_recv, f_send, q_send, q_recv, t_send, t_recv, o_send, o_recv, out_sem,
                  *, scale2, rows, nope, rot, vdim, heads, groups):
@@ -78,12 +78,12 @@
 
     def query_copies(to):
         return (remote(qlat.at[0], qlat.at[1], q_send.at[0], q_recv.at[0], to),
-                remote(trig.at[0], trig.at[1], t_send, t_recv, to))
+                remote(posf.at[0], posf.at[1], t_send, t_recv, to))
 
     def query_halves():
         top, low = pl.ds(0, half), pl.ds(half, half)
         return (remote(qlat.at[0, low], qlat.at[1, low], q_send.at[1], q_recv.at[1], 2),
-                remote(trig.at[0], trig.at[1], t_send, t_recv, 0),
+                remote(posf.at[0], posf.at[1], t_send, t_recv, 0),
                 remote(qlat.at[0, top], qlat.at[1, top], q_send.at[0], q_recv.at[0], 0))
 
     def query_relay():
@@ -108,10 +108,15 @@
     freq = jnp.zeros((hr, rows), f32)
     for i, f in enumerate(rope_freqs(rot)):
         freq = jnp.where(freq_i == i, f, freq)
-    angle = pos_ref[...].astype(f32).reshape(1, rows) * freq
-    cos_t, sin_t = jnp.cos(angle), jnp.sin(angle)
-    trig[0, :hr] = cos_t
-    trig[0, hr:] = sin_t
+
+    def turn(i):
+        angle = posf[i, :1] * freq
+        trig[i, :hr] = jnp.cos(angle)
+        trig[i, hr:] = jnp.sin(angle)
+
+    posf[0] = jnp.broadcast_to(pos_ref[...].astype(f32).reshape(1, rows), (8, rows))
+    turn(0)
+    cos_t, sin_t = trig[0, :hr], trig[0, hr:]
     loads[0].wait()
     loads[1].wait()
     kvt = lax.dot_general(wdkv[...], x[...], NT, preferred_element_type=f32)
@@ -270,7 +275,7 @@
                 help_half(k, 1, partner).start()
 
     def step(carry, new, own, after=None):
-        (slot1, blk1, last1, gi1), (slot2, blk2, last2, gi2) = carry
+        (slot1, _, _, _), (slot2, blk2, last2, gi2) = carry
         for u in range(GROUP):
             value_stage(u, slot2, blk2)
             exp_stage(u, slot1)
@@ -282,8 +287,6 @@
         @pl.when(last2 == 1)
         def _():
             finish(slot2, gi2)
-
-        return (new if new is not None else (SLOTS, 0, 0, 0)), (slot1, blk1, last1, gi1)
 
     def keys_and_values(slot, head0, blk):
         c = ckv[blk]
@@ -315,70 +318,70 @@
         for u in range(GROUP):
             m_s[slot * GROUP + u] = jnp.full((1, rows), -jnp.inf, f32)
 
-    def earlier(target, j):
-        return lax.rem(j + target - 1, jnp.maximum(target, 1))
+    def block_at(helping, target, i):
+        usual = jnp.where(i == 0, target, lax.rem(i + target - 2, jnp.maximum(target, 1)))
+        return jnp.where(helping & (me == 0), jnp.where(i < 2, i, 5 - i), usual)
 
     def group(gi, carry):
-        _, target, grp, slot = place_of(gi)
+        helping, target, grp, slot = place_of(gi)
         gn = jnp.minimum(gi + 1, n_all - 1)
         helping_n, target_n, grp_n, _ = place_of(gn)
         slot_n = lax.rem(gi + 1, SLOTS)
-        head0, head_n = grp * GROUP, grp_n * GROUP
 
         @pl.when((gi == n_own - 2) & (me == 3))
         def _():
             for c in query_copies(me):
                 c.wait_recv()
+            turn(1)
 
         @pl.when((gi == n_own - 2) & (me == 0))
         def _():
             for c in query_halves()[1:] + (query_relay(),):
                 c.wait_recv()
-            received(3)
-
-        @pl.when((gi == n_own - 1) & (me == 0))
-        def _():
-            received(1)
-            received(2)
-
-        def arrived(j):
-            @pl.when((gi == 0) & (j < target))
+            turn(1)
+
+        fresh = jnp.where(me == 0, gi == n_own - 1, gi == 0)
+
+        def one(i, carry):
+            blk = block_at(helping, target, i)
+            more = i < target
+            blk_n = jnp.where(more, block_at(helping, target, i + 1), block_at(helping_n, target_n, 0))
+
+            @pl.when(fresh & more)
             def _():
-                blk = earlier(target, j)
-                received(blk)
-
-                @pl.when((me >= 2) & (blk == 3 - me))
+                received(blk_n)
+
+                @pl.when((me >= 2) & (blk_n == 3 - me))
                 def _():
-                    start(forward_copies(blk))
-
-        def next_keys(j):
-            more = j < target
-            keys_and_values(jnp.where(more, slot, slot_n), jnp.where(more, head0, head_n),
-                            jnp.where(more, earlier(target, j), target_n))
-
-        def after_own():
-            queries(lax.rem(gi + 1, 2), helping_n.astype(jnp.int32), head_n)
-            next_keys(0)
-            clear(slot_n)
-
-        arrived(0)
-
-        @pl.when((gi == 0) & (me == 2))
-        def _():
-            query_halves()[0].wait_recv()
-            query_relay().start()
-            start(latent_copies(me, 0))
-
-        carry = step(carry, (slot, target, (target == 0).astype(jnp.int32), gi), True, after_own)
-
-        def previous(j, carry):
-            arrived(j + 1)
-            return step(carry, (slot, earlier(target, j), (j == target - 1).astype(jnp.int32), gi), False,
-                        lambda: next_keys(j + 1))
-
-        carry = lax.fori_loop(0, target, previous, carry)
-
-        return carry
+                    start(forward_copies(blk_n))
+
+            @pl.when((gi == 0) & (me == 2) & (i == 0))
+            def _():
+                query_halves()[0].wait_recv()
+                query_relay().start()
+                start(latent_copies(me, 0))
+
+            new = (slot, blk, (i == target).astype(jnp.int32), gi)
+
+            def next_keys():
+                keys_and_values(jnp.where(more, slot, slot_n), jnp.where(more, grp, grp_n) * GROUP, blk_n)
+
+            def after_own():
+                queries(lax.rem(gi + 1, 2), helping_n.astype(jnp.int32), grp_n * GROUP)
+                next_keys()
+                clear(slot_n)
+
+            @pl.when(blk == target)
+            def _():
+                step(carry, new, True, after_own)
+
+            @pl.when(blk != target)
+            def _():
+                step(carry, new, False, next_keys)
+
+            return new, carry[0]
+
+        return lax.fori_loop(0, target + 1, one, carry)
 
     idle = (jnp.int32(SLOTS), jnp.int32(0), jnp.int32(0), jnp.int32(0))
     acc[...] = jnp.zeros_like(acc)
@@ -386,8 +389,8 @@
     keys_and_values(0, 0, me)
     clear(0)
     carry = lax.fori_loop(0, n_all, group, (idle, idle))
-    carry = step(carry, None, False)
     step(carry, None, False)
+    step((idle, carry[0]), None, False)
 
     @pl.when(me == 1)
     def _():
@@ -461,6 +464,7 @@
             pltpu.VMEM(wuk.shape, bf16),
             pltpu.VMEM(wuv.shape, bf16),
             pltpu.VMEM((2, rows, qrank), bf16),
+            pltpu.VMEM((2, 8, rows), f32),
             pltpu.VMEM((2, rot, rows), f32),
             pltpu.VMEM((groups, rows, rank), bf16),
             pltpu.VMEM((groups, rot, rows), bf16),
@@ -487,33 +491,64 @@
     )(pos, gq, gkv, x, wdkv, wdq, wuq, wuk, wuv)
 
 
-def project_kernel(o_ref, ckv_ref, cpe_ref, w_ref, out_ref, ckv_out, cpe_out):
-    @pl.when(pl.program_id(0) == 0)
-    def _():
-        ckv_out[...] = ckv_ref[...]
-        cpe_out[...] = cpe_ref[...]
-
-    o_all = jnp.concatenate([o_ref[j] for j in range(o_ref.shape[0])], axis=1)
-    out_ref[...] = jnp.dot(o_all, w_ref[...], preferred_element_type=jnp.float32).astype(out_ref.dtype)
+def project_kernel(ckv_ref, cpe_ref, o_hbm, w_hbm, out_hbm, ckv_out, cpe_out, o, w, total, out, o_sem, w_sem, first_sem, out_sem, *, tile):
+    f32 = jnp.float32
+    npair, rows, width = o.shape
+    depth, dim = w.shape
+    parts = dim // tile
+    deep = depth // parts
+    per = npair // parts
+
+    def cut(i):
+        return pl.ds(i * tile, tile)
+
+    o_copies = [pltpu.make_async_copy(o_hbm.at[pl.ds(i * per, per)], o.at[pl.ds(i * per, per)], o_sem.at[i]) for i in range(parts)]
+    first = [pltpu.make_async_copy(w_hbm.at[pl.ds(i * deep, deep), cut(0)], w.at[pl.ds(i * deep, deep), cut(0)], first_sem.at[i]) for i in range(parts)]
+    w_copies = [pltpu.make_async_copy(w_hbm.at[:, cut(i)], w.at[:, cut(i)], w_sem.at[i]) for i in range(parts)]
+    out_copies = [pltpu.make_async_copy(out.at[:, cut(i)], out_hbm.at[:, cut(i)], out_sem.at[i]) for i in range(parts)]
+    for i in range(parts):
+        o_copies[i].start()
+        first[i].start()
+    for c in w_copies[1:]:
+        c.start()
+    ckv_out[...] = ckv_ref[...]
+    cpe_out[...] = cpe_ref[...]
+    for i in range(parts):
+        o_copies[i].wait()
+        first[i].wait()
+        lhs = jnp.concatenate([o[i * per + j] for j in range(per)], axis=1)
+        t = jnp.dot(lhs, w[i * deep:(i + 1) * deep, :tile], preferred_element_type=f32)
+        total[...] = t if i == 0 else total[...] + t
+    out[:, cut(0)] = total[...].astype(out.dtype)
+    out_copies[0].start()
+    for i in range(1, parts):
+        w_copies[i].wait()
+        lhs = jnp.concatenate([o[j] for j in range(npair)], axis=1)
+        out[:, cut(i)] = jnp.dot(lhs, w[:, cut(i)], preferred_element_type=f32).astype(out.dtype)
+        out_copies[i].start()
+    for c in out_copies:
+        c.wait()
 
 
 def project(o, ckv, cpe, w):
     npair, rows, width = o.shape
     dim = w.shape[1]
     tile = 512
-
-    def whole(a):
-        return pl.BlockSpec(a.shape, lambda i: (0,) * a.ndim)
-
+    parts = dim // tile
+    bf16 = jnp.bfloat16
+    vm = pl.BlockSpec(memory_space=pltpu.VMEM)
+    anym = pl.BlockSpec(memory_space=pl.ANY)
+    dma = pltpu.SemaphoreType.DMA
     return pl.pallas_call(
-        project_kernel,
-        grid=(dim // tile,),
-        in_specs=[whole(o), whole(ckv), whole(cpe), pl.BlockSpec((w.shape[0], tile), lambda i: (0, i))],
-        out_specs=(pl.BlockSpec((rows, tile), lambda i: (0, i)), whole(ckv), whole(cpe)),
-        out_shape=(jax.ShapeDtypeStruct((rows, dim), jnp.bfloat16), jax.ShapeDtypeStruct(ckv.shape, ckv.dtype), jax.ShapeDtypeStruct(cpe.shape, cpe.dtype)),
+        functools.partial(project_kernel, tile=tile),
+        in_specs=[vm, vm, anym, anym],
+        out_specs=(anym, vm, vm),
+        out_shape=(jax.ShapeDtypeStruct((rows, dim), bf16), jax.ShapeDtypeStruct(ckv.shape, ckv.dtype), jax.ShapeDtypeStruct(cpe.shape, cpe.dtype)),
+        scratch_shapes=[pltpu.VMEM(o.shape, bf16), pltpu.VMEM(w.shape, bf16), pltpu.VMEM((rows, tile), jnp.float32), pltpu.VMEM((rows, dim), bf16),
+                        dma((parts,)), dma((parts,)), dma((parts,)), dma((parts,))],
         compiler_params=pltpu.CompilerParams(vmem_limit_bytes=62 * 1024 * 1024),
         cost_estimate=pl.CostEstimate(flops=2 * rows * dim * w.shape[0], bytes_accessed=2 * w.size, transcendentals=0),
-    )(o, ckv, cpe, w)
+    )(ckv, cpe, o, w)
 
 
 def solution(mesh):

time: 74.3 us -> 76.4 us (1.028)
  Pallas kernels: 73.4 us -> 75.5 us
    pallas_call x1, Pallas kernels: 11.9 us -> 13.9 us  [project(): pl.pallas_call(functools.partial(project_kernel, tile=tile), in_specs=[vm...]
where the time goes in v7:
time: 76.4 us; the launch traced here: 76.3 us
  Pallas kernels  75.5 us (99%)
  between operations  0.8 us (1%)
    pallas_call x1, Pallas kernels, layer(): pl.pallas_call(functools.partial(layer_kernel, scale2=scale2, rows=rows,...  61.6 us
    pallas_call x1, Pallas kernels, project(): pl.pallas_call(functools.partial(project_kernel, tile=tile), in_specs=[vm...  13.9 us

profile of v7, /device:TPU:3, one launch (start us, length us, event | category | flops | bytes accessed | tf_op | source)
XLA Modules:
  0.0 76.3 jit_solution(5683289623347298411)
XLA Ops:
  0.6 61.6 %shard_map.121 = (bf16[20,512,128]{2,1,0:T(8,128)(2,1)}, bf16[512,256]{1,0:T(8,128)(2,1)}, bf16[32,512]{1,0:T(8,128)(2,1)}) custom-call(s32[512]{0:T(512)} %pos_ref.1, f32[768]{0:T(1024)} %gq_ref.1, f32[256]{0:T(256)} %gkv_ref.1, bf16[512,2560]{1,0:T(8,128)(2,1)} %x_hbm.1, bf16[288,2560]{1,0:T(8,128)(2,1)} %bitcast.14, bf16[2560,768]{1,0:T(8,128)(2,1)} %wdq_hbm.1, ...), custom_call_target="tpu_custom_call" | custom-call | flops 40000000000 | bytes 40000000 | tf_op jit(solution)/shard_map/pallas_call | solution.py:452
  62.2 13.9 %shard_map.122 = (bf16[512,2560]{1,0:T(8,128)(2,1)}, bf16[512,256]{1,0:T(8,128)(2,1)}, bf16[32,512]{1,0:T(8,128)(2,1)}) custom-call(bf16[512,256]{1,0:T(8,128)(2,1)} %get-tuple-element.9.ckv_ref, bf16[32,512]{1,0:T(8,128)(2,1)} %get-tuple-element.10.cpe_ref, bf16[20,512,128]{2,1,0:T(8,128)(2,1)} %get-tuple-element.11.o_hbm, bf16[2560,2560]{1,0:T(8,128)(2,1)} %bitcast.12), custom_call_target="tpu_custom_call" | custom-call | flops 6710886400 | bytes 13107200 | tf_op jit(solution)/shard_map/pallas_call | solution.py:542

commit v8 on v7

--- a/solution.py
+++ b/solution.py
@@ -57,7 +57,7 @@
 
     loads = [pltpu.make_async_copy(s, d, load_sem.at[i]) for i, (s, d) in enumerate(
         ((x_hbm, x), (wdkv_hbm, wdkv), (wdq_hbm, wdq), (wuq_hbm, wuq), (wuk_hbm, wuk), (wuv_hbm, wuv)))]
-    for c in loads:
+    for c in loads[:3]:
         c.start()
     barrier = pltpu.get_barrier_semaphore()
     for d in range(1, groups):
@@ -119,6 +119,8 @@
     cos_t, sin_t = trig[0, :hr], trig[0, hr:]
     loads[0].wait()
     loads[1].wait()
+    for c in loads[3:]:
+        c.start()
     kvt = lax.dot_general(wdkv[...], x[...], NT, preferred_element_type=f32)
     rank = ckv.shape[2]
     a = kvt[:rank]
@@ -491,9 +493,9 @@
     )(pos, gq, gkv, x, wdkv, wdq, wuq, wuk, wuv)
 
 
-def project_kernel(ckv_ref, cpe_ref, o_hbm, w_hbm, out_hbm, ckv_out, cpe_out, o, w, total, out, o_sem, w_sem, first_sem, out_sem, *, tile):
+def project_kernel(ckv_ref, cpe_ref, o_hbm, w_hbm, out_hbm, ckv_out, cpe_out, o, w, total, out, o_sem, w_sem, out_sem, *, tile):
     f32 = jnp.float32
-    npair, rows, width = o.shape
+    npair = o.shape[0]
     depth, dim = w.shape
     parts = dim // tile
     deep = depth // parts
@@ -503,29 +505,26 @@
         return pl.ds(i * tile, tile)
 
     o_copies = [pltpu.make_async_copy(o_hbm.at[pl.ds(i * per, per)], o.at[pl.ds(i * per, per)], o_sem.at[i]) for i in range(parts)]
-    first = [pltpu.make_async_copy(w_hbm.at[pl.ds(i * deep, deep), cut(0)], w.at[pl.ds(i * deep, deep), cut(0)], first_sem.at[i]) for i in range(parts)]
-    w_copies = [pltpu.make_async_copy(w_hbm.at[:, cut(i)], w.at[:, cut(i)], w_sem.at[i]) for i in range(parts)]
+    w_copies = [pltpu.make_async_copy(w_hbm.at[pl.ds(i * deep, deep)], w.at[pl.ds(i * deep, deep)], w_sem.at[i]) for i in range(parts)]
     out_copies = [pltpu.make_async_copy(out.at[:, cut(i)], out_hbm.at[:, cut(i)], out_sem.at[i]) for i in range(parts)]
     for i in range(parts):
         o_copies[i].start()
-        first[i].start()
-    for c in w_copies[1:]:
-        c.start()
+        w_copies[i].start()
     ckv_out[...] = ckv_ref[...]
     cpe_out[...] = cpe_ref[...]
     for i in range(parts):
         o_copies[i].wait()
-        first[i].wait()
+        w_copies[i].wait()
         lhs = jnp.concatenate([o[i * per + j] for j in range(per)], axis=1)
-        t = jnp.dot(lhs, w[i * deep:(i + 1) * deep, :tile], preferred_element_type=f32)
-        total[...] = t if i == 0 else total[...] + t
-    out[:, cut(0)] = total[...].astype(out.dtype)
-    out_copies[0].start()
-    for i in range(1, parts):
-        w_copies[i].wait()
-        lhs = jnp.concatenate([o[j] for j in range(npair)], axis=1)
-        out[:, cut(i)] = jnp.dot(lhs, w[:, cut(i)], preferred_element_type=f32).astype(out.dtype)
-        out_copies[i].start()
+        for n in range(parts):
+            t = jnp.dot(lhs, w[i * deep:(i + 1) * deep, cut(n)], preferred_element_type=f32)
+            if i > 0:
+                t = t + total[:, cut(n)]
+            if i < parts - 1:
+                total[:, cut(n)] = t
+            else:
+                out[:, cut(n)] = t.astype(out.dtype)
+                out_copies[n].start()
     for c in out_copies:
         c.wait()
 
@@ -544,8 +543,8 @@
         in_specs=[vm, vm, anym, anym],
         out_specs=(anym, vm, vm),
         out_shape=(jax.ShapeDtypeStruct((rows, dim), bf16), jax.ShapeDtypeStruct(ckv.shape, ckv.dtype), jax.ShapeDtypeStruct(cpe.shape, cpe.dtype)),
-        scratch_shapes=[pltpu.VMEM(o.shape, bf16), pltpu.VMEM(w.shape, bf16), pltpu.VMEM((rows, tile), jnp.float32), pltpu.VMEM((rows, dim), bf16),
-                        dma((parts,)), dma((parts,)), dma((parts,)), dma((parts,))],
+        scratch_shapes=[pltpu.VMEM(o.shape, bf16), pltpu.VMEM(w.shape, bf16), pltpu.VMEM((rows, dim), jnp.float32), pltpu.VMEM((rows, dim), bf16),
+                        dma((parts,)), dma((parts,)), dma((parts,))],
         compiler_params=pltpu.CompilerParams(vmem_limit_bytes=62 * 1024 * 1024),
         cost_estimate=pl.CostEstimate(flops=2 * rows * dim * w.shape[0], bytes_accessed=2 * w.size, transcendentals=0),
     )(ckv, cpe, o, w)

time: 76.4 us -> 74.6 us (0.976)
  Pallas kernels: 75.5 us -> 73.7 us
    pallas_call x1, Pallas kernels: 13.9 us -> 12.1 us  [project(): pl.pallas_call(functools.partial(project_kernel, tile=tile), in_specs=[vm...]
where the time goes in v8:
time: 74.6 us; the launch traced here: 74.5 us
  Pallas kernels  73.7 us (99%)
  between operations  0.8 us (1%)
    pallas_call x1, Pallas kernels, layer(): pl.pallas_call(functools.partial(layer_kernel, scale2=scale2, rows=rows,...  61.6 us
    pallas_call x1, Pallas kernels, project(): pl.pallas_call(functools.partial(project_kernel, tile=tile), in_specs=[vm...  12.1 us

profile of v8, /device:TPU:3, one launch (start us, length us, event | category | flops | bytes accessed | tf_op | source)
XLA Modules:
  0.0 74.5 jit_solution(13104316292788769999)
XLA Ops:
  0.6 61.6 %shard_map.121 = (bf16[20,512,128]{2,1,0:T(8,128)(2,1)}, bf16[512,256]{1,0:T(8,128)(2,1)}, bf16[32,512]{1,0:T(8,128)(2,1)}) custom-call(s32[512]{0:T(512)} %pos_ref.1, f32[768]{0:T(1024)} %gq_ref.1, f32[256]{0:T(256)} %gkv_ref.1, bf16[512,2560]{1,0:T(8,128)(2,1)} %x_hbm.1, bf16[288,2560]{1,0:T(8,128)(2,1)} %bitcast.14, bf16[2560,768]{1,0:T(8,128)(2,1)} %wdq_hbm.1, ...), custom_call_target="tpu_custom_call" | custom-call | flops 40000000000 | bytes 40000000 | tf_op jit(solution)/shard_map/pallas_call | solution.py:454
  62.2 12.1 %shard_map.122 = (bf16[512,2560]{1,0:T(8,128)(2,1)}, bf16[512,256]{1,0:T(8,128)(2,1)}, bf16[32,512]{1,0:T(8,128)(2,1)}) custom-call(bf16[512,256]{1,0:T(8,128)(2,1)} %get-tuple-element.9.ckv_ref, bf16[32,512]{1,0:T(8,128)(2,1)} %get-tuple-element.10.cpe_ref, bf16[20,512,128]{2,1,0:T(8,128)(2,1)} %get-tuple-element.11.o_hbm, bf16[2560,2560]{1,0:T(8,128)(2,1)} %bitcast.12), custom_call_target="tpu_custom_call" | custom-call | flops 6710886400 | bytes 13107200 | tf_op jit(solution)/shard_map/pallas_call | solution.py:541

commit v9 on v8

--- a/solution.py
+++ b/solution.py
@@ -104,6 +104,10 @@
         pen[origin] = wide.T.astype(bf16)
 
     hr = rot // 2
+
+    def cols(i):
+        return slice(i * half, (i + 1) * half)
+
     freq_i = lax.broadcasted_iota(jnp.int32, (hr, rows), 0)
     freq = jnp.zeros((hr, rows), f32)
     for i, f in enumerate(rope_freqs(rot)):
@@ -117,6 +121,9 @@
     posf[0] = jnp.broadcast_to(pos_ref[...].astype(f32).reshape(1, rows), (8, rows))
     turn(0)
     cos_t, sin_t = trig[0, :hr], trig[0, hr:]
+    qaug[...] = jnp.zeros_like(qaug)
+    vt[:, vdim:, :] = jnp.ones((vt.shape[0], vt.shape[1] - vdim, vt.shape[2]), vt.dtype)
+    acc[...] = jnp.zeros_like(acc)
     loads[0].wait()
     loads[1].wait()
     for c in loads[3:]:
@@ -133,10 +140,14 @@
     pet[me] = pe_own
     cpe_out[...] = pe_own
     loads[2].wait()
-    tile = 256
     qrank = wdq.shape[1]
-    first = lax.dot_general(x[...], wdq[:, :tile], NN, preferred_element_type=f32)
-    s_buf[0, :, :tile] = first
+
+    def query_latent(part):
+        ql = lax.dot_general(x[cols(part)], wdq[...], NN, preferred_element_type=f32)
+        ql = ql * lax.rsqrt(jnp.sum(ql * ql, axis=1, keepdims=True) / qrank + NORM_EPS) * gq_ref[...].reshape(1, qrank)
+        qlat[0, cols(part)] = ql.astype(bf16)
+
+    query_latent(0)
     pl.semaphore_wait(barrier, groups - 1)
 
     @pl.when(me == 0)
@@ -153,12 +164,8 @@
     def _():
         start(latent_copies(me, 3))
 
-    rest = lax.dot_general(x[...], wdq[:, tile:], NN, preferred_element_type=f32)
-    ql = jnp.concatenate([s_buf[0, :, :tile], rest], axis=1)
-    qlat[0] = (ql * lax.rsqrt(jnp.sum(ql * ql, axis=1, keepdims=True) / qrank + NORM_EPS) * gq_ref[...].reshape(1, qrank)).astype(bf16)
+    query_latent(1)
     unpack_rope(me)
-    qaug[...] = jnp.zeros_like(qaug)
-    vt[:, vdim:, :] = jnp.ones((vt.shape[0], vt.shape[1] - vdim, vt.shape[2]), vt.dtype)
     for c in loads[3:]:
         c.wait()
 
@@ -175,9 +182,6 @@
     OWN = ((0, 0), (0, 1), (1, 1))
     row_i = lax.broadcasted_iota(jnp.int32, (half, half), 0)
     col_i = lax.broadcasted_iota(jnp.int32, (half, half), 1)
-
-    def cols(i):
-        return slice(i * half, (i + 1) * half)
 
     def score_stage(u, blk, own, gi):
         tops = [None, None]
@@ -276,11 +280,12 @@
             def _():
                 help_half(k, 1, partner).start()
 
-    def step(carry, new, own, after=None):
+    def step(carry, new, own, after=None, values_only=False):
         (slot1, _, _, _), (slot2, blk2, last2, gi2) = carry
         for u in range(GROUP):
             value_stage(u, slot2, blk2)
-            exp_stage(u, slot1)
+            if not values_only:
+                exp_stage(u, slot1)
             if new is not None:
                 score_stage(u, new[1], own, new[3])
         if after is not None:
@@ -386,13 +391,16 @@
         return lax.fori_loop(0, target + 1, one, carry)
 
     idle = (jnp.int32(SLOTS), jnp.int32(0), jnp.int32(0), jnp.int32(0))
-    acc[...] = jnp.zeros_like(acc)
     queries(0, 0, 0)
-    keys_and_values(0, 0, me)
-    clear(0)
+
+    @pl.when(me >= 0)
+    def _():
+        keys_and_values(0, 0, me)
+        clear(0)
+
     carry = lax.fori_loop(0, n_all, group, (idle, idle))
     step(carry, None, False)
-    step((idle, carry[0]), None, False)
+    step((idle, carry[0]), None, False, values_only=True)
 
     @pl.when(me == 1)
     def _():
@@ -507,14 +515,20 @@
     o_copies = [pltpu.make_async_copy(o_hbm.at[pl.ds(i * per, per)], o.at[pl.ds(i * per, per)], o_sem.at[i]) for i in range(parts)]
     w_copies = [pltpu.make_async_copy(w_hbm.at[pl.ds(i * deep, deep)], w.at[pl.ds(i * deep, deep)], w_sem.at[i]) for i in range(parts)]
     out_copies = [pltpu.make_async_copy(out.at[:, cut(i)], out_hbm.at[:, cut(i)], out_sem.at[i]) for i in range(parts)]
-    for i in range(parts):
-        o_copies[i].start()
-        w_copies[i].start()
+    def fetch(i):
+        if i < parts:
+            o_copies[i].start()
+            w_copies[i].start()
+
+    fetch(0)
     ckv_out[...] = ckv_ref[...]
     cpe_out[...] = cpe_ref[...]
     for i in range(parts):
         o_copies[i].wait()
         w_copies[i].wait()
+        if i == 0:
+            fetch(1)
+        fetch(i + 2)
         lhs = jnp.concatenate([o[i * per + j] for j in range(per)], axis=1)
         for n in range(parts):
             t = jnp.dot(lhs, w[i * deep:(i + 1) * deep, cut(n)], preferred_element_type=f32)

time: 74.6 us -> 75.6 us (1.013)
  Pallas kernels: 73.7 us -> 74.7 us
    pallas_call x1, Pallas kernels: 12.1 us -> 13.3 us  [project(): pl.pallas_call(functools.partial(project_kernel, tile=tile), in_specs=[vm...]
where the time goes in v9:
time: 75.6 us; the launch traced here: 75.5 us
  Pallas kernels  74.7 us (99%)
  between operations  0.82 us (1%)
    pallas_call x1, Pallas kernels, layer(): pl.pallas_call(functools.partial(layer_kernel, scale2=scale2, rows=rows,...  61.4 us
    pallas_call x1, Pallas kernels, project(): pl.pallas_call(functools.partial(project_kernel, tile=tile), in_specs=[vm...  13.3 us

profile of v9, /device:TPU:3, one launch (start us, length us, event | category | flops | bytes accessed | tf_op | source)
XLA Modules:
  0.0 75.5 jit_solution(6834699359535265575)
XLA Ops:
  0.6 61.4 %shard_map.121 = (bf16[20,512,128]{2,1,0:T(8,128)(2,1)}, bf16[512,256]{1,0:T(8,128)(2,1)}, bf16[32,512]{1,0:T(8,128)(2,1)}) custom-call(s32[512]{0:T(512)} %pos_ref.1, f32[768]{0:T(1024)} %gq_ref.1, f32[256]{0:T(256)} %gkv_ref.1, bf16[512,2560]{1,0:T(8,128)(2,1)} %x_hbm.1, bf16[288,2560]{1,0:T(8,128)(2,1)} %bitcast.14, bf16[2560,768]{1,0:T(8,128)(2,1)} %wdq_hbm.1, ...), custom_call_target="tpu_custom_call" | custom-call | flops 40000000000 | bytes 40000000 | tf_op jit(solution)/shard_map/pallas_call | solution.py:462
  62.0 13.3 %shard_map.122 = (bf16[512,2560]{1,0:T(8,128)(2,1)}, bf16[512,256]{1,0:T(8,128)(2,1)}, bf16[32,512]{1,0:T(8,128)(2,1)}) custom-call(bf16[512,256]{1,0:T(8,128)(2,1)} %get-tuple-element.9.ckv_ref, bf16[32,512]{1,0:T(8,128)(2,1)} %get-tuple-element.10.cpe_ref, bf16[20,512,128]{2,1,0:T(8,128)(2,1)} %get-tuple-element.11.o_hbm, bf16[2560,2560]{1,0:T(8,128)(2,1)} %bitcast.12), custom_call_target="tpu_custom_call" | custom-call | flops 6710886400 | bytes 13107200 | tf_op jit(solution)/shard_map/pallas_call | solution.py:555

commit v10 on v9

--- a/solution.py
+++ b/solution.py
@@ -31,7 +31,6 @@
 
 GROUP = 8
 SLOTS = 3
-MOST_HELPED = 2
 
 
 def layer_kernel(pos_ref, gq_ref, gkv_ref, x_hbm, wdkv_hbm, wdq_hbm, wuq_hbm, wuk_hbm, wuv_hbm,
@@ -50,8 +49,10 @@
     ngroup = heads // GROUP
     me = lax.axis_index('sp')
     given = jnp.where(me == 3, 2, jnp.where(me == 2, 1, 0))
-    helped = jnp.where(me == 0, 2, jnp.where(me == 3, 1, 0))
-    partner = jnp.where(me == 0, 3, 2)
+    helped = jnp.where(me == 2, 0, 1)
+    partner = jnp.where(me == 3, 2, 3)
+    help_group = jnp.where(me == 1, 3, 4)
+    help_turn = jnp.where(me == 2, 2 * ngroup, jnp.where(me == 3, 2, 3))
     n_own = ngroup - given
     n_all = n_own + helped
 
@@ -89,6 +90,15 @@
     def query_relay():
         low = pl.ds(half, half)
         return remote(qlat.at[1, low], qlat.at[1, low], q_send.at[2], q_recv.at[2], 0)
+
+    def query_share():
+        return (remote(qlat.at[1], qlat.at[1], q_send.at[0], q_recv.at[0], 1),
+                remote(posf.at[1], posf.at[1], t_send, t_recv, 1))
+
+    def latent_share(origin):
+        spare = 6 - 2 * origin
+        return (remote(ckv.at[origin], ckv.at[origin], c_send.at[spare], c_recv.at[origin], 1),
+                remote(pet.at[origin], pet.at[origin], pe_send.at[spare], pe_recv.at[origin], 1))
 
     def start(copies):
         for c in copies:
@@ -226,27 +236,16 @@
             acc[h, :, cols(i)] = t + acc[h, :, cols(i)] * al_buf[u, :, cols(i)]
 
     def place_of(gi):
-        helping = (gi >= n_own - 1) & (gi < n_own - 1 + helped)
+        helping = gi == help_turn
         target = jnp.where(helping, partner, me)
-        grp = jnp.where(helping, ngroup - helped + gi - n_own + 1, jnp.minimum(gi, n_own - 1))
+        grp = jnp.where(helping, help_group, gi - (gi > help_turn).astype(jnp.int32))
         return helping, target, grp, lax.rem(gi, SLOTS)
 
     def output_copy(grp):
         return pltpu.make_async_copy(o_nat.at[pl.ds(grp * pairs, pairs)], o_hbm.at[pl.ds(grp * pairs, pairs)], out_sem.at[grp])
 
-    def half_at(grp, part):
-        return o_nat.at[pl.ds(grp * pairs + part * (pairs // 2), pairs // 2)]
-
-    def help_half(k, part, to):
-        grp = ngroup - helped + k
-        return remote(o_help.at[k, pl.ds(part * (pairs // 2), pairs // 2)], half_at(grp, part), o_send.at[k, part], o_recv.at[grp, part], to)
-
-    def help_detour():
-        spot = o_help.at[1, pl.ds(pairs // 2, pairs // 2)]
-        return remote(spot, spot, o_send.at[1, 1], o_recv.at[ngroup - 1, 1], 1)
-
-    def help_relay():
-        return remote(o_help.at[1, pl.ds(pairs // 2, pairs // 2)], half_at(ngroup - 1, 1), o_send.at[1, 1], o_recv.at[ngroup - 1, 1], 3)
+    def help_copy(grp, to):
+        return remote(o_help, o_nat.at[pl.ds(grp * pairs, pairs)], o_send, o_recv.at[grp], to)
 
     def finish(slot, gi):
         outs = []
@@ -266,19 +265,9 @@
 
         @pl.when(helping)
         def _():
-            k = gi - n_own + 1
             for j in range(pairs):
-                o_help[k, j] = outs[j]
-            help_half(k, 0, partner).start()
-            detour = (me == 0) & (k == 1)
-
-            @pl.when(detour)
-            def _():
-                help_detour().start()
-
-            @pl.when(jnp.logical_not(detour))
-            def _():
-                help_half(k, 1, partner).start()
+                o_help[j] = outs[j]
+            help_copy(help_group, partner).start()
 
     def step(carry, new, own, after=None, values_only=False):
         (slot1, _, _, _), (slot2, blk2, last2, gi2) = carry
@@ -327,7 +316,7 @@
 
     def block_at(helping, target, i):
         usual = jnp.where(i == 0, target, lax.rem(i + target - 2, jnp.maximum(target, 1)))
-        return jnp.where(helping & (me == 0), jnp.where(i < 2, i, 5 - i), usual)
+        return jnp.where(helping & (me < 2), jnp.where(i < 2, i, 5 - i), usual)
 
     def group(gi, carry):
         helping, target, grp, slot = place_of(gi)
@@ -335,32 +324,37 @@
         helping_n, target_n, grp_n, _ = place_of(gn)
         slot_n = lax.rem(gi + 1, SLOTS)
 
-        @pl.when((gi == n_own - 2) & (me == 3))
+        @pl.when((gi == help_turn - 1) & ((me == 1) | (me == 3)))
         def _():
             for c in query_copies(me):
                 c.wait_recv()
             turn(1)
 
-        @pl.when((gi == n_own - 2) & (me == 0))
+        @pl.when((gi == help_turn - 1) & (me == 0))
         def _():
             for c in query_halves()[1:] + (query_relay(),):
                 c.wait_recv()
+            start(query_share())
             turn(1)
 
-        fresh = jnp.where(me == 0, gi == n_own - 1, gi == 0)
+        fresh = ((gi == 0) & (me > 0)) | (helping & (me < 2))
 
         def one(i, carry):
             blk = block_at(helping, target, i)
             more = i < target
             blk_n = jnp.where(more, block_at(helping, target, i + 1), block_at(helping_n, target_n, 0))
 
-            @pl.when(fresh & more)
+            @pl.when(fresh & more & (blk_n != me))
             def _():
                 received(blk_n)
 
                 @pl.when((me >= 2) & (blk_n == 3 - me))
                 def _():
                     start(forward_copies(blk_n))
+
+                @pl.when((me == 0) & (blk_n >= 2))
+                def _():
+                    start(latent_share(blk_n))
 
             @pl.when((gi == 0) & (me == 2) & (i == 0))
             def _():
@@ -402,19 +396,13 @@
     step(carry, None, False)
     step((idle, carry[0]), None, False, values_only=True)
 
-    @pl.when(me == 1)
-    def _():
-        help_detour().wait_recv()
-        help_relay().start()
-        help_relay().wait_send()
-
     def sent(copies):
         for c in copies:
             c.wait_send()
 
     @pl.when(me == 0)
     def _():
-        sent(latent_copies(me, 1) + latent_copies(me, 3))
+        sent(latent_copies(me, 1) + latent_copies(me, 3) + query_share() + latent_share(2) + latent_share(3))
 
     @pl.when(me == 1)
     def _():
@@ -428,18 +416,15 @@
     def _():
         sent(latent_copies(me, 0) + forward_copies(0) + query_halves())
 
-    for k in range(MOST_HELPED):
-        @pl.when(k < helped)
-        def _():
-            for part in range(2):
-                help_half(k, part, partner).wait_send()
-
+    @pl.when(helped > 0)
+    def _():
+        help_copy(help_group, partner).wait_send()
+
+    for k in range(2):
         @pl.when(k < given)
         def _():
-            grp = n_own + k
-            for part in range(2):
-                remote(half_at(grp, part), half_at(grp, part), o_send.at[k, part], o_recv.at[grp, part], me).wait_recv()
-            output_copy(grp).start()
+            help_copy(n_own + k, me).wait_recv()
+            output_copy(n_own + k).start()
 
     for grp in range(ngroup):
         output_copy(grp).wait()
@@ -458,7 +443,6 @@
     f32 = jnp.float32
     bf16 = jnp.bfloat16
     dma = pltpu.SemaphoreType.DMA
-    nhelp = MOST_HELPED
     return pl.pallas_call(
         functools.partial(layer_kernel, scale2=scale2, rows=rows, nope=nope, rot=rot, vdim=vdim, heads=heads, groups=groups),
         out_shape=(jax.ShapeDtypeStruct((heads // 2, rows, 2 * vdim), bf16),
@@ -489,11 +473,11 @@
             pltpu.VMEM(((SLOTS + 1) * GROUP, 1, rows), f32),
             pltpu.VMEM(((SLOTS + 1) * GROUP, vdim + 16, rows), f32),
             pltpu.VMEM((heads // 2, rows, 2 * vdim), bf16),
-            pltpu.VMEM((nhelp, GROUP // 2, rows, 2 * vdim), bf16),
+            pltpu.VMEM((GROUP // 2, rows, 2 * vdim), bf16),
             dma((6,)),
             dma((groups,)), dma((groups,)), dma((groups,)), dma((groups,)), dma((2,)),
             dma((3,)), dma((3,)), dma, dma,
-            dma((nhelp, 2)), dma((heads // GROUP, 2)),
+            dma, dma((heads // GROUP,)),
             dma((heads // GROUP,)),
         ],
         compiler_params=pltpu.CompilerParams(vmem_limit_bytes=62 * 1024 * 1024, collective_id=0, has_side_effects=True),
@@ -513,22 +497,20 @@
         return pl.ds(i * tile, tile)
 
     o_copies = [pltpu.make_async_copy(o_hbm.at[pl.ds(i * per, per)], o.at[pl.ds(i * per, per)], o_sem.at[i]) for i in range(parts)]
-    w_copies = [pltpu.make_async_copy(w_hbm.at[pl.ds(i * deep, deep)], w.at[pl.ds(i * deep, deep)], w_sem.at[i]) for i in range(parts)]
+    fine = deep // 4
+    w_copies = [[pltpu.make_async_copy(w_hbm.at[pl.ds(i * deep + j * fine, fine)], w.at[pl.ds(i * deep + j * fine, fine)], w_sem.at[i, j])
+                 for j in range(4)] for i in range(parts)]
     out_copies = [pltpu.make_async_copy(out.at[:, cut(i)], out_hbm.at[:, cut(i)], out_sem.at[i]) for i in range(parts)]
-    def fetch(i):
-        if i < parts:
-            o_copies[i].start()
-            w_copies[i].start()
-
-    fetch(0)
+    for i in range(parts):
+        o_copies[i].start()
+        for c in w_copies[i]:
+            c.start()
     ckv_out[...] = ckv_ref[...]
     cpe_out[...] = cpe_ref[...]
     for i in range(parts):
         o_copies[i].wait()
-        w_copies[i].wait()
-        if i == 0:
-            fetch(1)
-        fetch(i + 2)
+        for c in w_copies[i]:
+            c.wait()
         lhs = jnp.concatenate([o[i * per + j] for j in range(per)], axis=1)
         for n in range(parts):
             t = jnp.dot(lhs, w[i * deep:(i + 1) * deep, cut(n)], preferred_element_type=f32)
@@ -558,7 +540,7 @@
         out_specs=(anym, vm, vm),
         out_shape=(jax.ShapeDtypeStruct((rows, dim), bf16), jax.ShapeDtypeStruct(ckv.shape, ckv.dtype), jax.ShapeDtypeStruct(cpe.shape, cpe.dtype)),
         scratch_shapes=[pltpu.VMEM(o.shape, bf16), pltpu.VMEM(w.shape, bf16), pltpu.VMEM((rows, dim), jnp.float32), pltpu.VMEM((rows, dim), bf16),
-                        dma((parts,)), dma((parts,)), dma((parts,))],
+                        dma((parts,)), dma((parts, 4)), dma((parts,))],
         compiler_params=pltpu.CompilerParams(vmem_limit_bytes=62 * 1024 * 1024),
         cost_estimate=pl.CostEstimate(flops=2 * rows * dim * w.shape[0], bytes_accessed=2 * w.size, transcendentals=0),
     )(ckv, cpe, o, w)

time: 75.6 us -> 73.2 us (0.968)
  Pallas kernels: 74.7 us -> 72.2 us
    pallas_call x1, Pallas kernels: 61.4 us -> 57.9 us  [layer(): pl.pallas_call(functools.partial(layer_kernel, scale2=scale2, rows=rows,...]
    pallas_call x1, Pallas kernels: 13.3 us -> 14.3 us  [project(): pl.pallas_call(functools.partial(project_kernel, tile=tile), in_specs=[vm...]
where the time goes in v10:
time: 73.2 us; the launch traced here: 73 us
  Pallas kernels  72.2 us (99%)
  between operations  0.82 us (1%)
    pallas_call x1, Pallas kernels, layer(): pl.pallas_call(functools.partial(layer_kernel, scale2=scale2, rows=rows,...  57.9 us
    pallas_call x1, Pallas kernels, project(): pl.pallas_call(functools.partial(project_kernel, tile=tile), in_specs=[vm...  14.3 us

profile of v10, /device:TPU:3, one launch (start us, length us, event | category | flops | bytes accessed | tf_op | source)
XLA Modules:
  0.0 73.0 jit_solution(2255510850943138748)
XLA Ops:
  0.6 57.9 %shard_map.121 = (bf16[20,512,128]{2,1,0:T(8,128)(2,1)}, bf16[512,256]{1,0:T(8,128)(2,1)}, bf16[32,512]{1,0:T(8,128)(2,1)}) custom-call(s32[512]{0:T(512)} %pos_ref.1, f32[768]{0:T(1024)} %gq_ref.1, f32[256]{0:T(256)} %gkv_ref.1, bf16[512,2560]{1,0:T(8,128)(2,1)} %x_hbm.1, bf16[288,2560]{1,0:T(8,128)(2,1)} %bitcast.14, bf16[2560,768]{1,0:T(8,128)(2,1)} %wdq_hbm.1, ...), custom_call_target="tpu_custom_call" | custom-call | flops 40000000000 | bytes 40000000 | tf_op jit(solution)/shard_map/pallas_call | solution.py:446
  58.6 14.3 %shard_map.122 = (bf16[512,2560]{1,0:T(8,128)(2,1)}, bf16[512,256]{1,0:T(8,128)(2,1)}, bf16[32,512]{1,0:T(8,128)(2,1)}) custom-call(bf16[512,256]{1,0:T(8,128)(2,1)} %get-tuple-element.9.ckv_ref, bf16[32,512]{1,0:T(8,128)(2,1)} %get-tuple-element.10.cpe_ref, bf16[20,512,128]{2,1,0:T(8,128)(2,1)} %get-tuple-element.11.o_hbm, bf16[2560,2560]{1,0:T(8,128)(2,1)} %bitcast.12), custom_call_target="tpu_custom_call" | custom-call | flops 6710886400 | bytes 13107200 | tf_op jit(solution)/shard_map/pallas_call | solution.py:537

commit v11 on v10

--- a/solution.py
+++ b/solution.py
@@ -31,13 +31,14 @@
 
 GROUP = 8
 SLOTS = 3
-
-
-def layer_kernel(pos_ref, gq_ref, gkv_ref, x_hbm, wdkv_hbm, wdq_hbm, wuq_hbm, wuk_hbm, wuv_hbm,
-                 o_hbm, ckv_out, cpe_out,
-                 x, wdkv, wdq, wuq, wuk, wuv, qlat, posf, trig, ckv, pet, pen, qaug, kn, vt,
+LAYER_VMEM = 65500000
+
+
+def layer_kernel(pos_ref, gq_ref, gkv_ref, x_hbm, wdkv_hbm, wdq_hbm, wuq_hbm, wuk_hbm, wuv_hbm, wo_hbm,
+                 out_hbm, ckv_out, cpe_out,
+                 wdkv, wo, wuq, wuk, wuv, qlat, posf, trig, ckv, pet, pen, qaug, kn, vt,
                  s_buf, c_buf, p_buf, al_buf, m_s, acc, o_nat, o_help,
-                 load_sem, c_send, c_recv, pe_send, pe_recv, f_send, q_send, q_recv, t_send, t_recv, o_send, o_recv, out_sem,
+                 load_sem, c_send, c_recv, pe_send, pe_recv, f_send, q_send, q_recv, t_send, t_recv, o_send, o_recv, wo_sem, out_sem,
                  *, scale2, rows, nope, rot, vdim, heads, groups):
     f32 = jnp.float32
     bf16 = jnp.bfloat16
@@ -56,9 +57,17 @@
     n_own = ngroup - given
     n_all = n_own + helped
 
-    loads = [pltpu.make_async_copy(s, d, load_sem.at[i]) for i, (s, d) in enumerate(
-        ((x_hbm, x), (wdkv_hbm, wdkv), (wdq_hbm, wdq), (wuq_hbm, wuq), (wuk_hbm, wuk), (wuv_hbm, wuv)))]
-    for c in loads[:3]:
+    tiles = x_hbm.shape[1] // rows
+    x_loads = [pltpu.make_async_copy(x_hbm.at[:, pl.ds(i * rows, rows)], p_buf.at[i], load_sem.at[i]) for i in range(tiles)]
+    qrank = wdq_hbm.shape[1]
+    part = GROUP * qk
+    w_loads = [pltpu.make_async_copy(s, d, load_sem.at[tiles + i]) for i, (s, d) in enumerate(
+        ((wdkv_hbm, wdkv), (wdq_hbm, wo.at[:, pl.ds(0, qrank)]), (wuk_hbm, wuk), (wuv_hbm, wuv)))]
+    uq_loads = [pltpu.make_async_copy(wuq_hbm.at[pl.ds(i * part, part)], wuq.at[pl.ds(i * part, part)], load_sem.at[tiles + 4 + i]) for i in range(ngroup)]
+    wide = wo_hbm.shape[1] - qrank
+    wo_loads = [pltpu.make_async_copy(wo_hbm.at[:, pl.ds(a, n)], wo.at[:, pl.ds(a, n)], wo_sem.at[i])
+                for i, (a, n) in enumerate(((qrank, wide), (0, qrank)))]
+    for c in x_loads + w_loads[:2]:
         c.start()
     barrier = pltpu.get_barrier_semaphore()
     for d in range(1, groups):
@@ -134,11 +143,15 @@
     qaug[...] = jnp.zeros_like(qaug)
     vt[:, vdim:, :] = jnp.ones((vt.shape[0], vt.shape[1] - vdim, vt.shape[2]), vt.dtype)
     acc[...] = jnp.zeros_like(acc)
-    loads[0].wait()
-    loads[1].wait()
-    for c in loads[3:]:
+    for c in x_loads + w_loads[:1]:
+        c.wait()
+    for c in uq_loads[:1] + w_loads[2:] + uq_loads[1:]:
         c.start()
-    kvt = lax.dot_general(wdkv[...], x[...], NT, preferred_element_type=f32)
+
+    def x_rows(cut):
+        return jnp.concatenate([p_buf[i, cut, :] for i in range(tiles)], axis=1)
+
+    kvt = lax.dot_general(wdkv[...], x_rows(slice(0, rows)), NT, preferred_element_type=f32)
     rank = ckv.shape[2]
     a = kvt[:rank]
     norm = a * lax.rsqrt(jnp.sum(a * a, axis=0, keepdims=True) / rank + NORM_EPS)
@@ -149,11 +162,9 @@
     pe_own = jnp.concatenate([z1 * cos_t - z2 * sin_t, z2 * cos_t + z1 * sin_t], axis=0).astype(bf16)
     pet[me] = pe_own
     cpe_out[...] = pe_own
-    loads[2].wait()
-    qrank = wdq.shape[1]
-
+    w_loads[1].wait()
     def query_latent(part):
-        ql = lax.dot_general(x[cols(part)], wdq[...], NN, preferred_element_type=f32)
+        ql = lax.dot_general(x_rows(cols(part)), wo[:, :qrank], NN, preferred_element_type=f32)
         ql = ql * lax.rsqrt(jnp.sum(ql * ql, axis=1, keepdims=True) / qrank + NORM_EPS) * gq_ref[...].reshape(1, qrank)
         qlat[0, cols(part)] = ql.astype(bf16)
 
@@ -176,9 +187,6 @@
 
     query_latent(1)
     unpack_rope(me)
-    for c in loads[3:]:
-        c.wait()
-
     @pl.when(me == 2)
     def _():
         start(query_copies(3))
@@ -230,7 +238,7 @@
 
     def value_stage(u, slot, blk):
         h = slot * GROUP + u
-        v = vt[jnp.minimum(slot, SLOTS - 1) * GROUP + u, :, pl.ds(pl.multiple_of(blk * rows, rows), rows)]
+        v = vt[h, :, pl.ds(pl.multiple_of(blk * rows, rows), rows)]
         for i in range(2):
             t = lax.dot_general(v, p_buf[u, :, cols(i)], NN, preferred_element_type=f32)
             acc[h, :, cols(i)] = t + acc[h, :, cols(i)] * al_buf[u, :, cols(i)]
@@ -240,9 +248,6 @@
         target = jnp.where(helping, partner, me)
         grp = jnp.where(helping, help_group, gi - (gi > help_turn).astype(jnp.int32))
         return helping, target, grp, lax.rem(gi, SLOTS)
-
-    def output_copy(grp):
-        return pltpu.make_async_copy(o_nat.at[pl.ds(grp * pairs, pairs)], o_hbm.at[pl.ds(grp * pairs, pairs)], out_sem.at[grp])
 
     def help_copy(grp, to):
         return remote(o_help, o_nat.at[pl.ds(grp * pairs, pairs)], o_send, o_recv.at[grp], to)
@@ -261,7 +266,6 @@
         def _():
             for j in range(pairs):
                 o_nat[grp * pairs + j] = outs[j]
-            output_copy(grp).start()
 
         @pl.when(helping)
         def _():
@@ -337,6 +341,16 @@
             start(query_share())
             turn(1)
 
+        @pl.when(gi == 0)
+        def _():
+            for c in uq_loads[1:]:
+                c.wait()
+
+        @pl.when(gi == 1)
+        def _():
+            for c in wo_loads:
+                c.start()
+
         fresh = ((gi == 0) & (me > 0)) | (helping & (me < 2))
 
         def one(i, carry):
@@ -382,10 +396,20 @@
 
             return new, carry[0]
 
-        return lax.fori_loop(0, target + 1, one, carry)
-
-    idle = (jnp.int32(SLOTS), jnp.int32(0), jnp.int32(0), jnp.int32(0))
+        carry = lax.fori_loop(0, target + 1, one, carry)
+
+        @pl.when(gi == 1)
+        def _():
+            for u in range(GROUP):
+                acc[(SLOTS - 1) * GROUP + u] = jnp.zeros(acc.shape[1:], f32)
+
+        return carry
+
+    idle = (jnp.int32(SLOTS - 1), jnp.int32(0), jnp.int32(0), jnp.int32(0))
+    uq_loads[0].wait()
     queries(0, 0, 0)
+    for c in w_loads[2:]:
+        c.wait()
 
     @pl.when(me >= 0)
     def _():
@@ -420,17 +444,39 @@
     def _():
         help_copy(help_group, partner).wait_send()
 
-    for k in range(2):
-        @pl.when(k < given)
-        def _():
-            help_copy(n_own + k, me).wait_recv()
-            output_copy(n_own + k).start()
-
-    for grp in range(ngroup):
-        output_copy(grp).wait()
-
-
-def layer(pos, gq, gkv, x, wdkv, wdq, wuq, wuk, wuv, scale2, heads, groups):
+    for c in wo_loads:
+        c.wait()
+    deep = GROUP * vdim
+    outs = [pltpu.make_async_copy(p_buf.at[n], out_hbm.at[:, pl.ds(n * rows, rows)], out_sem.at[n]) for n in range(tiles)]
+    def product(grp, n):
+        lhs = jnp.concatenate([o_nat[grp * pairs + j] for j in range(pairs)], axis=1)
+        w = wo[pl.ds(pl.multiple_of(grp * deep, deep), deep), n * rows:(n + 1) * rows]
+        return lax.dot_general(lhs, w, NN, preferred_element_type=f32)
+
+    def arrive(grp):
+        @pl.when(grp >= n_own)
+        def _():
+            help_copy(grp, me).wait_recv()
+
+    for n in range(tiles):
+        s_buf[n] = jnp.zeros((rows, rows), f32)
+
+    def accumulate(grp, c):
+        arrive(grp)
+        for n in range(tiles):
+            s_buf[n] = product(grp, n) + s_buf[n]
+        return c
+
+    lax.fori_loop(0, ngroup - 1, accumulate, 0)
+    arrive(ngroup - 1)
+    for n in range(tiles):
+        p_buf[n] = (product(ngroup - 1, n) + s_buf[n]).astype(bf16)
+        outs[n].start()
+    for c in outs:
+        c.wait()
+
+
+def layer(pos, gq, gkv, x, wdkv, wdq, wuq, wuk, wuv, wo, scale2, heads, groups):
     rows, dim = x.shape
     rank = gkv.shape[0]
     rot = wdkv.shape[0] - rank
@@ -439,21 +485,20 @@
     vdim = wuv.shape[0] // heads
     seq = rows * groups
     vm = pl.BlockSpec(memory_space=pltpu.VMEM)
-    anym = pl.BlockSpec(memory_space=pl.ANY)
+    anym = pl.BlockSpec(memory_space=pltpu.HBM)
     f32 = jnp.float32
     bf16 = jnp.bfloat16
     dma = pltpu.SemaphoreType.DMA
     return pl.pallas_call(
         functools.partial(layer_kernel, scale2=scale2, rows=rows, nope=nope, rot=rot, vdim=vdim, heads=heads, groups=groups),
-        out_shape=(jax.ShapeDtypeStruct((heads // 2, rows, 2 * vdim), bf16),
+        out_shape=(jax.ShapeDtypeStruct((rows, dim), bf16),
                    jax.ShapeDtypeStruct((rows, rank), bf16),
                    jax.ShapeDtypeStruct((rot, rows), bf16)),
-        in_specs=[vm, vm, vm] + [anym] * 6,
+        in_specs=[vm, vm, vm] + [anym] * 7,
         out_specs=(anym, vm, vm),
         scratch_shapes=[
-            pltpu.VMEM(x.shape, bf16),
             pltpu.VMEM(wdkv.shape, bf16),
-            pltpu.VMEM(wdq.shape, bf16),
+            pltpu.VMEM(wo.shape, bf16),
             pltpu.VMEM(wuq.shape, bf16),
             pltpu.VMEM(wuk.shape, bf16),
             pltpu.VMEM(wuv.shape, bf16),
@@ -470,80 +515,19 @@
             pltpu.VMEM((GROUP, 1, rows), f32),
             pltpu.VMEM((GROUP, rows, rows), bf16),
             pltpu.VMEM((GROUP, 1, rows), f32),
-            pltpu.VMEM(((SLOTS + 1) * GROUP, 1, rows), f32),
-            pltpu.VMEM(((SLOTS + 1) * GROUP, vdim + 16, rows), f32),
+            pltpu.VMEM((SLOTS * GROUP, 1, rows), f32),
+            pltpu.VMEM((SLOTS * GROUP, vdim + 16, rows), f32),
             pltpu.VMEM((heads // 2, rows, 2 * vdim), bf16),
             pltpu.VMEM((GROUP // 2, rows, 2 * vdim), bf16),
-            dma((6,)),
+            dma((x.shape[1] // rows + 4 + heads // GROUP,)),
             dma((groups,)), dma((groups,)), dma((groups,)), dma((groups,)), dma((2,)),
             dma((3,)), dma((3,)), dma, dma,
             dma, dma((heads // GROUP,)),
-            dma((heads // GROUP,)),
+            dma((2,)), dma((dim // rows,)),
         ],
-        compiler_params=pltpu.CompilerParams(vmem_limit_bytes=62 * 1024 * 1024, collective_id=0, has_side_effects=True),
+        compiler_params=pltpu.CompilerParams(vmem_limit_bytes=LAYER_VMEM, collective_id=0, has_side_effects=True),
         cost_estimate=pl.CostEstimate(flops=40_000_000_000, bytes_accessed=40_000_000, transcendentals=30_000_000),
-    )(pos, gq, gkv, x, wdkv, wdq, wuq, wuk, wuv)
-
-
-def project_kernel(ckv_ref, cpe_ref, o_hbm, w_hbm, out_hbm, ckv_out, cpe_out, o, w, total, out, o_sem, w_sem, out_sem, *, tile):
-    f32 = jnp.float32
-    npair = o.shape[0]
-    depth, dim = w.shape
-    parts = dim // tile
-    deep = depth // parts
-    per = npair // parts
-
-    def cut(i):
-        return pl.ds(i * tile, tile)
-
-    o_copies = [pltpu.make_async_copy(o_hbm.at[pl.ds(i * per, per)], o.at[pl.ds(i * per, per)], o_sem.at[i]) for i in range(parts)]
-    fine = deep // 4
-    w_copies = [[pltpu.make_async_copy(w_hbm.at[pl.ds(i * deep + j * fine, fine)], w.at[pl.ds(i * deep + j * fine, fine)], w_sem.at[i, j])
-                 for j in range(4)] for i in range(parts)]
-    out_copies = [pltpu.make_async_copy(out.at[:, cut(i)], out_hbm.at[:, cut(i)], out_sem.at[i]) for i in range(parts)]
-    for i in range(parts):
-        o_copies[i].start()
-        for c in w_copies[i]:
-            c.start()
-    ckv_out[...] = ckv_ref[...]
-    cpe_out[...] = cpe_ref[...]
-    for i in range(parts):
-        o_copies[i].wait()
-        for c in w_copies[i]:
-            c.wait()
-        lhs = jnp.concatenate([o[i * per + j] for j in range(per)], axis=1)
-        for n in range(parts):
-            t = jnp.dot(lhs, w[i * deep:(i + 1) * deep, cut(n)], preferred_element_type=f32)
-            if i > 0:
-                t = t + total[:, cut(n)]
-            if i < parts - 1:
-                total[:, cut(n)] = t
-            else:
-                out[:, cut(n)] = t.astype(out.dtype)
-                out_copies[n].start()
-    for c in out_copies:
-        c.wait()
-
-
-def project(o, ckv, cpe, w):
-    npair, rows, width = o.shape
-    dim = w.shape[1]
-    tile = 512
-    parts = dim // tile
-    bf16 = jnp.bfloat16
-    vm = pl.BlockSpec(memory_space=pltpu.VMEM)
-    anym = pl.BlockSpec(memory_space=pl.ANY)
-    dma = pltpu.SemaphoreType.DMA
-    return pl.pallas_call(
-        functools.partial(project_kernel, tile=tile),
-        in_specs=[vm, vm, anym, anym],
-        out_specs=(anym, vm, vm),
-        out_shape=(jax.ShapeDtypeStruct((rows, dim), bf16), jax.ShapeDtypeStruct(ckv.shape, ckv.dtype), jax.ShapeDtypeStruct(cpe.shape, cpe.dtype)),
-        scratch_shapes=[pltpu.VMEM(o.shape, bf16), pltpu.VMEM(w.shape, bf16), pltpu.VMEM((rows, dim), jnp.float32), pltpu.VMEM((rows, dim), bf16),
-                        dma((parts,)), dma((parts, 4)), dma((parts,))],
-        compiler_params=pltpu.CompilerParams(vmem_limit_bytes=62 * 1024 * 1024),
-        cost_estimate=pl.CostEstimate(flops=2 * rows * dim * w.shape[0], bytes_accessed=2 * w.size, transcendentals=0),
-    )(ckv, cpe, o, w)
+    )(pos, gq, gkv, x, wdkv, wdq, wuq, wuk, wuv, wo)
 
 
 def solution(mesh):
@@ -561,9 +545,8 @@
         def flat(w):
             return jnp.transpose(w, (1, 2, 0)).reshape(-1, w.shape[0])
 
-        o, ckv, cpe = layer(tok_pos, g_q, g_kv, tok_in, w_dkv.T, w_dq, flat(w_uq), flat(w_uk), flat(w_uv),
+        attn_out, cache_kv, cache_pe = layer(tok_pos, g_q, g_kv, tok_in, w_dkv.T, w_dq, flat(w_uq), flat(w_uk), flat(w_uv), w_o.reshape(heads * v_dim, -1),
                                       attn_scale * math.log2(math.e), heads, groups)
-        attn_out, cache_kv, cache_pe = project(o, ckv, cpe, w_o.reshape(heads * v_dim, -1))
         return attn_out, cache_kv, cache_pe.T
 
     return jax.shard_map(local_step, mesh=mesh, in_specs=(rows_spec, tok_spec, replicated, replicated, replicated, replicated, replicated, replicated, replicated, replicated), out_specs=(rows_spec, rows_spec, rows_spec), check_vma=False)

time: 73.2 us -> 71.6 us (0.978)
  the two profiles are of different devices: /device:TPU:3 before, /device:TPU:1 now
where the time goes in v11:
time: 71.6 us; the launch traced here: 71.5 us
  Pallas kernels  66 us (92%)
  local copies, waits for them, and re-layouts  4.77 us (7%)
    pallas_call x1, Pallas kernels, layer(): pl.pallas_call(functools.partial(layer_kernel, scale2=scale2, rows=rows,...  66 us
    unnamed x7, local copies, waits for them, and re-layouts  4.77 us

profile of v11, /device:TPU:1, one launch (start us, length us, event | category | flops | bytes accessed | tf_op | source)
XLA Modules:
  0.0 71.5 jit_solution(12116402995841245620)
XLA Ops:
  0.6 66.0 %shard_map.121 = (bf16[512,2560]{1,0:T(8,128)(2,1)}, bf16[512,256]{1,0:T(8,128)(2,1)}, bf16[32,512]{1,0:T(8,128)(2,1)}) custom-call(s32[512]{0:T(512)} %pos_ref.1, f32[768]{0:T(1024)} %gq_ref.1, f32[256]{0:T(256)} %gkv_ref.1, bf16[512,2560]{1,0:T(8,128)(2,1)} %x_hbm.1, bf16[288,2560]{1,0:T(8,128)(2,1)} %bitcast.15, bf16[2560,768]{1,0:T(8,128)(2,1)} %wdq_hbm.1, ...), custom_call_target="tpu_custom_call" | custom-call | flops 40000000000 | bytes 40000000 | tf_op jit(solution)/shard_map/pallas_call | solution.py:492
  66.7 0.0 copy-start
  66.7 0.0 copy-start.1
  66.7 3.4 %copy.16 = bf16[512,2560]{1,0:T(8,128)(2,1)} copy(bf16[512,2560]{1,0:T(8,128)(2,1)} %get-tuple-element.12) | data formatting | bytes 5242880
  70.1 0.0 copy-done
  70.2 0.7 copy.17
  70.9 0.0 copy-done.1
  70.9 0.6 copy.18
Async XLA Ops:
  66.7 3.5 %copy-start = (bf16[512,256]{1,0:T(8,128)(2,1)S(1)}, bf16[512,256]{1,0:T(8,128)(2,1)}, u32[]{:S(2)}) copy-start(bf16[512,256]{1,0:T(8,128)(2,1)} %get-tuple-element.13) | copy-start | bytes 786436
  66.7 4.2 %copy-start.1 = (bf16[32,512]{1,0:T(8,128)(2,1)S(1)}, bf16[32,512]{1,0:T(8,128)(2,1)}, u32[]{:S(2)}) copy-start(bf16[32,512]{1,0:T(8,128)(2,1)} %get-tuple-element.8) | copy-start | bytes 98308

commit v12 on v11

--- a/solution.py
+++ b/solution.py
@@ -420,30 +420,6 @@
     step(carry, None, False)
     step((idle, carry[0]), None, False, values_only=True)
 
-    def sent(copies):
-        for c in copies:
-            c.wait_send()
-
-    @pl.when(me == 0)
-    def _():
-        sent(latent_copies(me, 1) + latent_copies(me, 3) + query_share() + latent_share(2) + latent_share(3))
-
-    @pl.when(me == 1)
-    def _():
-        sent(latent_copies(me, 2) + latent_copies(me, 0))
-
-    @pl.when(me == 2)
-    def _():
-        sent(latent_copies(me, 3) + latent_copies(me, 0) + forward_copies(1) + query_copies(3) + (query_relay(),))
-
-    @pl.when(me == 3)
-    def _():
-        sent(latent_copies(me, 0) + forward_copies(0) + query_halves())
-
-    @pl.when(helped > 0)
-    def _():
-        help_copy(help_group, partner).wait_send()
-
     for c in wo_loads:
         c.wait()
     deep = GROUP * vdim
@@ -472,6 +448,30 @@
     for n in range(tiles):
         p_buf[n] = (product(ngroup - 1, n) + s_buf[n]).astype(bf16)
         outs[n].start()
+    def sent(copies):
+        for c in copies:
+            c.wait_send()
+
+    @pl.when(me == 0)
+    def _():
+        sent(latent_copies(me, 1) + latent_copies(me, 3) + query_share() + latent_share(2) + latent_share(3))
+
+    @pl.when(me == 1)
+    def _():
+        sent(latent_copies(me, 2) + latent_copies(me, 0))
+
+    @pl.when(me == 2)
+    def _():
+        sent(latent_copies(me, 3) + latent_copies(me, 0) + forward_copies(1) + query_copies(3) + (query_relay(),))
+
+    @pl.when(me == 3)
+    def _():
+        sent(latent_copies(me, 0) + forward_copies(0) + query_halves())
+
+    @pl.when(helped > 0)
+    def _():
+        help_copy(help_group, partner).wait_send()
+
     for c in outs:
         c.wait()
 
@@ -530,6 +530,37 @@
     )(pos, gq, gkv, x, wdkv, wdq, wuq, wuk, wuv, wo)
 
 
+def deliver_kernel(out_in, ckv_in, cpe_in, out_hbm, ckv_out, cpe_out, out, ckv, cpe, in_sem, out_sem):
+    half = out.shape[0] // 2
+    steps = ((ckv_in, ckv, ckv_out, None), (cpe_in, cpe, cpe_out, None), (out_in, out, out_hbm, 0), (out_in, out, out_hbm, half))
+
+    def view(ref, start):
+        return ref if start is None else ref.at[pl.ds(start, half)]
+
+    ins = [pltpu.make_async_copy(view(a, n), view(b, n), in_sem.at[i]) for i, (a, b, _, n) in enumerate(steps)]
+    outs = [pltpu.make_async_copy(view(b, n), view(c, n), out_sem.at[i]) for i, (_, b, c, n) in enumerate(steps)]
+    for c in ins:
+        c.start()
+    for a, b in zip(ins, outs):
+        a.wait()
+        b.start()
+    for c in outs:
+        c.wait()
+
+
+def deliver(*arrays):
+    anym = pl.BlockSpec(memory_space=pl.ANY)
+    return pl.pallas_call(
+        deliver_kernel,
+        in_specs=[anym] * 3,
+        out_specs=(anym,) * 3,
+        out_shape=tuple(jax.ShapeDtypeStruct(a.shape, a.dtype) for a in arrays),
+        scratch_shapes=[pltpu.VMEM(a.shape, a.dtype) for a in arrays] + [pltpu.SemaphoreType.DMA((4,)), pltpu.SemaphoreType.DMA((4,))],
+        compiler_params=pltpu.CompilerParams(vmem_limit_bytes=62 * 1024 * 1024),
+        cost_estimate=pl.CostEstimate(flops=1000, bytes_accessed=6_000_000, transcendentals=0),
+    )(*arrays)
+
+
 def solution(mesh):
     groups = mesh.shape['sp']
     tok_spec = P(('dp', 'sp'))
@@ -547,6 +578,7 @@
 
         attn_out, cache_kv, cache_pe = layer(tok_pos, g_q, g_kv, tok_in, w_dkv.T, w_dq, flat(w_uq), flat(w_uk), flat(w_uv), w_o.reshape(heads * v_dim, -1),
                                       attn_scale * math.log2(math.e), heads, groups)
+        attn_out, cache_kv, cache_pe = deliver(attn_out, cache_kv, cache_pe)
         return attn_out, cache_kv, cache_pe.T
 
     return jax.shard_map(local_step, mesh=mesh, in_specs=(rows_spec, tok_spec, replicated, replicated, replicated, replicated, replicated, replicated, replicated, replicated), out_specs=(rows_spec, rows_spec, rows_spec), check_vma=False)

time: 71.6 us -> 69.9 us (0.976)
  local copies, waits for them, and re-layouts: 4.77 us -> 0 us
  Pallas kernels: 66 us -> 69 us
    unnamed x7 -> x0, local copies, waits for them, and re-layouts: 4.77 us -> none
    pallas_call x0 -> x1, Pallas kernels: none -> 2.99 us  [deliver(): pl.pallas_call(deliver_kernel, in_specs=[anym] * 3, out_specs=(anym,) * 3...]
where the time goes in v12:
time: 69.9 us; the launch traced here: 69.8 us
  Pallas kernels  69 us (99%)
  between operations  0.8 us (1%)
    pallas_call x1, Pallas kernels, layer(): pl.pallas_call(functools.partial(layer_kernel, scale2=scale2, rows=rows,...  66 us
    pallas_call x1, Pallas kernels, deliver(): pl.pallas_call(deliver_kernel, in_specs=[anym] * 3, out_specs=(anym,) * 3...  2.99 us

profile of v12, /device:TPU:1, one launch (start us, length us, event | category | flops | bytes accessed | tf_op | source)
XLA Modules:
  0.0 69.8 jit_solution(17426725965085980159)
XLA Ops:
  0.6 66.0 %shard_map.121 = (bf16[512,2560]{1,0:T(8,128)(2,1)}, bf16[512,256]{1,0:T(8,128)(2,1)}, bf16[32,512]{1,0:T(8,128)(2,1)}) custom-call(s32[512]{0:T(512)} %pos_ref.1, f32[768]{0:T(1024)} %gq_ref.1, f32[256]{0:T(256)} %gkv_ref.1, bf16[512,2560]{1,0:T(8,128)(2,1)} %x_hbm.1, bf16[288,2560]{1,0:T(8,128)(2,1)} %bitcast.14, bf16[2560,768]{1,0:T(8,128)(2,1)} %wdq_hbm.1, ...), custom_call_target="tpu_custom_call" | custom-call | flops 40000000000 | bytes 40000000 | tf_op jit(solution)/shard_map/pallas_call | solution.py:492
  66.6 3.0 %shard_map.122 = (bf16[512,2560]{1,0:T(8,128)(2,1)}, bf16[512,256]{1,0:T(8,128)(2,1)}, bf16[32,512]{1,0:T(8,128)(2,1)}) custom-call(bf16[512,2560]{1,0:T(8,128)(2,1)} %get-tuple-element.9.out_in, bf16[512,256]{1,0:T(8,128)(2,1)} %get-tuple-element.10.ckv_in, bf16[32,512]{1,0:T(8,128)(2,1)} %get-tuple-element.11.cpe_in), custom_call_target="tpu_custom_call" | custom-call | flops 1000 | bytes 6000000 | tf_op jit(solution)/shard_map/pallas_call | solution.py:553

commit v13 on v12

--- a/solution.py
+++ b/solution.py
@@ -370,12 +370,6 @@
                 def _():
                     start(latent_share(blk_n))
 
-            @pl.when((gi == 0) & (me == 2) & (i == 0))
-            def _():
-                query_halves()[0].wait_recv()
-                query_relay().start()
-                start(latent_copies(me, 0))
-
             new = (slot, blk, (i == target).astype(jnp.int32), gi)
 
             def next_keys():
@@ -408,6 +402,13 @@
     idle = (jnp.int32(SLOTS - 1), jnp.int32(0), jnp.int32(0), jnp.int32(0))
     uq_loads[0].wait()
     queries(0, 0, 0)
+
+    @pl.when(me == 2)
+    def _():
+        query_halves()[0].wait_recv()
+        query_relay().start()
+        start(latent_copies(me, 0))
+
     for c in w_loads[2:]:
         c.wait()
 

time: 69.9 us -> 68.5 us (0.980)
  Pallas kernels: 69 us -> 67.5 us
    pallas_call x1, Pallas kernels: 66 us -> 64.5 us  [layer(): pl.pallas_call(functools.partial(layer_kernel, scale2=scale2, rows=rows,...]
where the time goes in v13:
time: 68.5 us; the launch traced here: 68.3 us
  Pallas kernels  67.5 us (99%)
  between operations  0.8 us (1%)
    pallas_call x1, Pallas kernels, layer(): pl.pallas_call(functools.partial(layer_kernel, scale2=scale2, rows=rows,...  64.5 us
    pallas_call x1, Pallas kernels, deliver(): pl.pallas_call(deliver_kernel, in_specs=[anym] * 3, out_specs=(anym,) * 3...  2.99 us

profile of v13, /device:TPU:1, one launch (start us, length us, event | category | flops | bytes accessed | tf_op | source)
XLA Modules:
  0.0 68.3 jit_solution(8620960050186830217)
XLA Ops:
  0.6 64.5 %shard_map.121 = (bf16[512,2560]{1,0:T(8,128)(2,1)}, bf16[512,256]{1,0:T(8,128)(2,1)}, bf16[32,512]{1,0:T(8,128)(2,1)}) custom-call(s32[512]{0:T(512)} %pos_ref.1, f32[768]{0:T(1024)} %gq_ref.1, f32[256]{0:T(256)} %gkv_ref.1, bf16[512,2560]{1,0:T(8,128)(2,1)} %x_hbm.1, bf16[288,2560]{1,0:T(8,128)(2,1)} %bitcast.14, bf16[2560,768]{1,0:T(8,128)(2,1)} %wdq_hbm.1, ...), custom_call_target="tpu_custom_call" | custom-call | flops 40000000000 | bytes 40000000 | tf_op jit(solution)/shard_map/pallas_call | solution.py:493
  65.2 3.0 %shard_map.122 = (bf16[512,2560]{1,0:T(8,128)(2,1)}, bf16[512,256]{1,0:T(8,128)(2,1)}, bf16[32,512]{1,0:T(8,128)(2,1)}) custom-call(bf16[512,2560]{1,0:T(8,128)(2,1)} %get-tuple-element.9.out_in, bf16[512,256]{1,0:T(8,128)(2,1)} %get-tuple-element.10.ckv_in, bf16[32,512]{1,0:T(8,128)(2,1)} %get-tuple-element.11.cpe_in), custom_call_target="tpu_custom_call" | custom-call | flops 1000 | bytes 6000000 | tf_op jit(solution)/shard_map/pallas_call | solution.py:554

commit v14 on v13

--- a/solution.py
+++ b/solution.py
@@ -92,13 +92,13 @@
 
     def query_halves():
         top, low = pl.ds(0, half), pl.ds(half, half)
-        return (remote(qlat.at[0, low], qlat.at[1, low], q_send.at[1], q_recv.at[1], 2),
+        return (remote(qlat.at[0, top], qlat.at[1, top], q_send.at[1], q_recv.at[1], 2),
                 remote(posf.at[0], posf.at[1], t_send, t_recv, 0),
-                remote(qlat.at[0, top], qlat.at[1, top], q_send.at[0], q_recv.at[0], 0))
+                remote(qlat.at[0, low], qlat.at[1, low], q_send.at[0], q_recv.at[0], 0))
 
     def query_relay():
-        low = pl.ds(half, half)
-        return remote(qlat.at[1, low], qlat.at[1, low], q_send.at[2], q_recv.at[2], 0)
+        top = pl.ds(0, half)
+        return remote(qlat.at[1, top], qlat.at[1, top], q_send.at[2], q_recv.at[2], 0)
 
     def query_share():
         return (remote(qlat.at[1], qlat.at[1], q_send.at[0], q_recv.at[0], 1),
@@ -185,15 +185,22 @@
     def _():
         start(latent_copies(me, 3))
 
+    @pl.when(me == 3)
+    def _():
+        query_halves()[0].start()
+
     query_latent(1)
     unpack_rope(me)
     @pl.when(me == 2)
     def _():
         start(query_copies(3))
+        query_halves()[0].wait_recv()
+        query_relay().start()
+        start(latent_copies(me, 0))
 
     @pl.when(me == 3)
     def _():
-        start(query_halves())
+        start(query_halves()[1:])
         start(latent_copies(me, 0))
 
     FULL = ((0, 0), (1, 0), (0, 1), (1, 1))
@@ -402,12 +409,6 @@
     idle = (jnp.int32(SLOTS - 1), jnp.int32(0), jnp.int32(0), jnp.int32(0))
     uq_loads[0].wait()
     queries(0, 0, 0)
-
-    @pl.when(me == 2)
-    def _():
-        query_halves()[0].wait_recv()
-        query_relay().start()
-        start(latent_copies(me, 0))
 
     for c in w_loads[2:]:
         c.wait()

time: 68.5 us -> 67.6 us (0.987)
  the two profiles are of different devices: /device:TPU:1 before, /device:TPU:3 now
where the time goes in v14:
time: 67.6 us; the launch traced here: 66.6 us
  Pallas kernels  65.8 us (97%)
  between operations  0.8 us (1%)
    pallas_call x1, Pallas kernels, layer(): pl.pallas_call(functools.partial(layer_kernel, scale2=scale2, rows=rows,...  62.8 us
    pallas_call x1, Pallas kernels, deliver(): pl.pallas_call(deliver_kernel, in_specs=[anym] * 3, out_specs=(anym,) * 3...  2.99 us

profile of v14, /device:TPU:3, one launch (start us, length us, event | category | flops | bytes accessed | tf_op | source)
XLA Modules:
  0.0 66.6 jit_solution(16349973262765416312)
XLA Ops:
  0.6 62.8 %shard_map.121 = (bf16[512,2560]{1,0:T(8,128)(2,1)}, bf16[512,256]{1,0:T(8,128)(2,1)}, bf16[32,512]{1,0:T(8,128)(2,1)}) custom-call(s32[512]{0:T(512)} %pos_ref.1, f32[768]{0:T(1024)} %gq_ref.1, f32[256]{0:T(256)} %gkv_ref.1, bf16[512,2560]{1,0:T(8,128)(2,1)} %x_hbm.1, bf16[288,2560]{1,0:T(8,128)(2,1)} %bitcast.14, bf16[2560,768]{1,0:T(8,128)(2,1)} %wdq_hbm.1, ...), custom_call_target="tpu_custom_call" | custom-call | flops 40000000000 | bytes 40000000 | tf_op jit(solution)/shard_map/pallas_call | solution.py:494
  63.5 3.0 %shard_map.122 = (bf16[512,2560]{1,0:T(8,128)(2,1)}, bf16[512,256]{1,0:T(8,128)(2,1)}, bf16[32,512]{1,0:T(8,128)(2,1)}) custom-call(bf16[512,2560]{1,0:T(8,128)(2,1)} %get-tuple-element.9.out_in, bf16[512,256]{1,0:T(8,128)(2,1)} %get-tuple-element.10.ckv_in, bf16[32,512]{1,0:T(8,128)(2,1)} %get-tuple-element.11.cpe_in), custom_call_target="tpu_custom_call" | custom-call | flops 1000 | bytes 6000000 | tf_op jit(solution)/shard_map/pallas_call | solution.py:555

commit v15 on v14

--- a/solution.py
+++ b/solution.py
@@ -437,18 +437,21 @@
             help_copy(grp, me).wait_recv()
 
     for n in range(tiles):
-        s_buf[n] = jnp.zeros((rows, rows), f32)
-
-    def accumulate(grp, c):
+        s_buf[n] = product(0, n)
+
+    last = ngroup - 2
+
+    def accumulate(i, c):
+        grp = i + (i == last).astype(jnp.int32)
         arrive(grp)
         for n in range(tiles):
             s_buf[n] = product(grp, n) + s_buf[n]
         return c
 
-    lax.fori_loop(0, ngroup - 1, accumulate, 0)
-    arrive(ngroup - 1)
+    lax.fori_loop(1, ngroup - 1, accumulate, 0)
+    arrive(last)
     for n in range(tiles):
-        p_buf[n] = (product(ngroup - 1, n) + s_buf[n]).astype(bf16)
+        p_buf[n] = (product(last, n) + s_buf[n]).astype(bf16)
         outs[n].start()
     def sent(copies):
         for c in copies:

time: 67.6 us -> 67.3 us (level)
  no operation moved by 1% of the time
where the time goes in v15:
time: 67.3 us; the launch traced here: 66.3 us
  Pallas kernels  65.5 us (97%)
  between operations  0.8 us (1%)
    pallas_call x1, Pallas kernels, layer(): pl.pallas_call(functools.partial(layer_kernel, scale2=scale2, rows=rows,...  62.5 us
    pallas_call x1, Pallas kernels, deliver(): pl.pallas_call(deliver_kernel, in_specs=[anym] * 3, out_specs=(anym,) * 3...  2.99 us

profile of v15, /device:TPU:3, one launch (start us, length us, event | category | flops | bytes accessed | tf_op | source)
XLA Modules:
  0.0 66.3 jit_solution(3044614563337238788)
XLA Ops:
  0.6 62.5 %shard_map.121 = (bf16[512,2560]{1,0:T(8,128)(2,1)}, bf16[512,256]{1,0:T(8,128)(2,1)}, bf16[32,512]{1,0:T(8,128)(2,1)}) custom-call(s32[512]{0:T(512)} %pos_ref.1, f32[768]{0:T(1024)} %gq_ref.1, f32[256]{0:T(256)} %gkv_ref.1, bf16[512,2560]{1,0:T(8,128)(2,1)} %x_hbm.1, bf16[288,2560]{1,0:T(8,128)(2,1)} %bitcast.14, bf16[2560,768]{1,0:T(8,128)(2,1)} %wdq_hbm.1, ...), custom_call_target="tpu_custom_call" | custom-call | flops 40000000000 | bytes 40000000 | tf_op jit(solution)/shard_map/pallas_call | solution.py:497
  63.1 3.0 %shard_map.122 = (bf16[512,2560]{1,0:T(8,128)(2,1)}, bf16[512,256]{1,0:T(8,128)(2,1)}, bf16[32,512]{1,0:T(8,128)(2,1)}) custom-call(bf16[512,2560]{1,0:T(8,128)(2,1)} %get-tuple-element.9.out_in, bf16[512,256]{1,0:T(8,128)(2,1)} %get-tuple-element.10.ckv_in, bf16[32,512]{1,0:T(8,128)(2,1)} %get-tuple-element.11.cpe_in), custom_call_target="tpu_custom_call" | custom-call | flops 1000 | bytes 6000000 | tf_op jit(solution)/shard_map/pallas_call | solution.py:558
